TPU v7x, 32 devices: a whole 2x2x4 slice. The times are simulated.
32 devices in a mesh: row: 8 (over y, x, core), col: 4 (over z).
Axes of the slice: x: 2, y: 2, z: 4, core: 2. Of those that a mesh axis runs over, the one named last changes fastest.
Arguments:
- features: bfloat16 [65536, 256], P(('col', 'row')), may hold values from -6 to 6
- block_values: bfloat16 [8, 4, 192, 128, 128], P('row', 'col'), may hold values from -0.1875 to 0.1875
- row_ptr: int32 [8, 4, 65], P('row', 'col'), may hold values from 0 to 144, as said below
- block_cols: int32 [8, 4, 192], P('row', 'col'), may hold values from 0 to 511, as said below
Outputs:
- product: bfloat16 [65536, 256], P(('row', 'col'))
Inputs may be any that keep to these rules, and one draw needn't show every extreme that they name: row_ptr[r, c, 0] = 0, row_ptr never falls along its last dimension, row_ptr[r, c, 64] <= 144, and on exactly one device row_ptr[r, c, 64] = 144. block_cols[r, c, s] lies in c * 128 to (c + 1) * 128 - 1; a block column may repeat within a block row, and repeated blocks add.
All inputs are finite; a program needn't handle non-finite values.
Results may differ from a plain program's by a relative error of at most 0.001.
Values may be sent and summed in bfloat16 or wider, within the bound.
No kernel may reach another device: no remote copies, remote signals or barrier semaphores. Data moves between devices by JAX's collectives and lax.ppermute only.
A program may use at most 128 MiB of HBM per device.

v0:
```python
import jax
import jax.numpy as jnp
from jax import lax
from jax.sharding import PartitionSpec as P


def row_weights(pointers, slot_count):
    slot_ids = jnp.arange(slot_count, dtype=jnp.int32)
    inside = (pointers[:-1, None] <= slot_ids[None, :]) & (slot_ids[None, :] < pointers[1:, None])
    return inside.astype(jnp.float32)


def local(features, block_values, row_ptr, block_cols):
    values = block_values[0, 0]
    pointers = row_ptr[0, 0]
    slot_count = values.shape[0]
    block_size = values.shape[1]
    local_rows = pointers.shape[0] - 1
    group_blocks = features.shape[0] * lax.axis_size("row") // block_size
    columns = block_cols[0, 0] - lax.axis_index("col") * group_blocks
    weights = row_weights(pointers, slot_count)
    panel = lax.all_gather(features, "row", axis=0, tiled=True)
    panel_blocks = panel.reshape(group_blocks, block_size, panel.shape[1])
    blocks = panel_blocks[columns]
    panel_width = blocks.shape[2]
    products = jnp.einsum("sij,sjk->sik", values, blocks, preferred_element_type=jnp.float32)
    summed = jnp.einsum("rs,sik->rik", weights, products, precision=lax.Precision.HIGHEST)
    partial_value = summed.reshape(local_rows * block_size, panel_width)
    return lax.psum_scatter(partial_value, "col", scatter_dimension=0, tiled=True).astype(
        jnp.bfloat16
    )


def solution(mesh):
    return jax.shard_map(
        local,
        mesh=mesh,
        in_specs=(
            P(("col", "row"), None),
            P("row", "col", None, None, None),
            P("row", "col", None),
            P("row", "col", None),
        ),
        out_specs=P(("row", "col"), None),
        check_vma=False,
    )
```

profile of v0, /device:TPU:0, one launch (start us, length us, event | category | flops | bytes accessed | tf_op | source)
XLA Modules:
  0.0 294.7 jit_solution(13050265332513122472)
XLA Ops:
  6.5 0.0 all-gather.2.cloned.1.call-start
  6.5 0.7 all-gather.2.cloned.1.call-update
  7.3 0.0 reduce-scatter.2.cloned.1.call-start
  7.3 0.7 compare_select_fusion
  8.0 0.8 slice_bitcast_fusion.1
  8.8 57.4 %all-gather.2.cloned.1.call-done = bf16[16384,256]{1,0:T(8,128)(2,1)} async-done(((bf16[2048,256]{1,0:T(8,128)(2,1)}), bf16[16384,256]{1,0:T(8,128)(2,1)}) %all-gather.2.cloned.1.call-update) | async-done | bytes 8388624 | tf_op jit(solution)/shard_map/all_gather | solution.py:22
  66.2 11.7 %gather_fusion = bf16[192,128,256]{2,1,0:T(8,128)(2,1)} fusion(bf16[128,128,256]{2,1,0:T(8,128)(2,1)} %bitcast.20, s32[1024]{0:T(1024)S(1)} %pad_clamp_fusion), kind=kCustom, calls=%fused_computation | custom fusion | bytes 25166592 | tf_op jit(solution)/shard_map/gather | solution.py:24
  77.9 13.8 %fusion.2 = f32[192,256,128]{2,1,0:T(8,128)} fusion(bf16[192,128,256]{2,1,0:T(8,128)(2,1)} %gather_fusion, bf16[1,1,192,128,128]{4,3,2,1,0:T(8,128)(2,1)} %param.5), kind=kOutput, calls=%fused_computation.3 | convolution fusion | flops 1610612736 | bytes 44040192 | tf_op jit(solution)/shard_map/sij,sjk->sik/dot_general | solution.py:26
  91.7 24.9 %copy.6 = f32[192,256,128]{1,0,2:T(8,128)} copy(f32[192,256,128]{2,1,0:T(8,128)} %fusion.2) | data formatting | bytes 50331648 | tf_op jit(solution)/shard_map/sij,sjk->sik/dot_general | solution.py:26
  116.6 15.7 %fusion = f32[64,128,256]{2,0,1:T(8,128)S(1)} fusion(f32[192,256,128]{1,0,2:T(8,128)} %copy.6, s32[64]{0:T(128)S(1)} %get-tuple-element.6, s32[64]{0:T(128)S(1)} %get-tuple-element.5), kind=kOutput, calls=%fused_computation.1 | convolution fusion | flops 4831875072 | bytes 33554944 | tf_op jit(solution)/shard_map/rs,sik->rik/dot_general | solution.py:27
  132.3 8.1 %copy.5 = f32[64,128,256]{2,1,0:T(8,128)} copy(f32[64,128,256]{2,0,1:T(8,128)S(1)} %fusion) | data formatting | bytes 16777216 | tf_op jit(solution)/shard_map/rs,sik->rik/dot_general | solution.py:27
  140.4 0.0 reduce-scatter.2.cloned.1.call-update
  140.4 144.8 %reduce-scatter.2.cloned.1.call-done = f32[2048,256]{1,0:T(8,128)} async-done(((f32[8192,256]{1,0:T(8,128)}), f32[2048,256]{1,0:T(8,128)}) %reduce-scatter.2.cloned.1.call-update) | async-done | bytes 2097168 | tf_op jit(solution)/shard_map/reduce_scatter | solution.py:29
  285.2 2.7 convert_element_type.4
  (1 shorter events, 0.0 us)
Async XLA Ops:
  6.5 59.7 %all-gather.2.cloned.1.call-start = ((), (), s32[]{:S(2)}) async-start(), calls=%async_computation.1 | async-start | bytes 9437184 | tf_op jit(solution)/shard_map/all_gather | solution.py:22
  7.3 277.9 %reduce-scatter.2.cloned.1.call-start = ((), (), s32[]{:S(2)}) async-start(), calls=%async_computation.2 | async-start | bytes 10485760 | tf_op jit(solution)/shard_map/reduce_scatter | solution.py:29
Sparse Core Ops, SparseCore 0:
  9.2 56.9 all-gather.1
  140.5 144.6 reduce-scatter.1
where the time goes:
time: 295 us
  waiting for transfers between devices  203 us (69%)
  local copies, waits for them, and re-layouts  45.4 us (15%)
  matrix products  29.5 us (10%)
  between operations  13.4 us (5%)
  other arithmetic  3.35 us (1%)
    reduce_scatter x1, waiting for transfers between devices, local(): lax.psum_scatter(partial_value, 'col', scatter_dimension=0, tiled=True)  145 us
    all_gather x1, waiting for transfers between devices, local(): panel = lax.all_gather(features, 'row', axis=0, tiled=True)  57.4 us
    dot_general x1, local copies, waits for them, and re-layouts, local(): jnp.einsum('sij,sjk->sik', values, blocks, preferred_element_type=jnp.flo...  24.9 us
    dot_general x1, matrix products, local(): jnp.einsum('rs,sik->rik', weights, products, precision=lax.Precision.HIGH...  15.7 us
    dot_general x1, matrix products, local(): jnp.einsum('sij,sjk->sik', values, blocks, preferred_element_type=jnp.flo...  13.8 us
    gather x1, local copies, waits for them, and re-layouts, local(): blocks = panel_blocks[columns]  11.7 us
    dot_general x1, local copies, waits for them, and re-layouts, local(): jnp.einsum('rs,sik->rik', weights, products, precision=lax.Precision.HIGH...  8.07 us
  transfers between devices with their start and end apart: 2, of which 2 were waited for; matrix products, arithmetic and copies ran while one was open for 1% of the time, Pallas kernels for 0%

commit v1 on v0

v1 whole, which is shorter than its diff:
```python
import functools

import jax
import jax.numpy as jnp
from jax import lax
from jax.experimental import pallas as pl
from jax.experimental.pallas import tpu as pltpu
from jax.sharding import PartitionSpec as P


LANES = 128
UNROLL = 8
MIB = 1 << 20
CHUNKS = (4, 4, 2)
TOP = 32700.0
STEPS = 8.0
TINY = 2.0**-110


def code_of(peak):
    return jnp.ceil(jnp.log2(jnp.maximum(peak, TINY)) * STEPS)


def encode(y):
    code = code_of(jnp.max(jnp.abs(y), axis=0, keepdims=True))
    coded = jnp.round(y * (jnp.exp2(code * (-1.0 / STEPS)) * TOP))
    return coded.astype(jnp.int32).astype(jnp.int16), code


def scale_of(codes):
    return jnp.exp2(codes.astype(jnp.float32) * (1.0 / STEPS)) * (1.0 / TOP)


def rows_of(i, size):
    return pl.ds(pl.multiple_of(i * size, size), size)


def params(mib):
    return pltpu.CompilerParams(vmem_limit_bytes=mib * MIB)


def turn_kernel(block, sizes, x_ref, *out_refs):
    @pl.loop(0, out_refs[0].shape[0])
    def _(j):
        y = x_ref[rows_of(j, block), :].T
        at = 0
        for width, out_ref in zip(sizes, out_refs):
            out_ref[j] = y[at : at + width, :]
            at += width


def turn(features, block, place, sizes):
    rows = features.shape[0]
    mine, width = rows // block, sum(sizes)
    whole = lambda shape: pl.BlockSpec(shape, functools.partial(lambda n, i: (0,) * n, len(shape)))
    shapes = [(mine, size, block) for size in sizes]
    return pl.pallas_call(
        functools.partial(turn_kernel, block, sizes),
        out_shape=[jax.ShapeDtypeStruct(shape, features.dtype) for shape in shapes],
        grid=(1,),
        in_specs=[pl.BlockSpec((rows, width), lambda i: (0, place))],
        out_specs=[whole(shape) for shape in shapes],
        compiler_params=params(8),
        cost_estimate=pl.CostEstimate(flops=1 << 26, bytes_accessed=1 << 20, transcendentals=0),
    )(features)


def stage_kernel(
    owner_of, mine, pointer_ref, column_ref, values_ref, range_ref, index_ref, row_ref, store_ref, sem
):
    local_rows = pointer_ref.shape[0] - 1
    slots = column_ref.shape[0]
    count = pointer_ref[local_rows]
    steps = (count + UNROLL - 1) // UNROLL

    def copy(t):
        span = pl.ds(t * UNROLL, UNROLL)
        return pltpu.make_async_copy(values_ref.at[span], store_ref.at[span], sem.at[t])

    @pl.loop(0, steps)
    def _(t):
        copy(t).start()

    row, col = lax.axis_index("row"), lax.axis_index("col")
    group = mine * lax.axis_size("row")

    @pl.loop(0, slots)
    def _(s):
        column = column_ref[s] - col * group
        device = lax.div(column, mine)
        index_ref[s] = (device ^ row) * mine + column - device * mine
        row_ref[s] = local_rows

    @pl.loop(0, local_rows)
    def _(i):
        @pl.loop(pointer_ref[i], pointer_ref[i + 1])
        def _(s):
            row_ref[s] = i

    owned = local_rows // lax.axis_size("col")
    for m, owner in enumerate(owner_of(col)):
        first = jnp.clip(owner, 0, lax.axis_size("col") - 1) * owned
        range_ref[3 * m] = pointer_ref[first]
        range_ref[3 * m + 1] = pointer_ref[first + owned]
        range_ref[3 * m + 2] = first

    @pl.loop(0, steps)
    def _(t):
        copy(t).wait()


def stage(pointers, columns, values, owner_of, count, mine):
    smem = pl.BlockSpec(memory_space=pltpu.SMEM)
    slots = values.shape[0]
    return pl.pallas_call(
        functools.partial(stage_kernel, owner_of, mine),
        out_shape=[
            jax.ShapeDtypeStruct((3 * count,), jnp.int32),
            jax.ShapeDtypeStruct((slots,), jnp.int32),
            jax.ShapeDtypeStruct((slots,), jnp.int32),
            jax.ShapeDtypeStruct(values.shape, values.dtype),
        ],
        in_specs=[smem, smem, pl.BlockSpec(memory_space=pltpu.HBM)],
        out_specs=[smem] * 3 + [pl.BlockSpec(memory_space=pltpu.VMEM)],
        scratch_shapes=[pltpu.SemaphoreType.DMA((slots // UNROLL,))],
        compiler_params=params(8),
        cost_estimate=pl.CostEstimate(flops=1 << 26, bytes_accessed=1 << 22, transcendentals=0),
    )(pointers, columns, values)


def product_kernel(sizes, range_ref, index_ref, row_ref, store, *refs):
    pieces, start, messages, own, owned, mine, width = sizes
    piece_refs = refs[:pieces]
    out_refs = refs[pieces : pieces + messages + own]
    panel, scratch, codes = refs[pieces + messages + own :]

    for p in range(pieces):

        @pl.loop(0, mine)
        def _(j):
            panel[p * mine + j] = piece_refs[p][j]

    for m in range(messages + own):
        low, high, first_row = (range_ref[3 * (start + m) + n] for n in range(3))
        acc = scratch if m < messages else out_refs[m]

        @pl.loop(0, owned)
        def _(i):
            acc[i] = jnp.zeros((width, LANES), jnp.float32)

        @pl.loop(0, (high - low + UNROLL - 1) // UNROLL)
        def _(t):
            terms = []
            for u in range(UNROLL):
                s = low + t * UNROLL + u
                terms.append(
                    lax.dot_general(
                        panel[index_ref[s]],
                        store[s],
                        (((1,), (1,)), ((), ())),
                        preferred_element_type=jnp.float32,
                    )
                )
            for u in range(UNROLL):
                s = low + t * UNROLL + u
                acc[jnp.where(s < high, row_ref[s] - first_row, owned)] += terms[u]

        if m < messages:

            @pl.loop(0, owned)
            def _(i):
                y, code = encode(acc[i])
                out_refs[m][rows_of(i, width), :] = y
                codes[pl.ds(i, 1), :] = code

            tail = codes.shape[0]
            out_refs[m][owned * width : owned * width + tail, :] = (
                codes[...].astype(jnp.int32).astype(jnp.int16)
            )


def products(ranges, index, rows, store, pieces, owned, start, messages, own):
    slots, block = store.shape[:2]
    mine, width = pieces[0].shape[:2]
    tail = -(-owned // 16) * 16
    length = owned * width + tail
    smem = pl.BlockSpec(memory_space=pltpu.SMEM)
    whole = pl.BlockSpec(memory_space=pltpu.VMEM)
    flops = 2 * slots * block * block * width
    return pl.pallas_call(
        functools.partial(
            product_kernel, (len(pieces), start, messages, own, owned, mine, width)
        ),
        out_shape=[jax.ShapeDtypeStruct((length, block), jnp.int16)] * messages
        + [jax.ShapeDtypeStruct((owned + 1, width, block), jnp.float32)] * own,
        in_specs=[smem] * 3 + [whole] * (1 + len(pieces)),
        out_specs=[whole] * (messages + own),
        scratch_shapes=[
            pltpu.VMEM((len(pieces) * mine, width, block), store.dtype),
            pltpu.VMEM((owned + 1, width, block), jnp.float32),
            pltpu.VMEM((tail, block), jnp.float32),
        ],
        compiler_params=params(20),
        cost_estimate=pl.CostEstimate(flops=2 * flops, bytes_accessed=1 << 23, transcendentals=0),
    )(ranges, index, rows, store, *pieces)


def decoded(ref, codes, i, width):
    q = ref[rows_of(i, width), :]
    return q.astype(jnp.int32).astype(jnp.float32) * codes[pl.ds(i, 1), :]


def merge_kernel(width, owned, *refs):
    *in_refs, out_ref, codes, new = refs
    for n, ref in enumerate(in_refs):
        codes[n] = scale_of(ref[owned * width :, :].astype(jnp.int32))

    @pl.loop(0, owned)
    def _(i):
        total = sum(decoded(ref, codes.at[n], i, width) for n, ref in enumerate(in_refs))
        y, code = encode(total)
        out_ref[rows_of(i, width), :] = y
        new[pl.ds(i, 1), :] = code

    out_ref[owned * width :, :] = new[...].astype(jnp.int32).astype(jnp.int16)


def merge(terms, width, owned):
    length, block = terms[0].shape
    tail = length - owned * width
    whole = pl.BlockSpec(memory_space=pltpu.VMEM)
    return pl.pallas_call(
        functools.partial(merge_kernel, width, owned),
        out_shape=jax.ShapeDtypeStruct((length, block), jnp.int16),
        in_specs=[whole] * len(terms),
        out_specs=whole,
        scratch_shapes=[
            pltpu.VMEM((len(terms), tail, block), jnp.float32),
            pltpu.VMEM((tail, block), jnp.float32),
        ],
        compiler_params=params(6),
        cost_estimate=pl.CostEstimate(
            flops=1 << 28, bytes_accessed=3 * length * width * 2, transcendentals=0
        ),
    )(*terms)


def finish_kernel(owned, groups, *refs):
    out_ref, total = refs[-2:]
    block = total.shape[1]
    refs = refs[:-2]

    @pl.loop(0, owned)
    def _(i):
        at, offset = 0, 0
        for width, terms in groups:
            y = refs[at][i]
            for ref in refs[at + 1 : at + 1 + terms]:
                scale = scale_of(ref[owned * width :, :].astype(jnp.int32))
                here = lax.broadcasted_iota(jnp.int32, scale.shape, 0) == i
                row = jnp.sum(jnp.where(here, scale, 0.0), axis=0, keepdims=True)
                y = y + ref[rows_of(i, width), :].astype(jnp.int32).astype(jnp.float32) * row
            total[offset : offset + width, :] = y
            at, offset = at + 1 + terms, offset + width
        out_ref[rows_of(i, block), :] = total[...].T.astype(out_ref.dtype)


def finish(groups, owned_rows, place, spans, earlier):
    arrays, sizes = [], []
    for own, got in groups:
        arrays += [own, *got]
        sizes.append((own.shape[1], len(got)))
    owned, block = owned_rows, groups[0][0].shape[2]
    width = sum(size for size, _ in sizes)
    specs = [pl.BlockSpec(a.shape, functools.partial(lambda n, i: (0,) * n, a.ndim)) for a in arrays]
    aliases = {}
    if earlier is not None:
        aliases = {len(arrays): 0}
        arrays.append(earlier)
        specs.append(pl.BlockSpec(memory_space=pl.ANY))
    return pl.pallas_call(
        functools.partial(finish_kernel, owned, sizes),
        out_shape=jax.ShapeDtypeStruct((owned * block, width * spans), jnp.bfloat16),
        grid=(1,),
        in_specs=specs,
        out_specs=pl.BlockSpec((owned * block, width), lambda i: (0, place)),
        scratch_shapes=[pltpu.VMEM((width, block), jnp.float32)],
        input_output_aliases=aliases,
        compiler_params=params(16),
        cost_estimate=pl.CostEstimate(
            flops=1 << 28, bytes_accessed=1 << 22, transcendentals=0
        ),
    )(*arrays)


def gather(part, devices):
    pieces = []
    for p in range(0, devices, 2):
        near = part if p == 0 else lax.ppermute(part, "row", [(d, d ^ p) for d in range(devices)])
        pieces += [near, lax.ppermute(near, "row", [(d, d ^ 1) for d in range(devices)])]
    return pieces


def plan(count):
    out = []
    for d in range(count - 1, 0, -1):
        right = [(z, z + d) for z in range(count - d)]
        left = [(z, z - d) for z in range(d, count)]
        out.append((d, right, left, count - 1 - d < d - 1 or (d == 2 and count == 4)))
    return out


def reduce(kinds, messages, width, owned):
    got = []
    relayed = {}
    for (d, side, pairs), message in zip(kinds, messages):
        sides = ("right", "left") if side == "both" else (side,)
        incoming = []
        fed = set()
        for s in sides:
            for array in relayed.get((d + 1, s), []):
                if not any(array is a for a in incoming):
                    incoming.append(array)
            fed |= relayed.get((d + 1, s, "to"), set())
        if d >= 3:
            if incoming:
                message = merge([message] + incoming, width, owned)
            hops = [(a, a + 1 if b > a else a - 1) for a, b in pairs]
            array = lax.ppermute(message, "col", hops)
            for s in sides:
                relayed.setdefault((d, s), []).append(array)
                relayed.setdefault((d, s, "to"), set()).update(
                    b for a, b in hops if (b > a) == (s == "right")
                )
        else:
            plain = [pair for pair in pairs if pair[0] not in fed]
            late = [pair for pair in pairs if pair[0] in fed]
            if plain:
                got.append(lax.ppermute(message, "col", plain))
            if late:
                merged = merge([message] + incoming, width, owned)
                got.append(lax.ppermute(merged, "col", late))
    return got


def local(features, block_values, row_ptr, block_cols):
    values = block_values[0, 0]
    pointers = row_ptr[0, 0]
    block = values.shape[1]
    row_count, col_count = lax.axis_size("row"), lax.axis_size("col")
    mine = features.shape[0] // block
    total_width = features.shape[1]
    owned = (pointers.shape[0] - 1) // col_count

    kinds = []
    for d, right, left, both in plan(col_count):
        if both:
            kinds.append((d, "both", right + left))
        else:
            kinds.append((d, "right", right))
            kinds.append((d, "left", left))

    def owner_of(col):
        for d, side, _ in kinds:
            right = side == "right" if side != "both" else col + d < col_count
            yield jnp.where(right, col + d, col - d)
        yield col

    widths = [total_width // part for part in CHUNKS]
    turned, taken = [], []
    for width in widths:
        taken.append(width)
        if sum(taken) % LANES == 0:
            turned += turn(features, block, sum(widths[: len(turned)]) // LANES, taken)
            taken = []
    parts = [gather(piece, row_count) for piece in turned]
    ranges, index, rows, store = stage(
        pointers, block_cols[0, 0], values, owner_of, len(kinds) + 1, mine
    )
    groups, filled, out = [], 0, None
    for width, pieces in zip(widths, parts):
        lead = products(ranges, index, rows, store, pieces, owned, 0, 1, 0)
        *others, own = products(
            ranges, index, rows, store, pieces, owned, 1, len(kinds) - 1, 1
        )
        groups.append((own, reduce(kinds, [*lead, *others], width, owned)))
        filled += width
        if filled % LANES == 0:
            out = finish(groups, owned, filled // LANES - 1, total_width // LANES, out)
            groups = []
    return out


def solution(mesh):
    return jax.shard_map(
        local,
        mesh=mesh,
        in_specs=(
            P(("col", "row"), None),
            P("row", "col", None, None, None),
            P("row", "col", None),
            P("row", "col", None),
        ),
        out_specs=P(("row", "col"), None),
        check_vma=False,
    )
```

time: 295 us -> 174 us (0.59)
  waiting for transfers between devices: 203 us -> 77.6 us
  starting transfers between devices: 0.04 us -> 49.2 us
  Pallas kernels: 0 us -> 41.1 us
  local copies, waits for them, and re-layouts: 45.4 us -> 5.34 us
  matrix products: 29.5 us -> 0 us
  between operations: 13.4 us -> 0.35 us
  other arithmetic: 3.35 us -> 0 us
    reduce_scatter x1 -> x0, waiting for transfers between devices: 145 us -> none  [local(): lax.psum_scatter(partial_value, 'col', scatter_dimension=0, tiled=True)]
    ppermute x0 -> x36, waiting for transfers between devices: none -> 77.6 us  [the longest x3 35.3 us: reduce(): got.append(lax.ppermute(merged, 'col', late))]
    all_gather x1 -> x0, waiting for transfers between devices: 57.4 us -> none  [local(): panel = lax.all_gather(features, 'row', axis=0, tiled=True)]
    ppermute x0 -> x36, starting transfers between devices: none -> 49.2 us  [the longest x9 21.9 us: reduce(): got.append(lax.ppermute(message, 'col', plain))]
    pallas_call x0 -> x14, Pallas kernels: none -> 41.1 us  [the longest x6 26.2 us: products(): pl.pallas_call(functools.partial(product_kernel, (len(pieces), start, mes...]
    dot_general x2 -> x0, local copies, waits for them, and re-layouts: 33 us -> none  [the longest x1 24.9 us: local(): jnp.einsum('sij,sjk->sik', values, blocks, preferred_element_type=jnp.flo...]
    dot_general x2 -> x0, matrix products: 29.5 us -> none  [the longest x1 15.7 us: local(): jnp.einsum('rs,sik->rik', weights, products, precision=lax.Precision.HIGH...]
    gather x1 -> x0, local copies, waits for them, and re-layouts: 11.7 us -> none  [local(): blocks = panel_blocks[columns]]
  transfers between devices with their start and end apart: 2 -> 36, of which waited for: 2 -> 10; matrix products, arithmetic and copies ran while one was open for 1% -> 0% of each run, Pallas kernels for 0% -> 21%
where the time goes in v1:
time: 174 us
  waiting for transfers between devices  77.6 us (45%)
  starting transfers between devices  49.2 us (28%)
  Pallas kernels  41.1 us (24%)
  local copies, waits for them, and re-layouts  5.34 us (3%)
    ppermute x3, waiting for transfers between devices, reduce(): got.append(lax.ppermute(merged, 'col', late))  35.3 us
    ppermute x9, waiting for transfers between devices, gather(): lax.ppermute(part, 'row', [(d, d ^ p) for d in range(devices)])  33.7 us
    pallas_call x6, Pallas kernels, products(): pl.pallas_call(functools.partial(product_kernel, (len(pieces), start, mes...  26.2 us
    ppermute x9, starting transfers between devices, reduce(): got.append(lax.ppermute(message, 'col', plain))  21.9 us
    ppermute x9, starting transfers between devices, gather(): lax.ppermute(part, 'row', [(d, d ^ p) for d in range(devices)])  15.1 us
    ppermute x3, starting transfers between devices, reduce(): array = lax.ppermute(message, 'col', hops)  6.03 us
    pallas_call x2, Pallas kernels, finish(): pl.pallas_call(functools.partial(finish_kernel, owned, sizes), out_shape=...  5.78 us
    unnamed x8, local copies, waits for them, and re-layouts  5.34 us
  transfers between devices with their start and end apart: 36, of which 10 were waited for; matrix products, arithmetic and copies ran while one was open for 0% of the time, Pallas kernels for 21%

profile of v1, /device:TPU:0, one launch (start us, length us, event | category | flops | bytes accessed | tf_op | source)
XLA Modules:
  0.0 173.7 jit_solution(15564290354422379614)
XLA Ops:
  2.4 3.0 %collective-permute-start.25 = (bf16[16,64,128]{2,1,0:T(8,128)(2,1)S(1)}, bf16[16,64,128]{2,1,0:T(8,128)(2,1)S(1)}, u32[]{:S(2)}, u32[]{:S(2)}) collective-permute-start(bf16[16,64,128]{2,1,0:T(8,128)(2,1)S(1)} %get-tuple-element.36.refs_0_), channel_id=1, source_target_pairs={{0,8},{4,12},{8,0},{12,4},{16,24},{20,28},{24,16},{28,20},{1,9},{5... | collective-permute-start | bytes 786440 | tf_op jit(solution)/shard_map/ppermute | solution.py:299
  9.0 3.7 %collective-permute-done.25.refs_2_ = bf16[16,64,128]{2,1,0:T(8,128)(2,1)S(1)} collective-permute-done((bf16[16,64,128]{2,1,0:T(8,128)(2,1)S(1)}, bf16[16,64,128]{2,1,0:T(8,128)(2,1)S(1)}, u32[]{:S(2)}, u32[]{:S(2)}) %collective-permute-start.25) | collective-permute-done | bytes 262176 | tf_op jit(solution)/shard_map/ppermute | solution.py:299
  12.6 2.0 %collective-permute-start.15 = (bf16[16,64,128]{2,1,0:T(8,128)(2,1)S(1)}, bf16[16,64,128]{2,1,0:T(8,128)(2,1)S(1)}, u32[]{:S(2)}, u32[]{:S(2)}) collective-permute-start(bf16[16,64,128]{2,1,0:T(8,128)(2,1)S(1)} %get-tuple-element.31.refs_0_), channel_id=1, source_target_pairs={{0,16},{4,20},{8,24},{12,28},{16,0},{20,4},{24,8},{28,12},{1,17},{... | collective-permute-start | bytes 786440 | tf_op jit(solution)/shard_map/ppermute | solution.py:299
  15.9 3.4 %collective-permute-done.27.refs_4_ = bf16[16,64,128]{2,1,0:T(8,128)(2,1)S(1)} collective-permute-done((bf16[16,64,128]{2,1,0:T(8,128)(2,1)S(1)}, bf16[16,64,128]{2,1,0:T(8,128)(2,1)S(1)}, u32[]{:S(2)}, u32[]{:S(2)}) %collective-permute-start.27) | collective-permute-done | bytes 262176 | tf_op jit(solution)/shard_map/ppermute | solution.py:299
  19.8 2.0 %collective-permute-start.3 = (bf16[16,128,128]{2,1,0:T(8,128)(2,1)S(1)}, bf16[16,128,128]{2,1,0:T(8,128)(2,1)S(1)}, u32[]{:S(2)}, u32[]{:S(2)}) collective-permute-start(bf16[16,128,128]{2,1,0:T(8,128)(2,1)S(1)} %shard_map.47.refs_0_), channel_id=1, source_target_pairs={{0,16},{4,20},{8,24},{12,28},{16,0},{20,4},{24,8},{28,12},{1,17},{... | collective-permute-start | bytes 1572872 | tf_op jit(solution)/shard_map/ppermute | solution.py:299
  23.9 3.0 %collective-permute-start.17 = (bf16[16,64,128]{2,1,0:T(8,128)(2,1)S(1)}, bf16[16,64,128]{2,1,0:T(8,128)(2,1)S(1)}, u32[]{:S(2)}, u32[]{:S(2)}) collective-permute-start(bf16[16,64,128]{2,1,0:T(8,128)(2,1)S(1)} %get-tuple-element.31.refs_0_), channel_id=1, source_target_pairs={{0,24},{4,28},{8,16},{12,20},{16,8},{20,12},{24,0},{28,4},{1,25},{... | collective-permute-start | bytes 786440 | tf_op jit(solution)/shard_map/ppermute | solution.py:299
  26.9 25.6 %collective-permute-done.17.refs_6_ = bf16[16,64,128]{2,1,0:T(8,128)(2,1)S(1)} collective-permute-done((bf16[16,64,128]{2,1,0:T(8,128)(2,1)S(1)}, bf16[16,64,128]{2,1,0:T(8,128)(2,1)S(1)}, u32[]{:S(2)}, u32[]{:S(2)}) %collective-permute-start.17) | collective-permute-done | bytes 262176 | tf_op jit(solution)/shard_map/ppermute | solution.py:299
  54.1 3.2 %collective-permute-done.30.refs_7_ = bf16[16,64,128]{2,1,0:T(8,128)(2,1)S(1)} collective-permute-done((bf16[16,64,128]{2,1,0:T(8,128)(2,1)S(1)}, bf16[16,64,128]{2,1,0:T(8,128)(2,1)S(1)}, u32[]{:S(2)}, u32[]{:S(2)}) %collective-permute-start.30) | collective-permute-done | bytes 262176 | tf_op jit(solution)/shard_map/ppermute | solution.py:300
  58.4 2.8 %copy-done = bf16[1,1,192,128,128]{4,3,2,1,0:T(8,128)(2,1)S(1)} copy-done((bf16[1,1,192,128,128]{4,3,2,1,0:T(8,128)(2,1)S(1)}, bf16[1,1,192,128,128]{4,3,2,1,0:T(8,128)(2,1)}, u32[]{:S(2)}) %copy-start) | copy-done | bytes 6291480
  62.5 4.5 %shard_map.46 = (s32[15]{0:T(128)S(1)}, s32[192]{0:T(256)S(1)}, s32[192]{0:T(256)S(1)}, bf16[192,128,128]{2,1,0:T(8,128)(2,1)S(1)}) custom-call(s32[65]{0:T(128)S(1)} %bitcast.5, s32[192]{0:T(256)S(1)} %bitcast.4, bf16[192,128,128]{2,1,0:T(8,128)(2,1)S(1)} %bitcast.3), custom_call_target="tpu_custom_call" | custom-call | flops 67108864 | bytes 4194304 | tf_op jit(solution)/shard_map/pallas_call | solution.py:115
  67.0 2.6 %shard_map.56 = s16[1040,128]{1,0:T(8,128)(2,1)S(1)} custom-call(s32[15]{0:T(128)S(1)} %get-tuple-element.23.range_ref, s32[192]{0:T(256)S(1)} %get-tuple-element.24.index_ref, s32[192]{0:T(256)S(1)} %get-tuple-element.25.row_ref, bf16[192,128,128]{2,1,0:T(8,128)(2,1)S(1)} %get-tuple-element.26.store, bf16[16,64,128]{2,1,0:T(8,128)(2,1)S(1)} %get-tuple-element.36.refs_0_, ...), custom_call_target="tpu_custom_call" | custom-call | flops 805306368 | bytes 8388608 | tf_op jit(solution)/shard_map/pallas_call | solution.py:190
  69.6 3.4 %collective-permute-start.32 = (s16[1040,128]{1,0:T(8,128)(2,1)S(1)}, s16[1040,128]{1,0:T(8,128)(2,1)S(1)}, u32[]{:S(2)}, u32[]{:S(2)}) collective-permute-start(s16[1040,128]{1,0:T(8,128)(2,1)S(1)} %shard_map.56), channel_id=1, source_target_pairs={{0,1},{3,2},{4,5},{7,6},{8,9},{11,10},{12,13},{15,14},{16,17},{19,... | collective-permute-start | bytes 798728 | tf_op jit(solution)/shard_map/ppermute | solution.py:329
  73.0 2.7 %shard_map.49 = s16[2064,128]{1,0:T(8,128)(2,1)S(1)} custom-call(s32[15]{0:T(128)S(1)} %get-tuple-element.23.range_ref, s32[192]{0:T(256)S(1)} %get-tuple-element.24.index_ref, s32[192]{0:T(256)S(1)} %get-tuple-element.25.row_ref, bf16[192,128,128]{2,1,0:T(8,128)(2,1)S(1)} %get-tuple-element.26.store, bf16[16,128,128]{2,1,0:T(8,128)(2,1)S(1)} %shard_map.47.refs_0_, ...), custom_call_target="tpu_custom_call" | custom-call | flops 1610612736 | bytes 8388608 | tf_op jit(solution)/shard_map/pallas_call | solution.py:190
  77.1 2.6 %shard_map.53 = s16[1040,128]{1,0:T(8,128)(2,1)S(1)} custom-call(s32[15]{0:T(128)S(1)} %get-tuple-element.23.range_ref, s32[192]{0:T(256)S(1)} %get-tuple-element.24.index_ref, s32[192]{0:T(256)S(1)} %get-tuple-element.25.row_ref, bf16[192,128,128]{2,1,0:T(8,128)(2,1)S(1)} %get-tuple-element.26.store, bf16[16,64,128]{2,1,0:T(8,128)(2,1)S(1)} %get-tuple-element.31.refs_0_, ...), custom_call_target="tpu_custom_call" | custom-call | flops 805306368 | bytes 8388608 | tf_op jit(solution)/shard_map/pallas_call | solution.py:190
  81.0 5.9 %shard_map.55 = (s16[1040,128]{1,0:T(8,128)(2,1)S(1)}, s16[1040,128]{1,0:T(8,128)(2,1)S(1)}, s16[1040,128]{1,0:T(8,128)(2,1)S(1)}, f32[17,64,128]{2,1,0:T(8,128)S(1)}) custom-call(s32[15]{0:T(128)S(1)} %get-tuple-element.23.range_ref, s32[192]{0:T(256)S(1)} %get-tuple-element.24.index_ref, s32[192]{0:T(256)S(1)} %get-tuple-element.25.row_ref, ...), custom_call_target="tpu_custom_call" | custom-call | flops 805306368 | bytes 8388608 | tf_op jit(solution)/shard_map/pallas_call | solution.py:190
  88.3 5.9 %shard_map.52 = (s16[1040,128]{1,0:T(8,128)(2,1)S(1)}, s16[1040,128]{1,0:T(8,128)(2,1)S(1)}, s16[1040,128]{1,0:T(8,128)(2,1)S(1)}, f32[17,64,128]{2,1,0:T(8,128)S(1)}) custom-call(s32[15]{0:T(128)S(1)} %get-tuple-element.23.range_ref, s32[192]{0:T(256)S(1)} %get-tuple-element.24.index_ref, s32[192]{0:T(256)S(1)} %get-tuple-element.25.row_ref, ...), custom_call_target="tpu_custom_call" | custom-call | flops 805306368 | bytes 8388608 | tf_op jit(solution)/shard_map/pallas_call | solution.py:190
  98.1 4.4 %collective-permute-done.31.refs_6_ = s16[1040,128]{1,0:T(8,128)(2,1)S(1)} collective-permute-done((s16[1040,128]{1,0:T(8,128)(2,1)S(1)}, s16[1040,128]{1,0:T(8,128)(2,1)S(1)}, u32[]{:S(2)}, u32[]{:S(2)}) %collective-permute-start.31) | collective-permute-done | bytes 266272 | tf_op jit(solution)/shard_map/ppermute | solution.py:339
  102.5 5.2 %collective-permute-start.22 = (s16[1040,128]{1,0:T(8,128)(2,1)S(1)}, s16[1040,128]{1,0:T(8,128)(2,1)S(1)}, u32[]{:S(2)}, u32[]{:S(2)}) collective-permute-start(s16[1040,128]{1,0:T(8,128)(2,1)S(1)} %get-tuple-element.34), channel_id=1, source_target_pairs={{0,1},{1,2},{2,3},{4,5},{5,6},{6,7},{8,9},{9,10},{10,11},{12,13},{... | collective-permute-start | bytes 798728 | tf_op jit(solution)/shard_map/ppermute | solution.py:339
  111.5 6.5 %shard_map.48 = (s16[2064,128]{1,0:T(8,128)(2,1)S(1)}, s16[2064,128]{1,0:T(8,128)(2,1)S(1)}, s16[2064,128]{1,0:T(8,128)(2,1)S(1)}, f32[17,128,128]{2,1,0:T(8,128)S(1)}) custom-call(s32[15]{0:T(128)S(1)} %get-tuple-element.23.range_ref, s32[192]{0:T(256)S(1)} %get-tuple-element.24.index_ref, s32[192]{0:T(256)S(1)} %get-tuple-element.25.row_ref, ...), custom_call_target="tpu_custom_call" | custom-call | flops 1610612736 | bytes 8388608 | tf_op jit(solution)/shard_map/pallas_call | solution.py:190
  118.9 7.0 %collective-permute-start.7 = (s16[2064,128]{1,0:T(8,128)(2,1)S(1)}, s16[2064,128]{1,0:T(8,128)(2,1)S(1)}, u32[]{:S(2)}, u32[]{:S(2)}) collective-permute-start(s16[2064,128]{1,0:T(8,128)(2,1)S(1)} %get-tuple-element.28.refs_0_), channel_id=1, source_target_pairs={{0,2},{3,1},{4,6},{7,5},{8,10},{11,9},{12,14},{15,13},{16,18},{19,... | collective-permute-start | bytes 1585160 | tf_op jit(solution)/shard_map/ppermute | solution.py:339
  125.9 2.0 %collective-permute-start.10 = (s16[2064,128]{1,0:T(8,128)(2,1)S(1)}, s16[2064,128]{1,0:T(8,128)(2,1)S(1)}, u32[]{:S(2)}, u32[]{:S(2)}) collective-permute-start(s16[2064,128]{1,0:T(8,128)(2,1)S(1)} %get-tuple-element.29), channel_id=1, source_target_pairs={{0,1},{1,2},{2,3},{4,5},{5,6},{6,7},{8,9},{9,10},{10,11},{12,13},{... | collective-permute-start | bytes 1585160 | tf_op jit(solution)/shard_map/ppermute | solution.py:339
  132.5 35.3 %collective-permute-done.21.refs_2_ = s16[1040,128]{1,0:T(8,128)(2,1)S(1)} collective-permute-done((s16[1040,128]{1,0:T(8,128)(2,1)S(1)}, s16[1040,128]{1,0:T(8,128)(2,1)S(1)}, u32[]{:S(2)}, u32[]{:S(2)}) %collective-permute-start.21) | collective-permute-done | bytes 266272 | tf_op jit(solution)/shard_map/ppermute | solution.py:342
  167.9 3.0 %shard_map.58.refs_5_ = bf16[2048,256]{1,0:T(8,128)(2,1)} custom-call(f32[17,64,128]{2,1,0:T(8,128)S(1)} %get-tuple-element.32.refs_0_, s16[1040,128]{1,0:T(8,128)(2,1)S(1)} %collective-permute-done.19.refs_1_, s16[1040,128]{1,0:T(8,128)(2,1)S(1)} %collective-permute-done.21.refs_2_, s16[1040,128]{1,0:T(8,128)(2,1)S(1)} %collective-permute-done.22.refs_3_, ...), custom_call_target="tpu_custom_call" | custom-call | flops 268435456 | bytes 4194304 | tf_op jit(solution)/shard_map/pallas_call | solution.py:281
  170.9 2.8 %shard_map.59 = bf16[2048,256]{1,0:T(8,128)(2,1)} custom-call(f32[17,128,128]{2,1,0:T(8,128)S(1)} %get-tuple-element.27.refs_0_, s16[2064,128]{1,0:T(8,128)(2,1)S(1)} %collective-permute-done.7.refs_1_, s16[2064,128]{1,0:T(8,128)(2,1)S(1)} %collective-permute-done.9.refs_2_, ...), custom_call_target="tpu_custom_call", output_to_operand_aliasing={{}: (5, {})} | custom-call | flops 268435456 | bytes 4194304 | tf_op jit(solution)/shard_map/pallas_call | solution.py:281
  (70 shorter events, 30.8 us)
Async XLA Ops:
  7.0 16.9 %collective-permute-start.13 = (bf16[16,64,128]{2,1,0:T(8,128)(2,1)S(1)}, bf16[16,64,128]{2,1,0:T(8,128)(2,1)S(1)}, u32[]{:S(2)}, u32[]{:S(2)}) collective-permute-start(bf16[16,64,128]{2,1,0:T(8,128)(2,1)S(1)} %get-tuple-element.31.refs_0_), channel_id=1, source_target_pairs={{0,8},{4,12},{8,0},{12,4},{16,24},{20,28},{24,16},{28,20},{1,9},{5... | collective-permute-start | bytes 786440 | tf_op jit(solution)/shard_map/ppermute | solution.py:299
  19.3 33.7 %collective-permute-start.1 = (bf16[16,128,128]{2,1,0:T(8,128)(2,1)S(1)}, bf16[16,128,128]{2,1,0:T(8,128)(2,1)S(1)}, u32[]{:S(2)}, u32[]{:S(2)}) collective-permute-start(bf16[16,128,128]{2,1,0:T(8,128)(2,1)S(1)} %shard_map.47.refs_0_), channel_id=1, source_target_pairs={{0,8},{4,12},{8,0},{12,4},{16,24},{20,28},{24,16},{28,20},{1,9},{5... | collective-permute-start | bytes 1572872 | tf_op jit(solution)/shard_map/ppermute | solution.py:299
  19.8 33.3 %collective-permute-start.3 = (bf16[16,128,128]{2,1,0:T(8,128)(2,1)S(1)}, bf16[16,128,128]{2,1,0:T(8,128)(2,1)S(1)}, u32[]{:S(2)}, u32[]{:S(2)}) collective-permute-start(bf16[16,128,128]{2,1,0:T(8,128)(2,1)S(1)} %shard_map.47.refs_0_), channel_id=1, source_target_pairs={{0,16},{4,20},{8,24},{12,28},{16,0},{20,4},{24,8},{28,12},{1,17},{... | collective-permute-start | bytes 1572872 | tf_op jit(solution)/shard_map/ppermute | solution.py:299
  21.8 31.7 %collective-permute-start.5 = (bf16[16,128,128]{2,1,0:T(8,128)(2,1)S(1)}, bf16[16,128,128]{2,1,0:T(8,128)(2,1)S(1)}, u32[]{:S(2)}, u32[]{:S(2)}) collective-permute-start(bf16[16,128,128]{2,1,0:T(8,128)(2,1)S(1)} %shard_map.47.refs_0_), channel_id=1, source_target_pairs={{0,24},{4,28},{8,16},{12,20},{16,8},{20,12},{24,0},{28,4},{1,25},{... | collective-permute-start | bytes 1572872 | tf_op jit(solution)/shard_map/ppermute | solution.py:299
  23.9 28.5 %collective-permute-start.17 = (bf16[16,64,128]{2,1,0:T(8,128)(2,1)S(1)}, bf16[16,64,128]{2,1,0:T(8,128)(2,1)S(1)}, u32[]{:S(2)}, u32[]{:S(2)}) collective-permute-start(bf16[16,64,128]{2,1,0:T(8,128)(2,1)S(1)} %get-tuple-element.31.refs_0_), channel_id=1, source_target_pairs={{0,24},{4,28},{8,16},{12,20},{16,8},{20,12},{24,0},{28,4},{1,25},{... | collective-permute-start | bytes 786440 | tf_op jit(solution)/shard_map/ppermute | solution.py:299
  26.9 25.6 %collective-permute-start.26 = (bf16[16,64,128]{2,1,0:T(8,128)(2,1)S(1)}, bf16[16,64,128]{2,1,0:T(8,128)(2,1)S(1)}, u32[]{:S(2)}, u32[]{:S(2)}) collective-permute-start(bf16[16,64,128]{2,1,0:T(8,128)(2,1)S(1)} %collective-permute-done.25.refs_2_), channel_id=1, source_target_pairs={{0,4},{4,0},{8,12},{12,8},{16,20},{20,16},{24,28},{28,24},{1,5},{5... | collective-permute-start | bytes 786440 | tf_op jit(solution)/shard_map/ppermute | solution.py:300
  53.5 16.1 %collective-permute-start.6 = (bf16[16,128,128]{2,1,0:T(8,128)(2,1)S(1)}, bf16[16,128,128]{2,1,0:T(8,128)(2,1)S(1)}, u32[]{:S(2)}, u32[]{:S(2)}) collective-permute-start(bf16[16,128,128]{2,1,0:T(8,128)(2,1)S(1)} %collective-permute-done.5.refs_6_), channel_id=1, source_target_pairs={{0,4},{4,0},{8,12},{12,8},{16,20},{20,16},{24,28},{28,24},{1,5},{5... | collective-permute-start | bytes 1572872 | tf_op jit(solution)/shard_map/ppermute | solution.py:300
  57.4 18.4 %collective-permute-start.12 = (bf16[16,64,128]{2,1,0:T(8,128)(2,1)S(1)}, bf16[16,64,128]{2,1,0:T(8,128)(2,1)S(1)}, u32[]{:S(2)}, u32[]{:S(2)}) collective-permute-start(bf16[16,64,128]{2,1,0:T(8,128)(2,1)S(1)} %get-tuple-element.31.refs_0_), channel_id=1, source_target_pairs={{0,4},{4,0},{8,12},{12,8},{16,20},{20,16},{24,28},{28,24},{1,5},{5... | collective-permute-start | bytes 786440 | tf_op jit(solution)/shard_map/ppermute | solution.py:300
  57.5 19.6 %collective-permute-start.14 = (bf16[16,64,128]{2,1,0:T(8,128)(2,1)S(1)}, bf16[16,64,128]{2,1,0:T(8,128)(2,1)S(1)}, u32[]{:S(2)}, u32[]{:S(2)}) collective-permute-start(bf16[16,64,128]{2,1,0:T(8,128)(2,1)S(1)} %collective-permute-done.13.refs_2_), channel_id=1, source_target_pairs={{0,4},{4,0},{8,12},{12,8},{16,20},{20,16},{24,28},{28,24},{1,5},{5... | collective-permute-start | bytes 786440 | tf_op jit(solution)/shard_map/ppermute | solution.py:300
  57.9 19.2 %collective-permute-start.16 = (bf16[16,64,128]{2,1,0:T(8,128)(2,1)S(1)}, bf16[16,64,128]{2,1,0:T(8,128)(2,1)S(1)}, u32[]{:S(2)}, u32[]{:S(2)}) collective-permute-start(bf16[16,64,128]{2,1,0:T(8,128)(2,1)S(1)} %collective-permute-done.15.refs_4_), channel_id=1, source_target_pairs={{0,4},{4,0},{8,12},{12,8},{16,20},{20,16},{24,28},{28,24},{1,5},{5... | collective-permute-start | bytes 786440 | tf_op jit(solution)/shard_map/ppermute | solution.py:300
  58.0 19.1 %collective-permute-start.18 = (bf16[16,64,128]{2,1,0:T(8,128)(2,1)S(1)}, bf16[16,64,128]{2,1,0:T(8,128)(2,1)S(1)}, u32[]{:S(2)}, u32[]{:S(2)}) collective-permute-start(bf16[16,64,128]{2,1,0:T(8,128)(2,1)S(1)} %collective-permute-done.17.refs_6_), channel_id=1, source_target_pairs={{0,4},{4,0},{8,12},{12,8},{16,20},{20,16},{24,28},{28,24},{1,5},{5... | collective-permute-start | bytes 786440 | tf_op jit(solution)/shard_map/ppermute | solution.py:300
  69.6 25.9 %collective-permute-start.32 = (s16[1040,128]{1,0:T(8,128)(2,1)S(1)}, s16[1040,128]{1,0:T(8,128)(2,1)S(1)}, u32[]{:S(2)}, u32[]{:S(2)}) collective-permute-start(s16[1040,128]{1,0:T(8,128)(2,1)S(1)} %shard_map.56), channel_id=1, source_target_pairs={{0,1},{3,2},{4,5},{7,6},{8,9},{11,10},{12,13},{15,14},{16,17},{19,... | collective-permute-start | bytes 798728 | tf_op jit(solution)/shard_map/ppermute | solution.py:329
  75.8 34.4 %collective-permute-start.8 = (s16[2064,128]{1,0:T(8,128)(2,1)S(1)}, s16[2064,128]{1,0:T(8,128)(2,1)S(1)}, u32[]{:S(2)}, u32[]{:S(2)}) collective-permute-start(s16[2064,128]{1,0:T(8,128)(2,1)S(1)} %shard_map.49), channel_id=1, source_target_pairs={{0,1},{3,2},{4,5},{7,6},{8,9},{11,10},{12,13},{15,14},{16,17},{19,... | collective-permute-start | bytes 1585160 | tf_op jit(solution)/shard_map/ppermute | solution.py:329
  79.7 17.1 %collective-permute-start.20 = (s16[1040,128]{1,0:T(8,128)(2,1)S(1)}, s16[1040,128]{1,0:T(8,128)(2,1)S(1)}, u32[]{:S(2)}, u32[]{:S(2)}) collective-permute-start(s16[1040,128]{1,0:T(8,128)(2,1)S(1)} %shard_map.53), channel_id=1, source_target_pairs={{0,1},{3,2},{4,5},{7,6},{8,9},{11,10},{12,13},{15,14},{16,17},{19,... | collective-permute-start | bytes 798728 | tf_op jit(solution)/shard_map/ppermute | solution.py:329
  95.5 23.4 %collective-permute-start.34 = (s16[1040,128]{1,0:T(8,128)(2,1)S(1)}, s16[1040,128]{1,0:T(8,128)(2,1)S(1)}, u32[]{:S(2)}, u32[]{:S(2)}) collective-permute-start(s16[1040,128]{1,0:T(8,128)(2,1)S(1)} %get-tuple-element.39), channel_id=1, source_target_pairs={{0,1},{1,2},{2,3},{4,5},{5,6},{6,7},{8,9},{9,10},{10,11},{12,13},{... | collective-permute-start | bytes 798728 | tf_op jit(solution)/shard_map/ppermute | solution.py:339
  96.8 29.1 %collective-permute-start.35 = (s16[1040,128]{1,0:T(8,128)(2,1)S(1)}, s16[1040,128]{1,0:T(8,128)(2,1)S(1)}, u32[]{:S(2)}, u32[]{:S(2)}) collective-permute-start(s16[1040,128]{1,0:T(8,128)(2,1)S(1)} %get-tuple-element.40), channel_id=1, source_target_pairs={{1,0},{2,1},{3,2},{5,4},{6,5},{7,6},{9,8},{10,9},{11,10},{13,12},{... | collective-permute-start | bytes 798728 | tf_op jit(solution)/shard_map/ppermute | solution.py:339
  102.5 25.4 %collective-permute-start.22 = (s16[1040,128]{1,0:T(8,128)(2,1)S(1)}, s16[1040,128]{1,0:T(8,128)(2,1)S(1)}, u32[]{:S(2)}, u32[]{:S(2)}) collective-permute-start(s16[1040,128]{1,0:T(8,128)(2,1)S(1)} %get-tuple-element.34), channel_id=1, source_target_pairs={{0,1},{1,2},{2,3},{4,5},{5,6},{6,7},{8,9},{9,10},{10,11},{12,13},{... | collective-permute-start | bytes 798728 | tf_op jit(solution)/shard_map/ppermute | solution.py:339
  108.2 21.0 %collective-permute-start.23 = (s16[1040,128]{1,0:T(8,128)(2,1)S(1)}, s16[1040,128]{1,0:T(8,128)(2,1)S(1)}, u32[]{:S(2)}, u32[]{:S(2)}) collective-permute-start(s16[1040,128]{1,0:T(8,128)(2,1)S(1)} %get-tuple-element.35), channel_id=1, source_target_pairs={{1,0},{2,1},{3,2},{5,4},{6,5},{7,6},{9,8},{10,9},{11,10},{13,12},{... | collective-permute-start | bytes 798728 | tf_op jit(solution)/shard_map/ppermute | solution.py:339
  110.2 21.0 %collective-permute-start.33 = (s16[1040,128]{1,0:T(8,128)(2,1)S(1)}, s16[1040,128]{1,0:T(8,128)(2,1)S(1)}, u32[]{:S(2)}, u32[]{:S(2)}) collective-permute-start(s16[1040,128]{1,0:T(8,128)(2,1)S(1)} %shard_map.57), channel_id=1, source_target_pairs={{1,3},{2,0},{5,7},{6,4},{9,11},{10,8},{13,15},{14,12},{17,19},{18,... | collective-permute-start | bytes 798728 | tf_op jit(solution)/shard_map/ppermute | solution.py:342
  118.9 51.9 %collective-permute-start.7 = (s16[2064,128]{1,0:T(8,128)(2,1)S(1)}, s16[2064,128]{1,0:T(8,128)(2,1)S(1)}, u32[]{:S(2)}, u32[]{:S(2)}) collective-permute-start(s16[2064,128]{1,0:T(8,128)(2,1)S(1)} %get-tuple-element.28.refs_0_), channel_id=1, source_target_pairs={{0,2},{3,1},{4,6},{7,5},{8,10},{11,9},{12,14},{15,13},{16,18},{19,... | collective-permute-start | bytes 1585160 | tf_op jit(solution)/shard_map/ppermute | solution.py:339
  125.9 44.9 %collective-permute-start.10 = (s16[2064,128]{1,0:T(8,128)(2,1)S(1)}, s16[2064,128]{1,0:T(8,128)(2,1)S(1)}, u32[]{:S(2)}, u32[]{:S(2)}) collective-permute-start(s16[2064,128]{1,0:T(8,128)(2,1)S(1)} %get-tuple-element.29), channel_id=1, source_target_pairs={{0,1},{1,2},{2,3},{4,5},{5,6},{6,7},{8,9},{9,10},{10,11},{12,13},{... | collective-permute-start | bytes 1585160 | tf_op jit(solution)/shard_map/ppermute | solution.py:339
  127.9 42.9 %collective-permute-start.11 = (s16[2064,128]{1,0:T(8,128)(2,1)S(1)}, s16[2064,128]{1,0:T(8,128)(2,1)S(1)}, u32[]{:S(2)}, u32[]{:S(2)}) collective-permute-start(s16[2064,128]{1,0:T(8,128)(2,1)S(1)} %get-tuple-element.30), channel_id=1, source_target_pairs={{1,0},{2,1},{3,2},{5,4},{6,5},{7,6},{9,8},{10,9},{11,10},{13,12},{... | collective-permute-start | bytes 1585160 | tf_op jit(solution)/shard_map/ppermute | solution.py:339
  129.2 41.6 %collective-permute-start.9 = (s16[2064,128]{1,0:T(8,128)(2,1)S(1)}, s16[2064,128]{1,0:T(8,128)(2,1)S(1)}, u32[]{:S(2)}, u32[]{:S(2)}) collective-permute-start(s16[2064,128]{1,0:T(8,128)(2,1)S(1)} %shard_map.50), channel_id=1, source_target_pairs={{1,3},{2,0},{5,7},{6,4},{9,11},{10,8},{13,15},{14,12},{17,19},{18,... | collective-permute-start | bytes 1585160 | tf_op jit(solution)/shard_map/ppermute | solution.py:342
  131.2 36.6 %collective-permute-start.21 = (s16[1040,128]{1,0:T(8,128)(2,1)S(1)}, s16[1040,128]{1,0:T(8,128)(2,1)S(1)}, u32[]{:S(2)}, u32[]{:S(2)}) collective-permute-start(s16[1040,128]{1,0:T(8,128)(2,1)S(1)} %shard_map.54), channel_id=1, source_target_pairs={{1,3},{2,0},{5,7},{6,4},{9,11},{10,8},{13,15},{14,12},{17,19},{18,... | collective-permute-start | bytes 798728 | tf_op jit(solution)/shard_map/ppermute | solution.py:342
  (16 other events, 120.7 us)

commit v2 on v1

v2 whole, which is shorter than its diff:
```python
import functools

import jax
import jax.numpy as jnp
from jax import lax
from jax.experimental import pallas as pl
from jax.experimental.pallas import tpu as pltpu
from jax.sharding import PartitionSpec as P


LANES = 128
UNROLL = 16
MIB = 1 << 20
CHUNKS = (8, 8)
TOP = 32700.0
STEPS = 8.0
TINY = 2.0**-110


def code_of(peak):
    return jnp.ceil(jnp.log2(jnp.maximum(peak, TINY)) * STEPS)


def encode(y):
    code = code_of(jnp.max(jnp.abs(y), axis=0, keepdims=True))
    coded = jnp.round(y * (jnp.exp2(code * (-1.0 / STEPS)) * TOP))
    return coded.astype(jnp.int32).astype(jnp.int16), code


def scale_of(codes):
    return jnp.exp2(codes.astype(jnp.float32) * (1.0 / STEPS)) * (1.0 / TOP)


def rows_of(i, size):
    return pl.ds(pl.multiple_of(i * size, size), size)


def params(mib):
    return pltpu.CompilerParams(vmem_limit_bytes=mib * MIB)


def turn_kernel(block, first, x_ref, out_ref):
    mine, width = out_ref.shape[:2]
    aligned, last = first // LANES * LANES, first + width
    end = -(-last // LANES) * LANES

    @pl.loop(0, mine, unroll=4)
    def _(j):
        y = x_ref[rows_of(j, block), aligned:end].T
        out_ref[j] = y[first - aligned : last - aligned, :]


def turn(features, block, first, width):
    mine = features.shape[0] // block
    whole = pl.BlockSpec(memory_space=pltpu.VMEM)
    return pl.pallas_call(
        functools.partial(turn_kernel, block, first),
        out_shape=jax.ShapeDtypeStruct((mine, width, block), features.dtype),
        in_specs=[whole],
        out_specs=whole,
        compiler_params=params(4),
        cost_estimate=pl.CostEstimate(flops=1 << 26, bytes_accessed=1 << 20, transcendentals=0),
    )(features)


def stage_kernel(
    owner_of, mine, pointer_ref, column_ref, values_ref, range_ref, index_ref, row_ref, store_ref
):
    local_rows = pointer_ref.shape[0] - 1
    slots = column_ref.shape[0]
    row, col = lax.axis_index("row"), lax.axis_index("col")
    group = mine * lax.axis_size("row")

    @pl.loop(0, slots, unroll=4)
    def _(s):
        column = column_ref[s] - col * group
        device = lax.div(column, mine)
        index_ref[s] = (device ^ row) * mine + column - device * mine
        row_ref[s] = local_rows

    @pl.loop(0, local_rows)
    def _(i):
        @pl.loop(pointer_ref[i], pointer_ref[i + 1])
        def _(s):
            row_ref[s] = i

    owned = local_rows // lax.axis_size("col")
    for m, owner in enumerate(owner_of(col)):
        first = jnp.clip(owner, 0, lax.axis_size("col") - 1) * owned
        sent = (owner >= 0) & (owner < lax.axis_size("col"))
        range_ref[3 * m] = jnp.where(sent, pointer_ref[first], 0)
        range_ref[3 * m + 1] = jnp.where(sent, pointer_ref[first + owned], 0)
        range_ref[3 * m + 2] = first
    range_ref[3 * m + 3] = pointer_ref[local_rows]

    @pl.loop(0, (pointer_ref[local_rows] + 3) // 4)
    def _(t):
        for u in range(4):
            store_ref[4 * t + u] = values_ref[4 * t + u].T


def stage(pointers, columns, values, owner_of, count, mine):
    smem = pl.BlockSpec(memory_space=pltpu.SMEM)
    whole = pl.BlockSpec(memory_space=pltpu.VMEM)
    slots = columns.shape[0]
    return pl.pallas_call(
        functools.partial(stage_kernel, owner_of, mine),
        out_shape=[
            jax.ShapeDtypeStruct((3 * count + 1,), jnp.int32),
            jax.ShapeDtypeStruct((slots,), jnp.int32),
            jax.ShapeDtypeStruct((slots,), jnp.int32),
            jax.ShapeDtypeStruct(values.shape, values.dtype),
        ],
        in_specs=[smem, smem, whole],
        out_specs=[smem] * 3 + [whole],
        compiler_params=params(4),
        cost_estimate=pl.CostEstimate(flops=1 << 26, bytes_accessed=1 << 12, transcendentals=0),
    )(pointers, columns, values)


def add_slots(low, high, spare, offset, index_ref, row_ref, store, panel, acc):
    @pl.loop(0, (high - low + UNROLL - 1) // UNROLL)
    def _(t):
        terms = []
        for u in range(UNROLL):
            s = low + t * UNROLL + u
            terms.append(
                jnp.dot(panel[index_ref[s]], store[s], preferred_element_type=jnp.float32)
            )
        for u in range(UNROLL):
            s = low + t * UNROLL + u
            acc[jnp.where(s < high, row_ref[s] - offset, spare)] += terms[u]


def write_message(acc, first, out_ref, codes, owned, width):
    @pl.loop(0, owned, unroll=4)
    def _(i):
        y, code = encode(acc[first + i])
        out_ref[rows_of(i, width), :] = y
        codes[pl.ds(i, 1), :] = code

    out_ref[owned * width :, :] = codes[...].astype(jnp.int32).astype(jnp.int16)


def clear(acc, count):
    @pl.loop(0, count, unroll=4)
    def _(i):
        acc[i] = jnp.zeros(acc.shape[1:], acc.dtype)


def head_kernel(owned, range_ref, index_ref, row_ref, store, *refs):
    *piece_refs, out_ref, panel, acc, codes = refs
    mine, width = piece_refs[0].shape[:2]

    for p, ref in enumerate(piece_refs):

        @pl.loop(0, mine, unroll=4)
        def _(j):
            panel[p * mine + j] = ref[j]

    clear(acc, owned)
    low, high, first = (range_ref[n] for n in range(3))
    add_slots(low, high, owned, first, index_ref, row_ref, store, panel, acc)
    write_message(acc, 0, out_ref, codes, owned, width)


def rest_kernel(owned, messages, local_rows, range_ref, index_ref, row_ref, store, panel, *refs):
    out_refs = refs[:messages]
    own_ref, acc, codes = refs[messages:]
    width = panel.shape[1]
    clear(acc, local_rows)
    low, high, total = range_ref[0], range_ref[1], range_ref[3 * messages + 6]
    add_slots(0, low, local_rows, 0, index_ref, row_ref, store, panel, acc)
    add_slots(high, total, local_rows, 0, index_ref, row_ref, store, panel, acc)
    for m, out_ref in enumerate(out_refs):
        write_message(acc, range_ref[3 * m + 5], out_ref, codes, owned, width)
    first = range_ref[3 * messages + 5]

    @pl.loop(0, owned, unroll=4)
    def _(i):
        own_ref[i] = acc[first + i]


def head(ranges, index, rows, store, pieces, owned):
    slots, block = store.shape[:2]
    mine, width = pieces[0].shape[:2]
    tail = -(-owned // 16) * 16
    smem = pl.BlockSpec(memory_space=pltpu.SMEM)
    whole = pl.BlockSpec(memory_space=pltpu.VMEM)
    flops = slots * block * block * width
    return pl.pallas_call(
        functools.partial(head_kernel, owned),
        out_shape=[
            jax.ShapeDtypeStruct((owned * width + tail, block), jnp.int16),
            jax.ShapeDtypeStruct((len(pieces) * mine, width, block), store.dtype),
        ],
        in_specs=[smem] * 3 + [whole] * (1 + len(pieces)),
        out_specs=[whole] * 2,
        scratch_shapes=[
            pltpu.VMEM((owned + 1, width, block), jnp.float32),
            pltpu.VMEM((tail, block), jnp.float32),
        ],
        compiler_params=params(10),
        cost_estimate=pl.CostEstimate(flops=flops, bytes_accessed=1 << 22, transcendentals=0),
    )(ranges, index, rows, store, *pieces)


def rest(ranges, index, rows, store, panel, owned, local_rows, messages):
    slots, block = store.shape[:2]
    width = panel.shape[1]
    tail = -(-owned // 16) * 16
    smem = pl.BlockSpec(memory_space=pltpu.SMEM)
    whole = pl.BlockSpec(memory_space=pltpu.VMEM)
    flops = 2 * slots * block * block * width
    return pl.pallas_call(
        functools.partial(rest_kernel, owned, messages, local_rows),
        out_shape=[jax.ShapeDtypeStruct((owned * width + tail, block), jnp.int16)] * messages
        + [jax.ShapeDtypeStruct((owned, width, block), jnp.float32)],
        in_specs=[smem] * 3 + [whole] * 2,
        out_specs=[whole] * (messages + 1),
        scratch_shapes=[
            pltpu.VMEM((local_rows + 1, width, block), jnp.float32),
            pltpu.VMEM((tail, block), jnp.float32),
        ],
        compiler_params=params(12),
        cost_estimate=pl.CostEstimate(flops=flops, bytes_accessed=1 << 22, transcendentals=0),
    )(ranges, index, rows, store, panel)


def decoded(ref, codes, i, width):
    q = ref[rows_of(i, width), :]
    return q.astype(jnp.int32).astype(jnp.float32) * codes[pl.ds(i, 1), :]


def merge_kernel(width, owned, *refs):
    *in_refs, out_ref, codes, new = refs
    for n, ref in enumerate(in_refs):
        codes[n] = scale_of(ref[owned * width :, :].astype(jnp.int32))

    @pl.loop(0, owned, unroll=4)
    def _(i):
        total = sum(decoded(ref, codes.at[n], i, width) for n, ref in enumerate(in_refs))
        y, code = encode(total)
        out_ref[rows_of(i, width), :] = y
        new[pl.ds(i, 1), :] = code

    out_ref[owned * width :, :] = new[...].astype(jnp.int32).astype(jnp.int16)


def merge(terms, width, owned):
    length, block = terms[0].shape
    tail = length - owned * width
    whole = pl.BlockSpec(memory_space=pltpu.VMEM)
    return pl.pallas_call(
        functools.partial(merge_kernel, width, owned),
        out_shape=jax.ShapeDtypeStruct((length, block), jnp.int16),
        in_specs=[whole] * len(terms),
        out_specs=whole,
        scratch_shapes=[
            pltpu.VMEM((len(terms), tail, block), jnp.float32),
            pltpu.VMEM((tail, block), jnp.float32),
        ],
        compiler_params=params(6),
        cost_estimate=pl.CostEstimate(
            flops=1 << 28, bytes_accessed=3 * length * width * 2, transcendentals=0
        ),
    )(*terms)


def finish_kernel(owned, parts, *refs):
    count = sum(1 + part[3] for part in parts)
    out_ref = refs[-2 - sum(part[3] for part in parts)]
    total, codes = refs[-1 - sum(part[3] for part in parts)], refs[-sum(part[3] for part in parts) :]
    in_refs = refs[:count]
    block = total.shape[2]

    at, n = 0, 0
    for width, _, _, terms in parts:
        for ref in in_refs[at + 1 : at + 1 + terms]:
            codes[n][...] = scale_of(ref[owned * width :, :].astype(jnp.int32))
            n += 1
        at += 1 + terms

    @pl.loop(0, owned // 2, unroll=2)
    def _(h):
        for k in range(2):
            i = 2 * h + k
            at, n, offset = 0, 0, 0
            for width, first, last, terms in parts:
                y = in_refs[at][i, first:last, :]
                for ref in in_refs[at + 1 : at + 1 + terms]:
                    rows = pl.ds(pl.multiple_of(i * width + first, 16), last - first)
                    y = y + ref[rows, :].astype(jnp.int32).astype(jnp.float32) * codes[n][pl.ds(i, 1), :]
                    n += 1
                total[k, offset : offset + last - first, :] = y
                at, offset = at + 1 + terms, offset + last - first
            out_ref[rows_of(i, block), :] = total[k].T.astype(out_ref.dtype)


def finish(parts, owned, place, spans, earlier):
    arrays, sizes = [], []
    for own, got, first, last in parts:
        arrays += [own, *got]
        sizes.append((own.shape[1], first, last, len(got)))
    block = own.shape[2]
    tail = got[0].shape[0] - owned * own.shape[1]
    specs = [pl.BlockSpec(a.shape, functools.partial(lambda n, i: (0,) * n, a.ndim)) for a in arrays]
    aliases = {}
    if earlier is not None:
        aliases = {len(arrays): 0}
        arrays.append(earlier)
        specs.append(pl.BlockSpec(memory_space=pl.ANY))
    return pl.pallas_call(
        functools.partial(finish_kernel, owned, sizes),
        out_shape=jax.ShapeDtypeStruct((owned * block, LANES * spans), jnp.bfloat16),
        grid=(1,),
        in_specs=specs,
        out_specs=pl.BlockSpec((owned * block, LANES), lambda i: (0, place)),
        scratch_shapes=[pltpu.VMEM((2, LANES, block), jnp.float32)]
        + [pltpu.VMEM((tail, block), jnp.float32)] * sum(size[3] for size in sizes),
        input_output_aliases=aliases,
        compiler_params=params(12),
        cost_estimate=pl.CostEstimate(
            flops=1 << 28, bytes_accessed=1 << 22, transcendentals=0
        ),
    )(*arrays)


def gather(part, devices):
    pieces = []
    for p in range(0, devices, 2):
        near = part if p == 0 else lax.ppermute(part, "row", [(d, d ^ p) for d in range(devices)])
        pieces += [near, lax.ppermute(near, "row", [(d, d ^ 1) for d in range(devices)])]
    return pieces


def plan(count):
    out = []
    for d in range(count - 1, 0, -1):
        right = [(z, z + d) for z in range(count - d)]
        left = [(z, z - d) for z in range(d, count)]
        out.append((d, right, left, count - 1 - d < d - 1 or (d == 2 and count == 4)))
    return out


def reduce(kinds, messages, width, owned):
    got = []
    relayed = {}
    for (d, side, pairs), message in zip(kinds, messages):
        sides = ("right", "left") if side == "both" else (side,)
        incoming = []
        for s in sides:
            for array in relayed.get((d + 1, s), []):
                if not any(array is a for a in incoming):
                    incoming.append(array)
        if d >= 3:
            if incoming:
                message = merge([message] + incoming, width, owned)
            hops = [(a, a + 1 if b > a else a - 1) for a, b in pairs]
            array = lax.ppermute(message, "col", hops)
            for s in sides:
                relayed.setdefault((d, s), []).append(array)
        elif incoming:
            merged = merge([message] + incoming, width, owned)
            got.append(lax.ppermute(merged, "col", pairs))
        else:
            got.append(lax.ppermute(message, "col", pairs))
    return got


def local(features, block_values, row_ptr, block_cols):
    values = block_values[0, 0]
    pointers = row_ptr[0, 0]
    block = values.shape[1]
    row_count, col_count = lax.axis_size("row"), lax.axis_size("col")
    mine = features.shape[0] // block
    total_width = features.shape[1]
    owned = (pointers.shape[0] - 1) // col_count

    kinds = []
    for d, right, left, both in plan(col_count):
        if both:
            kinds.append((d, "both", right + left))
        else:
            kinds.append((d, "right", right))
            kinds.append((d, "left", left))

    def owner_of(col):
        for d, side, _ in kinds:
            right = side == "right" if side != "both" else col + d < col_count
            yield jnp.where(right, col + d, col - d)
        yield col

    starts = [total_width * sum(CHUNKS[:n]) // sum(CHUNKS) for n in range(len(CHUNKS) + 1)]
    parts = []
    for first, last in zip(starts, starts[1:]):
        piece = turn(features, block, first, last - first)
        parts.append(gather(piece, row_count))
    ranges, index, rows, store = stage(
        pointers, block_cols[0, 0], values, owner_of, len(kinds) + 1, mine
    )
    sums, written, out = [], 0, None
    for chunk, pieces in enumerate(parts):
        lead, panel = head(ranges, index, rows, store, pieces, owned)
        *others, own = rest(
            ranges, index, rows, store, panel, owned, pointers.shape[0] - 1, len(kinds) - 1
        )
        got = reduce(kinds, [lead, *others], own.shape[1], owned)
        sums.append((own, got))
        while written + LANES <= starts[chunk + 1]:
            taken = [
                (*sums[n], max(written - first, 0), min(written + LANES, last) - first)
                for n, (first, last) in enumerate(zip(starts, starts[1:]))
                if first < written + LANES and last > written
            ]
            out = finish(taken, owned, written // LANES, total_width // LANES, out)
            written += LANES
    return out


def solution(mesh):
    return jax.shard_map(
        local,
        mesh=mesh,
        in_specs=(
            P(("col", "row"), None),
            P("row", "col", None, None, None),
            P("row", "col", None),
            P("row", "col", None),
        ),
        out_specs=P(("row", "col"), None),
        check_vma=False,
    )
```

time: 174 us -> 149 us (0.86)
  Pallas kernels: 41.1 us -> 17.7 us
  starting transfers between devices: 49.2 us -> 28.3 us
  waiting for transfers between devices: 77.6 us -> 97.4 us
    pallas_call x8 -> x6, Pallas kernels: 28.7 us -> 9.14 us  [the longest x2 5.34 us: rest(): pl.pallas_call(functools.partial(rest_kernel, owned, messages, local_rows...]
    ppermute x12 -> x6, starting transfers between devices: 25.8 us -> 13.4 us  [the longest x4 8.31 us: reduce(): got.append(lax.ppermute(message, 'col', pairs))]
    ppermute x12 -> x6, waiting for transfers between devices: 40.2 us -> 51.5 us  [the longest x2 37.2 us: reduce(): got.append(lax.ppermute(merged, 'col', pairs))]
    ppermute x9 -> x6, waiting for transfers between devices: 33.7 us -> 40 us  [gather(): lax.ppermute(part, 'row', [(d, d ^ p) for d in range(devices)])]
    ppermute x3 -> x2, waiting for transfers between devices: 0.01 us -> 5.88 us  [reduce(): array = lax.ppermute(message, 'col', hops)]
    ppermute x9 -> x6, starting transfers between devices: 15.1 us -> 9.22 us  [gather(): lax.ppermute(part, 'row', [(d, d ^ p) for d in range(devices)])]
    ppermute x12 -> x8, waiting for transfers between devices: 3.69 us -> 0.02 us  [gather(): lax.ppermute(near, 'row', [(d, d ^ 1) for d in range(devices)])]
    pallas_call x2, Pallas kernels: 5.78 us -> 3.16 us  [finish(): pl.pallas_call(functools.partial(finish_kernel, owned, sizes), out_shape=...]
  transfers between devices with their start and end apart: 36 -> 22, of which waited for: 10 -> 10; matrix products, arithmetic and copies ran while one was open for 0% -> 0% of each run, Pallas kernels for 21% -> 11%
where the time goes in v2:
time: 149 us
  waiting for transfers between devices  97.4 us (65%)
  starting transfers between devices  28.3 us (19%)
  Pallas kernels  17.7 us (12%)
  local copies, waits for them, and re-layouts  5.34 us (4%)
    ppermute x6, waiting for transfers between devices, gather(): lax.ppermute(part, 'row', [(d, d ^ p) for d in range(devices)])  40 us
    ppermute x2, waiting for transfers between devices, reduce(): got.append(lax.ppermute(merged, 'col', pairs))  37.2 us
    ppermute x4, waiting for transfers between devices, reduce(): got.append(lax.ppermute(message, 'col', pairs))  14.3 us
    ppermute x6, starting transfers between devices, gather(): lax.ppermute(part, 'row', [(d, d ^ p) for d in range(devices)])  9.22 us
    ppermute x4, starting transfers between devices, reduce(): got.append(lax.ppermute(message, 'col', pairs))  8.31 us
    ppermute x2, waiting for transfers between devices, reduce(): array = lax.ppermute(message, 'col', hops)  5.88 us
    unnamed x8, local copies, waits for them, and re-layouts  5.34 us
    pallas_call x2, Pallas kernels, rest(): pl.pallas_call(functools.partial(rest_kernel, owned, messages, local_rows...  5.34 us
  transfers between devices with their start and end apart: 22, of which 10 were waited for; matrix products, arithmetic and copies ran while one was open for 0% of the time, Pallas kernels for 11%

profile of v2, /device:TPU:0, one launch (start us, length us, event | category | flops | bytes accessed | tf_op | source)
XLA Modules:
  0.0 149.0 jit_solution(757449606285575890)
XLA Ops:
  1.6 3.0 %collective-permute-start.12 = (bf16[16,128,128]{2,1,0:T(8,128)(2,1)S(1)}, bf16[16,128,128]{2,1,0:T(8,128)(2,1)S(1)}, u32[]{:S(2)}, u32[]{:S(2)}) collective-permute-start(bf16[16,128,128]{2,1,0:T(8,128)(2,1)S(1)} %shard_map.51.refs_0_), channel_id=1, source_target_pairs={{0,8},{4,12},{8,0},{12,4},{16,24},{20,28},{24,16},{28,20},{1,9},{5... | collective-permute-start | bytes 1572872 | tf_op jit(solution)/shard_map/ppermute | solution.py:332
  4.6 1.5 %collective-permute-start.14 = (bf16[16,128,128]{2,1,0:T(8,128)(2,1)S(1)}, bf16[16,128,128]{2,1,0:T(8,128)(2,1)S(1)}, u32[]{:S(2)}, u32[]{:S(2)}) collective-permute-start(bf16[16,128,128]{2,1,0:T(8,128)(2,1)S(1)} %shard_map.51.refs_0_), channel_id=1, source_target_pairs={{0,16},{4,20},{8,24},{12,28},{16,0},{20,4},{24,8},{28,12},{1,17},{... | collective-permute-start | bytes 1572872 | tf_op jit(solution)/shard_map/ppermute | solution.py:332
  6.5 2.0 %collective-permute-start.1 = (bf16[16,128,128]{2,1,0:T(8,128)(2,1)S(1)}, bf16[16,128,128]{2,1,0:T(8,128)(2,1)S(1)}, u32[]{:S(2)}, u32[]{:S(2)}) collective-permute-start(bf16[16,128,128]{2,1,0:T(8,128)(2,1)S(1)} %shard_map.47.refs_0_), channel_id=1, source_target_pairs={{0,8},{4,12},{8,0},{12,4},{16,24},{20,28},{24,16},{28,20},{1,9},{5... | collective-permute-start | bytes 1572872 | tf_op jit(solution)/shard_map/ppermute | solution.py:332
  8.5 8.9 %collective-permute-done.12.refs_2_ = bf16[16,128,128]{2,1,0:T(8,128)(2,1)S(1)} collective-permute-done((bf16[16,128,128]{2,1,0:T(8,128)(2,1)S(1)}, bf16[16,128,128]{2,1,0:T(8,128)(2,1)S(1)}, u32[]{:S(2)}, u32[]{:S(2)}) %collective-permute-start.12) | collective-permute-done | bytes 524320 | tf_op jit(solution)/shard_map/ppermute | solution.py:332
  17.4 2.0 %collective-permute-start.3 = (bf16[16,128,128]{2,1,0:T(8,128)(2,1)S(1)}, bf16[16,128,128]{2,1,0:T(8,128)(2,1)S(1)}, u32[]{:S(2)}, u32[]{:S(2)}) collective-permute-start(bf16[16,128,128]{2,1,0:T(8,128)(2,1)S(1)} %shard_map.47.refs_0_), channel_id=1, source_target_pairs={{0,16},{4,20},{8,24},{12,28},{16,0},{20,4},{24,8},{28,12},{1,17},{... | collective-permute-start | bytes 1572872 | tf_op jit(solution)/shard_map/ppermute | solution.py:332
  19.4 10.2 %collective-permute-done.14.refs_4_ = bf16[16,128,128]{2,1,0:T(8,128)(2,1)S(1)} collective-permute-done((bf16[16,128,128]{2,1,0:T(8,128)(2,1)S(1)}, bf16[16,128,128]{2,1,0:T(8,128)(2,1)S(1)}, u32[]{:S(2)}, u32[]{:S(2)}) %collective-permute-start.14) | collective-permute-done | bytes 524320 | tf_op jit(solution)/shard_map/ppermute | solution.py:332
  30.8 9.1 %collective-permute-done.1.refs_2_ = bf16[16,128,128]{2,1,0:T(8,128)(2,1)S(1)} collective-permute-done((bf16[16,128,128]{2,1,0:T(8,128)(2,1)S(1)}, bf16[16,128,128]{2,1,0:T(8,128)(2,1)S(1)}, u32[]{:S(2)}, u32[]{:S(2)}) %collective-permute-start.1) | collective-permute-done | bytes 524320 | tf_op jit(solution)/shard_map/ppermute | solution.py:332
  39.9 11.8 %collective-permute-done.3.refs_4_ = bf16[16,128,128]{2,1,0:T(8,128)(2,1)S(1)} collective-permute-done((bf16[16,128,128]{2,1,0:T(8,128)(2,1)S(1)}, bf16[16,128,128]{2,1,0:T(8,128)(2,1)S(1)}, u32[]{:S(2)}, u32[]{:S(2)}) %collective-permute-start.3) | collective-permute-done | bytes 524320 | tf_op jit(solution)/shard_map/ppermute | solution.py:332
  52.7 2.8 %copy-done = bf16[1,1,192,128,128]{4,3,2,1,0:T(8,128)(2,1)S(1)} copy-done((bf16[1,1,192,128,128]{4,3,2,1,0:T(8,128)(2,1)S(1)}, bf16[1,1,192,128,128]{4,3,2,1,0:T(8,128)(2,1)}, u32[]{:S(2)}) %copy-start) | copy-done | bytes 6291480
  56.9 4.4 %shard_map.46 = (s32[16]{0:T(128)S(1)}, s32[192]{0:T(256)S(1)}, s32[192]{0:T(256)S(1)}, bf16[192,128,128]{2,1,0:T(8,128)(2,1)S(1)}) custom-call(s32[65]{0:T(128)S(1)} %bitcast.5, s32[192]{0:T(256)S(1)} %bitcast.4, bf16[192,128,128]{2,1,0:T(8,128)(2,1)S(1)} %bitcast.3), custom_call_target="tpu_custom_call" | custom-call | flops 67108864 | bytes 4096 | tf_op jit(solution)/shard_map/pallas_call | solution.py:106
  61.3 1.6 %shard_map.52 = (s16[2064,128]{1,0:T(8,128)(2,1)S(1)}, bf16[128,128,128]{2,1,0:T(8,128)(2,1)S(1)}) custom-call(s32[16]{0:T(128)S(1)} %get-tuple-element.21.range_ref, s32[192]{0:T(256)S(1)} %get-tuple-element.22.index_ref, s32[192]{0:T(256)S(1)} %get-tuple-element.23.row_ref, bf16[192,128,128]{2,1,0:T(8,128)(2,1)S(1)} %get-tuple-element.24.store, ...), custom_call_target="tpu_custom_call" | custom-call | flops 402653184 | bytes 4194304 | tf_op jit(solution)/shard_map/pallas_call | solution.py:191
  62.9 2.8 %collective-permute-start.18 = (s16[2064,128]{1,0:T(8,128)(2,1)S(1)}, s16[2064,128]{1,0:T(8,128)(2,1)S(1)}, u32[]{:S(2)}, u32[]{:S(2)}) collective-permute-start(s16[2064,128]{1,0:T(8,128)(2,1)S(1)} %get-tuple-element.34), channel_id=1, source_target_pairs={{0,1},{3,2},{4,5},{7,6},{8,9},{11,10},{12,13},{15,14},{16,17},{19,... | collective-permute-start | bytes 1585160 | tf_op jit(solution)/shard_map/ppermute | solution.py:360
  65.8 1.5 %shard_map.48 = (s16[2064,128]{1,0:T(8,128)(2,1)S(1)}, bf16[128,128,128]{2,1,0:T(8,128)(2,1)S(1)}) custom-call(s32[16]{0:T(128)S(1)} %get-tuple-element.21.range_ref, s32[192]{0:T(256)S(1)} %get-tuple-element.22.index_ref, s32[192]{0:T(256)S(1)} %get-tuple-element.23.row_ref, bf16[192,128,128]{2,1,0:T(8,128)(2,1)S(1)} %get-tuple-element.24.store, ...), custom_call_target="tpu_custom_call" | custom-call | flops 402653184 | bytes 4194304 | tf_op jit(solution)/shard_map/pallas_call | solution.py:191
  68.6 2.7 %shard_map.53 = (s16[2064,128]{1,0:T(8,128)(2,1)S(1)}, s16[2064,128]{1,0:T(8,128)(2,1)S(1)}, s16[2064,128]{1,0:T(8,128)(2,1)S(1)}, f32[16,128,128]{2,1,0:T(8,128)S(1)}) custom-call(s32[16]{0:T(128)S(1)} %get-tuple-element.21.range_ref, s32[192]{0:T(256)S(1)} %get-tuple-element.22.index_ref, s32[192]{0:T(256)S(1)} %get-tuple-element.23.row_ref, ...), custom_call_target="tpu_custom_call" | custom-call | flops 805306368 | bytes 4194304 | tf_op jit(solution)/shard_map/pallas_call | solution.py:215
  74.0 2.7 %shard_map.49 = (s16[2064,128]{1,0:T(8,128)(2,1)S(1)}, s16[2064,128]{1,0:T(8,128)(2,1)S(1)}, s16[2064,128]{1,0:T(8,128)(2,1)S(1)}, f32[16,128,128]{2,1,0:T(8,128)S(1)}) custom-call(s32[16]{0:T(128)S(1)} %get-tuple-element.21.range_ref, s32[192]{0:T(256)S(1)} %get-tuple-element.22.index_ref, s32[192]{0:T(256)S(1)} %get-tuple-element.23.row_ref, ...), custom_call_target="tpu_custom_call" | custom-call | flops 805306368 | bytes 4194304 | tf_op jit(solution)/shard_map/pallas_call | solution.py:215
  78.6 5.1 %collective-permute-start.19 = (s16[2064,128]{1,0:T(8,128)(2,1)S(1)}, s16[2064,128]{1,0:T(8,128)(2,1)S(1)}, u32[]{:S(2)}, u32[]{:S(2)}) collective-permute-start(s16[2064,128]{1,0:T(8,128)(2,1)S(1)} %shard_map.54), channel_id=1, source_target_pairs={{0,2},{1,3},{2,0},{3,1},{4,6},{5,7},{6,4},{7,5},{8,10},{9,11},{10,... | collective-permute-start | bytes 1585160 | tf_op jit(solution)/shard_map/ppermute | solution.py:365
  83.7 5.7 %collective-permute-done.7.refs_1_ = s16[2064,128]{1,0:T(8,128)(2,1)S(1)} collective-permute-done((s16[2064,128]{1,0:T(8,128)(2,1)S(1)}, s16[2064,128]{1,0:T(8,128)(2,1)S(1)}, u32[]{:S(2)}, u32[]{:S(2)}) %collective-permute-start.7) | collective-permute-done | bytes 528416 | tf_op jit(solution)/shard_map/ppermute | solution.py:360
  89.4 4.4 %collective-permute-start.9 = (s16[2064,128]{1,0:T(8,128)(2,1)S(1)}, s16[2064,128]{1,0:T(8,128)(2,1)S(1)}, u32[]{:S(2)}, u32[]{:S(2)}) collective-permute-start(s16[2064,128]{1,0:T(8,128)(2,1)S(1)} %get-tuple-element.29), channel_id=1, source_target_pairs={{0,1},{1,2},{2,3},{4,5},{5,6},{6,7},{8,9},{9,10},{10,11},{12,13},{... | collective-permute-start | bytes 1585160 | tf_op jit(solution)/shard_map/ppermute | solution.py:367
  94.3 6.4 %collective-permute-done.20.refs_2_ = s16[2064,128]{1,0:T(8,128)(2,1)S(1)} collective-permute-done((s16[2064,128]{1,0:T(8,128)(2,1)S(1)}, s16[2064,128]{1,0:T(8,128)(2,1)S(1)}, u32[]{:S(2)}, u32[]{:S(2)}) %collective-permute-start.20) | collective-permute-done | bytes 528416 | tf_op jit(solution)/shard_map/ppermute | solution.py:367
  100.7 13.2 %collective-permute-done.19.refs_1_ = s16[2064,128]{1,0:T(8,128)(2,1)S(1)} collective-permute-done((s16[2064,128]{1,0:T(8,128)(2,1)S(1)}, s16[2064,128]{1,0:T(8,128)(2,1)S(1)}, u32[]{:S(2)}, u32[]{:S(2)}) %collective-permute-start.19) | collective-permute-done | bytes 528416 | tf_op jit(solution)/shard_map/ppermute | solution.py:365
  114.0 1.6 %shard_map.55.refs_4_ = bf16[2048,256]{1,0:T(8,128)(2,1)} custom-call(f32[16,128,128]{2,1,0:T(8,128)S(1)} %get-tuple-element.32.refs_0_, s16[2064,128]{1,0:T(8,128)(2,1)S(1)} %collective-permute-done.19.refs_1_, s16[2064,128]{1,0:T(8,128)(2,1)S(1)} %collective-permute-done.20.refs_2_, s16[2064,128]{1,0:T(8,128)(2,1)S(1)} %collective-permute-done.21.refs_3_), custom_call_target="tpu_custom_call" | custom-call | flops 268435456 | bytes 4194304 | tf_op jit(solution)/shard_map/pallas_call | solution.py:313
  115.5 7.9 %collective-permute-done.9.refs_2_ = s16[2064,128]{1,0:T(8,128)(2,1)S(1)} collective-permute-done((s16[2064,128]{1,0:T(8,128)(2,1)S(1)}, s16[2064,128]{1,0:T(8,128)(2,1)S(1)}, u32[]{:S(2)}, u32[]{:S(2)}) %collective-permute-start.9) | collective-permute-done | bytes 528416 | tf_op jit(solution)/shard_map/ppermute | solution.py:367
  123.4 24.0 %collective-permute-done.8.refs_1_ = s16[2064,128]{1,0:T(8,128)(2,1)S(1)} collective-permute-done((s16[2064,128]{1,0:T(8,128)(2,1)S(1)}, s16[2064,128]{1,0:T(8,128)(2,1)S(1)}, u32[]{:S(2)}, u32[]{:S(2)}) %collective-permute-start.8) | collective-permute-done | bytes 528416 | tf_op jit(solution)/shard_map/ppermute | solution.py:365
  147.4 1.6 %shard_map.56 = bf16[2048,256]{1,0:T(8,128)(2,1)} custom-call(f32[16,128,128]{2,1,0:T(8,128)S(1)} %get-tuple-element.26.refs_0_, s16[2064,128]{1,0:T(8,128)(2,1)S(1)} %collective-permute-done.8.refs_1_, s16[2064,128]{1,0:T(8,128)(2,1)S(1)} %collective-permute-done.9.refs_2_, ...), custom_call_target="tpu_custom_call", output_to_operand_aliasing={{}: (4, {})} | custom-call | flops 268435456 | bytes 4194304 | tf_op jit(solution)/shard_map/pallas_call | solution.py:313
  (39 shorter events, 11.8 us)
Async XLA Ops:
  0.0 1.2 copy-start.1
  1.6 15.8 %collective-permute-start.12 = (bf16[16,128,128]{2,1,0:T(8,128)(2,1)S(1)}, bf16[16,128,128]{2,1,0:T(8,128)(2,1)S(1)}, u32[]{:S(2)}, u32[]{:S(2)}) collective-permute-start(bf16[16,128,128]{2,1,0:T(8,128)(2,1)S(1)} %shard_map.51.refs_0_), channel_id=1, source_target_pairs={{0,8},{4,12},{8,0},{12,4},{16,24},{20,28},{24,16},{28,20},{1,9},{5... | collective-permute-start | bytes 1572872 | tf_op jit(solution)/shard_map/ppermute | solution.py:332
  4.6 25.1 %collective-permute-start.14 = (bf16[16,128,128]{2,1,0:T(8,128)(2,1)S(1)}, bf16[16,128,128]{2,1,0:T(8,128)(2,1)S(1)}, u32[]{:S(2)}, u32[]{:S(2)}) collective-permute-start(bf16[16,128,128]{2,1,0:T(8,128)(2,1)S(1)} %shard_map.51.refs_0_), channel_id=1, source_target_pairs={{0,16},{4,20},{8,24},{12,28},{16,0},{20,4},{24,8},{28,12},{1,17},{... | collective-permute-start | bytes 1572872 | tf_op jit(solution)/shard_map/ppermute | solution.py:332
  6.1 24.1 %collective-permute-start.16 = (bf16[16,128,128]{2,1,0:T(8,128)(2,1)S(1)}, bf16[16,128,128]{2,1,0:T(8,128)(2,1)S(1)}, u32[]{:S(2)}, u32[]{:S(2)}) collective-permute-start(bf16[16,128,128]{2,1,0:T(8,128)(2,1)S(1)} %shard_map.51.refs_0_), channel_id=1, source_target_pairs={{0,24},{4,28},{8,16},{12,20},{16,8},{20,12},{24,0},{28,4},{1,25},{... | collective-permute-start | bytes 1572872 | tf_op jit(solution)/shard_map/ppermute | solution.py:332
  6.2 24.1 %collective-permute-start.11 = (bf16[16,128,128]{2,1,0:T(8,128)(2,1)S(1)}, bf16[16,128,128]{2,1,0:T(8,128)(2,1)S(1)}, u32[]{:S(2)}, u32[]{:S(2)}) collective-permute-start(bf16[16,128,128]{2,1,0:T(8,128)(2,1)S(1)} %shard_map.51.refs_0_), channel_id=1, source_target_pairs={{0,4},{4,0},{8,12},{12,8},{16,20},{20,16},{24,28},{28,24},{1,5},{5... | collective-permute-start | bytes 1572872 | tf_op jit(solution)/shard_map/ppermute | solution.py:333
  6.5 33.4 %collective-permute-start.1 = (bf16[16,128,128]{2,1,0:T(8,128)(2,1)S(1)}, bf16[16,128,128]{2,1,0:T(8,128)(2,1)S(1)}, u32[]{:S(2)}, u32[]{:S(2)}) collective-permute-start(bf16[16,128,128]{2,1,0:T(8,128)(2,1)S(1)} %shard_map.47.refs_0_), channel_id=1, source_target_pairs={{0,8},{4,12},{8,0},{12,4},{16,24},{20,28},{24,16},{28,20},{1,9},{5... | collective-permute-start | bytes 1572872 | tf_op jit(solution)/shard_map/ppermute | solution.py:332
  17.4 34.3 %collective-permute-start.3 = (bf16[16,128,128]{2,1,0:T(8,128)(2,1)S(1)}, bf16[16,128,128]{2,1,0:T(8,128)(2,1)S(1)}, u32[]{:S(2)}, u32[]{:S(2)}) collective-permute-start(bf16[16,128,128]{2,1,0:T(8,128)(2,1)S(1)} %shard_map.47.refs_0_), channel_id=1, source_target_pairs={{0,16},{4,20},{8,24},{12,28},{16,0},{20,4},{24,8},{28,12},{1,17},{... | collective-permute-start | bytes 1572872 | tf_op jit(solution)/shard_map/ppermute | solution.py:332
  29.7 22.0 %collective-permute-start.5 = (bf16[16,128,128]{2,1,0:T(8,128)(2,1)S(1)}, bf16[16,128,128]{2,1,0:T(8,128)(2,1)S(1)}, u32[]{:S(2)}, u32[]{:S(2)}) collective-permute-start(bf16[16,128,128]{2,1,0:T(8,128)(2,1)S(1)} %shard_map.47.refs_0_), channel_id=1, source_target_pairs={{0,24},{4,28},{8,16},{12,20},{16,8},{20,12},{24,0},{28,4},{1,25},{... | collective-permute-start | bytes 1572872 | tf_op jit(solution)/shard_map/ppermute | solution.py:332
  30.3 21.9 %collective-permute-start.13 = (bf16[16,128,128]{2,1,0:T(8,128)(2,1)S(1)}, bf16[16,128,128]{2,1,0:T(8,128)(2,1)S(1)}, u32[]{:S(2)}, u32[]{:S(2)}) collective-permute-start(bf16[16,128,128]{2,1,0:T(8,128)(2,1)S(1)} %collective-permute-done.12.refs_2_), channel_id=1, source_target_pairs={{0,4},{4,0},{8,12},{12,8},{16,20},{20,16},{24,28},{28,24},{1,5},{5... | collective-permute-start | bytes 1572872 | tf_op jit(solution)/shard_map/ppermute | solution.py:333
  30.3 22.0 %collective-permute-start.15 = (bf16[16,128,128]{2,1,0:T(8,128)(2,1)S(1)}, bf16[16,128,128]{2,1,0:T(8,128)(2,1)S(1)}, u32[]{:S(2)}, u32[]{:S(2)}) collective-permute-start(bf16[16,128,128]{2,1,0:T(8,128)(2,1)S(1)} %collective-permute-done.14.refs_4_), channel_id=1, source_target_pairs={{0,4},{4,0},{8,12},{12,8},{16,20},{20,16},{24,28},{28,24},{1,5},{5... | collective-permute-start | bytes 1572872 | tf_op jit(solution)/shard_map/ppermute | solution.py:333
  39.9 21.4 %collective-permute-start.17 = (bf16[16,128,128]{2,1,0:T(8,128)(2,1)S(1)}, bf16[16,128,128]{2,1,0:T(8,128)(2,1)S(1)}, u32[]{:S(2)}, u32[]{:S(2)}) collective-permute-start(bf16[16,128,128]{2,1,0:T(8,128)(2,1)S(1)} %collective-permute-done.16.refs_6_), channel_id=1, source_target_pairs={{0,4},{4,0},{8,12},{12,8},{16,20},{20,16},{24,28},{28,24},{1,5},{5... | collective-permute-start | bytes 1572872 | tf_op jit(solution)/shard_map/ppermute | solution.py:333
  51.7 14.0 %collective-permute-start = (bf16[16,128,128]{2,1,0:T(8,128)(2,1)S(1)}, bf16[16,128,128]{2,1,0:T(8,128)(2,1)S(1)}, u32[]{:S(2)}, u32[]{:S(2)}) collective-permute-start(bf16[16,128,128]{2,1,0:T(8,128)(2,1)S(1)} %shard_map.47.refs_0_), channel_id=1, source_target_pairs={{0,4},{4,0},{8,12},{12,8},{16,20},{20,16},{24,28},{28,24},{1,5},{5... | collective-permute-start | bytes 1572872 | tf_op jit(solution)/shard_map/ppermute | solution.py:333
  51.7 14.0 %collective-permute-start.2 = (bf16[16,128,128]{2,1,0:T(8,128)(2,1)S(1)}, bf16[16,128,128]{2,1,0:T(8,128)(2,1)S(1)}, u32[]{:S(2)}, u32[]{:S(2)}) collective-permute-start(bf16[16,128,128]{2,1,0:T(8,128)(2,1)S(1)} %collective-permute-done.1.refs_2_), channel_id=1, source_target_pairs={{0,4},{4,0},{8,12},{12,8},{16,20},{20,16},{24,28},{28,24},{1,5},{5... | collective-permute-start | bytes 1572872 | tf_op jit(solution)/shard_map/ppermute | solution.py:333
  52.2 13.5 %collective-permute-start.4 = (bf16[16,128,128]{2,1,0:T(8,128)(2,1)S(1)}, bf16[16,128,128]{2,1,0:T(8,128)(2,1)S(1)}, u32[]{:S(2)}, u32[]{:S(2)}) collective-permute-start(bf16[16,128,128]{2,1,0:T(8,128)(2,1)S(1)} %collective-permute-done.3.refs_4_), channel_id=1, source_target_pairs={{0,4},{4,0},{8,12},{12,8},{16,20},{20,16},{24,28},{28,24},{1,5},{5... | collective-permute-start | bytes 1572872 | tf_op jit(solution)/shard_map/ppermute | solution.py:333
  52.3 13.5 %collective-permute-start.6 = (bf16[16,128,128]{2,1,0:T(8,128)(2,1)S(1)}, bf16[16,128,128]{2,1,0:T(8,128)(2,1)S(1)}, u32[]{:S(2)}, u32[]{:S(2)}) collective-permute-start(bf16[16,128,128]{2,1,0:T(8,128)(2,1)S(1)} %collective-permute-done.5.refs_6_), channel_id=1, source_target_pairs={{0,4},{4,0},{8,12},{12,8},{16,20},{20,16},{24,28},{28,24},{1,5},{5... | collective-permute-start | bytes 1572872 | tf_op jit(solution)/shard_map/ppermute | solution.py:333
  52.7 2.8 %copy-start = (bf16[1,1,192,128,128]{4,3,2,1,0:T(8,128)(2,1)S(1)}, bf16[1,1,192,128,128]{4,3,2,1,0:T(8,128)(2,1)}, u32[]{:S(2)}) copy-start(bf16[1,1,192,128,128]{4,3,2,1,0:T(8,128)(2,1)} %param.5) | copy-start | bytes 18874372
  62.9 15.2 %collective-permute-start.18 = (s16[2064,128]{1,0:T(8,128)(2,1)S(1)}, s16[2064,128]{1,0:T(8,128)(2,1)S(1)}, u32[]{:S(2)}, u32[]{:S(2)}) collective-permute-start(s16[2064,128]{1,0:T(8,128)(2,1)S(1)} %get-tuple-element.34), channel_id=1, source_target_pairs={{0,1},{3,2},{4,5},{7,6},{8,9},{11,10},{12,13},{15,14},{16,17},{19,... | collective-permute-start | bytes 1585160 | tf_op jit(solution)/shard_map/ppermute | solution.py:360
  67.3 22.1 %collective-permute-start.7 = (s16[2064,128]{1,0:T(8,128)(2,1)S(1)}, s16[2064,128]{1,0:T(8,128)(2,1)S(1)}, u32[]{:S(2)}, u32[]{:S(2)}) collective-permute-start(s16[2064,128]{1,0:T(8,128)(2,1)S(1)} %get-tuple-element.28), channel_id=1, source_target_pairs={{0,1},{3,2},{4,5},{7,6},{8,9},{11,10},{12,13},{15,14},{16,17},{19,... | collective-permute-start | bytes 1585160 | tf_op jit(solution)/shard_map/ppermute | solution.py:360
  71.3 29.4 %collective-permute-start.20 = (s16[2064,128]{1,0:T(8,128)(2,1)S(1)}, s16[2064,128]{1,0:T(8,128)(2,1)S(1)}, u32[]{:S(2)}, u32[]{:S(2)}) collective-permute-start(s16[2064,128]{1,0:T(8,128)(2,1)S(1)} %get-tuple-element.35), channel_id=1, source_target_pairs={{0,1},{1,2},{2,3},{4,5},{5,6},{6,7},{8,9},{9,10},{10,11},{12,13},{... | collective-permute-start | bytes 1585160 | tf_op jit(solution)/shard_map/ppermute | solution.py:367
  72.7 28.1 %collective-permute-start.21 = (s16[2064,128]{1,0:T(8,128)(2,1)S(1)}, s16[2064,128]{1,0:T(8,128)(2,1)S(1)}, u32[]{:S(2)}, u32[]{:S(2)}) collective-permute-start(s16[2064,128]{1,0:T(8,128)(2,1)S(1)} %get-tuple-element.36), channel_id=1, source_target_pairs={{1,0},{2,1},{3,2},{5,4},{6,5},{7,6},{9,8},{10,9},{11,10},{13,12},{... | collective-permute-start | bytes 1585160 | tf_op jit(solution)/shard_map/ppermute | solution.py:367
  76.6 38.9 %collective-permute-start.10 = (s16[2064,128]{1,0:T(8,128)(2,1)S(1)}, s16[2064,128]{1,0:T(8,128)(2,1)S(1)}, u32[]{:S(2)}, u32[]{:S(2)}) collective-permute-start(s16[2064,128]{1,0:T(8,128)(2,1)S(1)} %get-tuple-element.30), channel_id=1, source_target_pairs={{1,0},{2,1},{3,2},{5,4},{6,5},{7,6},{9,8},{10,9},{11,10},{13,12},{... | collective-permute-start | bytes 1585160 | tf_op jit(solution)/shard_map/ppermute | solution.py:367
  78.6 35.4 %collective-permute-start.19 = (s16[2064,128]{1,0:T(8,128)(2,1)S(1)}, s16[2064,128]{1,0:T(8,128)(2,1)S(1)}, u32[]{:S(2)}, u32[]{:S(2)}) collective-permute-start(s16[2064,128]{1,0:T(8,128)(2,1)S(1)} %shard_map.54), channel_id=1, source_target_pairs={{0,2},{1,3},{2,0},{3,1},{4,6},{5,7},{6,4},{7,5},{8,10},{9,11},{10,... | collective-permute-start | bytes 1585160 | tf_op jit(solution)/shard_map/ppermute | solution.py:365
  89.4 34.0 %collective-permute-start.9 = (s16[2064,128]{1,0:T(8,128)(2,1)S(1)}, s16[2064,128]{1,0:T(8,128)(2,1)S(1)}, u32[]{:S(2)}, u32[]{:S(2)}) collective-permute-start(s16[2064,128]{1,0:T(8,128)(2,1)S(1)} %get-tuple-element.29), channel_id=1, source_target_pairs={{0,1},{1,2},{2,3},{4,5},{5,6},{6,7},{8,9},{9,10},{10,11},{12,13},{... | collective-permute-start | bytes 1585160 | tf_op jit(solution)/shard_map/ppermute | solution.py:367
  100.7 46.7 %collective-permute-start.8 = (s16[2064,128]{1,0:T(8,128)(2,1)S(1)}, s16[2064,128]{1,0:T(8,128)(2,1)S(1)}, u32[]{:S(2)}, u32[]{:S(2)}) collective-permute-start(s16[2064,128]{1,0:T(8,128)(2,1)S(1)} %shard_map.50), channel_id=1, source_target_pairs={{0,2},{1,3},{2,0},{3,1},{4,6},{5,7},{6,4},{7,5},{8,10},{9,11},{10,... | collective-permute-start | bytes 1585160 | tf_op jit(solution)/shard_map/ppermute | solution.py:365
  (2 other events, 1.3 us)

commit v3 on v2

--- a/solution.py
+++ b/solution.py
@@ -11,7 +11,7 @@
 LANES = 128
 UNROLL = 16
 MIB = 1 << 20
-CHUNKS = (8, 8)
+CHUNKS = (4, 6, 6)
 TOP = 32700.0
 STEPS = 8.0
 TINY = 2.0**-110
@@ -336,33 +336,51 @@
 
 def plan(count):
     out = []
-    for d in range(count - 1, 0, -1):
+    for d in range(count - 1, 1, -1):
         right = [(z, z + d) for z in range(count - d)]
         left = [(z, z - d) for z in range(d, count)]
-        out.append((d, right, left, count - 1 - d < d - 1 or (d == 2 and count == 4)))
+        hop = [(a, a + 1 if b > a else a - 1) for a, b in right + left]
+        ends = [b for _, b in (hop if d > 2 else right + left)]
+        if len(set(ends)) == len(ends) and count <= 2 * d:
+            out.append(("both", d, right + left, lambda z, d=d: jnp.where(z + d < count, z + d, z - d)))
+        else:
+            out.append(("right", d, right, lambda z, d=d: z + d))
+            out.append(("left", d, left, lambda z, d=d: z - d))
+    outer = [(z, z ^ 1) for z in range(count) if z ^ 1 < count]
+    middle = [(z, z + 1) for z in range(1, count - 1, 2)]
+    out.append(("outer", 1, outer, lambda z: z ^ 1))
+    if middle:
+        middle += [(b, a) for a, b in middle]
+        out.append(("middle", 1, middle, lambda z: z + 2 * (z & 1) - 1))
     return out
+
+
+def shared(kinds):
+    return kinds[-1][0] == "middle" and not {a for a, _ in kinds[0][2]} & {a for a, _ in kinds[-1][2]}
 
 
 def reduce(kinds, messages, width, owned):
     got = []
     relayed = {}
-    for (d, side, pairs), message in zip(kinds, messages):
-        sides = ("right", "left") if side == "both" else (side,)
+    if shared(kinds):
+        got.append(lax.ppermute(messages[0], "col", kinds[-1][2]))
+    for (name, d, pairs, _), message in zip(kinds, messages):
+        if d == 1:
+            got.append(lax.ppermute(message, "col", pairs))
+            continue
+        sides = ("right", "left") if name == "both" else (name,)
         incoming = []
-        for s in sides:
-            for array in relayed.get((d + 1, s), []):
+        for side in sides:
+            for array in relayed.get((d + 1, side), []):
                 if not any(array is a for a in incoming):
                     incoming.append(array)
+        if incoming:
+            message = merge([message] + incoming, width, owned)
         if d >= 3:
-            if incoming:
-                message = merge([message] + incoming, width, owned)
             hops = [(a, a + 1 if b > a else a - 1) for a, b in pairs]
             array = lax.ppermute(message, "col", hops)
-            for s in sides:
-                relayed.setdefault((d, s), []).append(array)
-        elif incoming:
-            merged = merge([message] + incoming, width, owned)
-            got.append(lax.ppermute(merged, "col", pairs))
+            for side in sides:
+                relayed.setdefault((d, side), []).append(array)
         else:
             got.append(lax.ppermute(message, "col", pairs))
     return got
@@ -377,18 +395,16 @@
     total_width = features.shape[1]
     owned = (pointers.shape[0] - 1) // col_count
 
-    kinds = []
-    for d, right, left, both in plan(col_count):
-        if both:
-            kinds.append((d, "both", right + left))
-        else:
-            kinds.append((d, "right", right))
-            kinds.append((d, "left", left))
+    kinds = plan(col_count)
+    count = len(kinds) - shared(kinds)
 
     def owner_of(col):
-        for d, side, _ in kinds:
-            right = side == "right" if side != "both" else col + d < col_count
-            yield jnp.where(right, col + d, col - d)
+        for n, (_, _, pairs, owner) in enumerate(kinds[:count]):
+            there = owner(col)
+            if n == 0 and shared(kinds):
+                first = sum((col == a).astype(jnp.int32) for a, _ in pairs)
+                there = jnp.where(first > 0, there, kinds[-1][3](col))
+            yield there
         yield col
 
     starts = [total_width * sum(CHUNKS[:n]) // sum(CHUNKS) for n in range(len(CHUNKS) + 1)]
@@ -397,13 +413,13 @@
         piece = turn(features, block, first, last - first)
         parts.append(gather(piece, row_count))
     ranges, index, rows, store = stage(
-        pointers, block_cols[0, 0], values, owner_of, len(kinds) + 1, mine
+        pointers, block_cols[0, 0], values, owner_of, count + 1, mine
     )
     sums, written, out = [], 0, None
     for chunk, pieces in enumerate(parts):
         lead, panel = head(ranges, index, rows, store, pieces, owned)
         *others, own = rest(
-            ranges, index, rows, store, panel, owned, pointers.shape[0] - 1, len(kinds) - 1
+            ranges, index, rows, store, panel, owned, pointers.shape[0] - 1, count - 1
         )
         got = reduce(kinds, [lead, *others], own.shape[1], owned)
         sums.append((own, got))

time: 149 us -> 156 us (1.047)
  starting transfers between devices: 28.3 us -> 35 us
  Pallas kernels: 17.7 us -> 20.3 us
  waiting for transfers between devices: 97.4 us -> 95.5 us
    ppermute x2 -> x3, waiting for transfers between devices: 37.2 us -> 0.01 us  [reduce(): got.append(lax.ppermute(messages[0], 'col', kinds[-1][2]))]
    ppermute x4 -> x6, waiting for transfers between devices: 14.3 us -> 43.6 us  [reduce(): got.append(lax.ppermute(message, 'col', pairs))]
    ppermute x6 -> x9, starting transfers between devices: 9.22 us -> 13.4 us  [gather(): lax.ppermute(part, 'row', [(d, d ^ p) for d in range(devices)])]
    ppermute x6 -> x9, waiting for transfers between devices: 40 us -> 44.1 us  [gather(): lax.ppermute(part, 'row', [(d, d ^ p) for d in range(devices)])]
    ppermute x2 -> x3, starting transfers between devices: 5.08 us -> 2.04 us  [reduce(): got.append(lax.ppermute(messages[0], 'col', kinds[-1][2]))]
    ppermute x4 -> x6, starting transfers between devices: 8.31 us -> 10.9 us  [reduce(): got.append(lax.ppermute(message, 'col', pairs))]
    ppermute x2 -> x3, starting transfers between devices: 4.14 us -> 5.72 us  [reduce(): array = lax.ppermute(message, 'col', hops)]
    pallas_call x2 -> x3, Pallas kernels: 5.34 us -> 6.43 us  [rest(): pl.pallas_call(functools.partial(rest_kernel, owned, messages, local_rows...]
  transfers between devices with their start and end apart: 22 -> 33, of which waited for: 10 -> 13; matrix products, arithmetic and copies ran while one was open for 0% -> 0% of each run, Pallas kernels for 11% -> 12%
where the time goes in v3:
time: 156 us; the launch traced here: 155 us
  waiting for transfers between devices  95.5 us (61%)
  starting transfers between devices  35 us (22%)
  Pallas kernels  20.3 us (13%)
  local copies, waits for them, and re-layouts  4.02 us (3%)
    ppermute x9, waiting for transfers between devices, gather(): lax.ppermute(part, 'row', [(d, d ^ p) for d in range(devices)])  44.1 us
    ppermute x6, waiting for transfers between devices, reduce(): got.append(lax.ppermute(message, 'col', pairs))  43.6 us
    ppermute x9, starting transfers between devices, gather(): lax.ppermute(part, 'row', [(d, d ^ p) for d in range(devices)])  13.4 us
    ppermute x6, starting transfers between devices, reduce(): got.append(lax.ppermute(message, 'col', pairs))  10.9 us
    ppermute x3, waiting for transfers between devices, reduce(): array = lax.ppermute(message, 'col', hops)  6.49 us
    pallas_call x3, Pallas kernels, rest(): pl.pallas_call(functools.partial(rest_kernel, owned, messages, local_rows...  6.43 us
    ppermute x3, starting transfers between devices, reduce(): array = lax.ppermute(message, 'col', hops)  5.72 us
    pallas_call x1, Pallas kernels, stage(): pl.pallas_call(functools.partial(stage_kernel, owner_of, mine), out_shape...  4.45 us
  transfers between devices with their start and end apart: 33, of which 13 were waited for; matrix products, arithmetic and copies ran while one was open for 0% of the time, Pallas kernels for 12%

profile of v3, /device:TPU:0, one launch (start us, length us, event | category | flops | bytes accessed | tf_op | source)
XLA Modules:
  0.0 155.0 jit_solution(3051488095514270601)
XLA Ops:
  2.6 3.0 %collective-permute-start.1 = (bf16[16,96,128]{2,1,0:T(8,128)(2,1)S(1)}, bf16[16,96,128]{2,1,0:T(8,128)(2,1)S(1)}, u32[]{:S(2)}, u32[]{:S(2)}) collective-permute-start(bf16[16,96,128]{2,1,0:T(8,128)(2,1)S(1)} %shard_map.47.refs_0_), channel_id=1, source_target_pairs={{0,8},{4,12},{8,0},{12,4},{16,24},{20,28},{24,16},{28,20},{1,9},{5... | collective-permute-start | bytes 1179656 | tf_op jit(solution)/shard_map/ppermute | solution.py:332
  5.6 2.0 %collective-permute-start.25 = (bf16[16,64,128]{2,1,0:T(8,128)(2,1)S(1)}, bf16[16,64,128]{2,1,0:T(8,128)(2,1)S(1)}, u32[]{:S(2)}, u32[]{:S(2)}) collective-permute-start(bf16[16,64,128]{2,1,0:T(8,128)(2,1)S(1)} %shard_map.55.refs_0_), channel_id=1, source_target_pairs={{0,16},{4,20},{8,24},{12,28},{16,0},{20,4},{24,8},{28,12},{1,17},{... | collective-permute-start | bytes 786440 | tf_op jit(solution)/shard_map/ppermute | solution.py:332
  9.4 11.7 %collective-permute-done.23.refs_2_ = bf16[16,64,128]{2,1,0:T(8,128)(2,1)S(1)} collective-permute-done((bf16[16,64,128]{2,1,0:T(8,128)(2,1)S(1)}, bf16[16,64,128]{2,1,0:T(8,128)(2,1)S(1)}, u32[]{:S(2)}, u32[]{:S(2)}) %collective-permute-start.23) | collective-permute-done | bytes 262176 | tf_op jit(solution)/shard_map/ppermute | solution.py:332
  21.2 2.1 %collective-permute-start.3 = (bf16[16,96,128]{2,1,0:T(8,128)(2,1)S(1)}, bf16[16,96,128]{2,1,0:T(8,128)(2,1)S(1)}, u32[]{:S(2)}, u32[]{:S(2)}) collective-permute-start(bf16[16,96,128]{2,1,0:T(8,128)(2,1)S(1)} %shard_map.47.refs_0_), channel_id=1, source_target_pairs={{0,16},{4,20},{8,24},{12,28},{16,0},{20,4},{24,8},{28,12},{1,17},{... | collective-permute-start | bytes 1179656 | tf_op jit(solution)/shard_map/ppermute | solution.py:332
  24.7 3.7 %collective-permute-done.27.refs_6_ = bf16[16,64,128]{2,1,0:T(8,128)(2,1)S(1)} collective-permute-done((bf16[16,64,128]{2,1,0:T(8,128)(2,1)S(1)}, bf16[16,64,128]{2,1,0:T(8,128)(2,1)S(1)}, u32[]{:S(2)}, u32[]{:S(2)}) %collective-permute-start.27) | collective-permute-done | bytes 262176 | tf_op jit(solution)/shard_map/ppermute | solution.py:332
  31.9 13.4 %collective-permute-done.3.refs_4_ = bf16[16,96,128]{2,1,0:T(8,128)(2,1)S(1)} collective-permute-done((bf16[16,96,128]{2,1,0:T(8,128)(2,1)S(1)}, bf16[16,96,128]{2,1,0:T(8,128)(2,1)S(1)}, u32[]{:S(2)}, u32[]{:S(2)}) %collective-permute-start.3) | collective-permute-done | bytes 393248 | tf_op jit(solution)/shard_map/ppermute | solution.py:332
  45.8 15.3 %collective-permute-done.14.refs_4_ = bf16[16,96,128]{2,1,0:T(8,128)(2,1)S(1)} collective-permute-done((bf16[16,96,128]{2,1,0:T(8,128)(2,1)S(1)}, bf16[16,96,128]{2,1,0:T(8,128)(2,1)S(1)}, u32[]{:S(2)}, u32[]{:S(2)}) %collective-permute-start.14) | collective-permute-done | bytes 393248 | tf_op jit(solution)/shard_map/ppermute | solution.py:332
  64.1 2.8 %copy-done.1 = bf16[1,1,192,128,128]{4,3,2,1,0:T(8,128)(2,1)S(1)} copy-done((bf16[1,1,192,128,128]{4,3,2,1,0:T(8,128)(2,1)S(1)}, bf16[1,1,192,128,128]{4,3,2,1,0:T(8,128)(2,1)}, u32[]{:S(2)}) %copy-start.1) | copy-done | bytes 6291480
  66.8 4.4 %shard_map.46 = (s32[13]{0:T(128)S(1)}, s32[192]{0:T(256)S(1)}, s32[192]{0:T(256)S(1)}, bf16[192,128,128]{2,1,0:T(8,128)(2,1)S(1)}) custom-call(s32[65]{0:T(128)S(1)} %bitcast.5, s32[192]{0:T(256)S(1)} %bitcast.4, bf16[192,128,128]{2,1,0:T(8,128)(2,1)S(1)} %bitcast.3), custom_call_target="tpu_custom_call" | custom-call | flops 67108864 | bytes 4096 | tf_op jit(solution)/shard_map/pallas_call | solution.py:106
  72.7 3.1 %collective-permute-start.8 = (s16[1552,128]{1,0:T(8,128)(2,1)S(1)}, s16[1552,128]{1,0:T(8,128)(2,1)S(1)}, u32[]{:S(2)}, u32[]{:S(2)}) collective-permute-start(s16[1552,128]{1,0:T(8,128)(2,1)S(1)} %get-tuple-element.30), channel_id=1, source_target_pairs={{0,1},{3,2},{4,5},{7,6},{8,9},{11,10},{12,13},{15,14},{16,17},{19,... | collective-permute-start | bytes 1191944 | tf_op jit(solution)/shard_map/ppermute | solution.py:381
  82.6 2.0 %shard_map.57 = (s16[1040,128]{1,0:T(8,128)(2,1)S(1)}, s16[1040,128]{1,0:T(8,128)(2,1)S(1)}, f32[16,64,128]{2,1,0:T(8,128)S(1)}) custom-call(s32[13]{0:T(128)S(1)} %get-tuple-element.24.range_ref, s32[192]{0:T(256)S(1)} %get-tuple-element.25.index_ref, s32[192]{0:T(256)S(1)} %get-tuple-element.26.row_ref, ...), custom_call_target="tpu_custom_call" | custom-call | flops 402653184 | bytes 4194304 | tf_op jit(solution)/shard_map/pallas_call | solution.py:215
  84.6 6.5 %collective-permute-done.30.refs_1_ = s16[1040,128]{1,0:T(8,128)(2,1)S(1)} collective-permute-done((s16[1040,128]{1,0:T(8,128)(2,1)S(1)}, s16[1040,128]{1,0:T(8,128)(2,1)S(1)}, u32[]{:S(2)}, u32[]{:S(2)}) %collective-permute-start.30) | collective-permute-done | bytes 266272 | tf_op jit(solution)/shard_map/ppermute | solution.py:381
  91.1 2.5 %collective-permute-start.32 = (s16[1040,128]{1,0:T(8,128)(2,1)S(1)}, s16[1040,128]{1,0:T(8,128)(2,1)S(1)}, u32[]{:S(2)}, u32[]{:S(2)}) collective-permute-start(s16[1040,128]{1,0:T(8,128)(2,1)S(1)} %get-tuple-element.42), channel_id=1, source_target_pairs={{0,1},{1,0},{2,3},{3,2},{4,5},{5,4},{6,7},{7,6},{8,9},{9,8},{10,11... | collective-permute-start | bytes 798728 | tf_op jit(solution)/shard_map/ppermute | solution.py:369
  95.3 2.2 %shard_map.49 = (s16[1552,128]{1,0:T(8,128)(2,1)S(1)}, s16[1552,128]{1,0:T(8,128)(2,1)S(1)}, f32[16,96,128]{2,1,0:T(8,128)S(1)}) custom-call(s32[13]{0:T(128)S(1)} %get-tuple-element.24.range_ref, s32[192]{0:T(256)S(1)} %get-tuple-element.25.index_ref, s32[192]{0:T(256)S(1)} %get-tuple-element.26.row_ref, ...), custom_call_target="tpu_custom_call" | custom-call | flops 603979776 | bytes 4194304 | tf_op jit(solution)/shard_map/pallas_call | solution.py:215
  97.5 2.2 %shard_map.53 = (s16[1552,128]{1,0:T(8,128)(2,1)S(1)}, s16[1552,128]{1,0:T(8,128)(2,1)S(1)}, f32[16,96,128]{2,1,0:T(8,128)S(1)}) custom-call(s32[13]{0:T(128)S(1)} %get-tuple-element.24.range_ref, s32[192]{0:T(256)S(1)} %get-tuple-element.25.index_ref, s32[192]{0:T(256)S(1)} %get-tuple-element.26.row_ref, ...), custom_call_target="tpu_custom_call" | custom-call | flops 603979776 | bytes 4194304 | tf_op jit(solution)/shard_map/pallas_call | solution.py:215
  100.1 2.1 %collective-permute-start.10 = (s16[1552,128]{1,0:T(8,128)(2,1)S(1)}, s16[1552,128]{1,0:T(8,128)(2,1)S(1)}, u32[]{:S(2)}, u32[]{:S(2)}) collective-permute-start(s16[1552,128]{1,0:T(8,128)(2,1)S(1)} %get-tuple-element.32), channel_id=1, source_target_pairs={{0,1},{1,0},{2,3},{3,2},{4,5},{5,4},{6,7},{7,6},{8,9},{9,8},{10,11... | collective-permute-start | bytes 1191944 | tf_op jit(solution)/shard_map/ppermute | solution.py:369
  103.8 4.4 %collective-permute-done.32.refs_3_ = s16[1040,128]{1,0:T(8,128)(2,1)S(1)} collective-permute-done((s16[1040,128]{1,0:T(8,128)(2,1)S(1)}, s16[1040,128]{1,0:T(8,128)(2,1)S(1)}, u32[]{:S(2)}, u32[]{:S(2)}) %collective-permute-start.32) | collective-permute-done | bytes 266272 | tf_op jit(solution)/shard_map/ppermute | solution.py:369
  108.9 2.2 %collective-permute-done.31.refs_2_ = s16[1040,128]{1,0:T(8,128)(2,1)S(1)} collective-permute-done((s16[1040,128]{1,0:T(8,128)(2,1)S(1)}, s16[1040,128]{1,0:T(8,128)(2,1)S(1)}, u32[]{:S(2)}, u32[]{:S(2)}) %collective-permute-start.31) | collective-permute-done | bytes 266272 | tf_op jit(solution)/shard_map/ppermute | solution.py:385
  111.1 3.8 %collective-permute-start.21 = (s16[1552,128]{1,0:T(8,128)(2,1)S(1)}, s16[1552,128]{1,0:T(8,128)(2,1)S(1)}, u32[]{:S(2)}, u32[]{:S(2)}) collective-permute-start(s16[1552,128]{1,0:T(8,128)(2,1)S(1)} %get-tuple-element.37), channel_id=1, source_target_pairs={{0,1},{1,0},{2,3},{3,2},{4,5},{5,4},{6,7},{7,6},{8,9},{9,8},{10,11... | collective-permute-start | bytes 1191944 | tf_op jit(solution)/shard_map/ppermute | solution.py:369
  114.9 7.6 %collective-permute-done.10.refs_7_.refs_3_ = s16[1552,128]{1,0:T(8,128)(2,1)S(1)} collective-permute-done((s16[1552,128]{1,0:T(8,128)(2,1)S(1)}, s16[1552,128]{1,0:T(8,128)(2,1)S(1)}, u32[]{:S(2)}, u32[]{:S(2)}) %collective-permute-start.10) | collective-permute-done | bytes 397344 | tf_op jit(solution)/shard_map/ppermute | solution.py:369
  122.5 5.7 %collective-permute-done.9.refs_6_.refs_2_ = s16[1552,128]{1,0:T(8,128)(2,1)S(1)} collective-permute-done((s16[1552,128]{1,0:T(8,128)(2,1)S(1)}, s16[1552,128]{1,0:T(8,128)(2,1)S(1)}, u32[]{:S(2)}, u32[]{:S(2)}) %collective-permute-start.9) | collective-permute-done | bytes 397344 | tf_op jit(solution)/shard_map/ppermute | solution.py:385
  129.7 6.9 %collective-permute-done.21.refs_7_ = s16[1552,128]{1,0:T(8,128)(2,1)S(1)} collective-permute-done((s16[1552,128]{1,0:T(8,128)(2,1)S(1)}, s16[1552,128]{1,0:T(8,128)(2,1)S(1)}, u32[]{:S(2)}, u32[]{:S(2)}) %collective-permute-start.21) | collective-permute-done | bytes 397344 | tf_op jit(solution)/shard_map/ppermute | solution.py:369
  136.7 16.8 %collective-permute-done.20.refs_6_ = s16[1552,128]{1,0:T(8,128)(2,1)S(1)} collective-permute-done((s16[1552,128]{1,0:T(8,128)(2,1)S(1)}, s16[1552,128]{1,0:T(8,128)(2,1)S(1)}, u32[]{:S(2)}, u32[]{:S(2)}) %collective-permute-start.20) | collective-permute-done | bytes 397344 | tf_op jit(solution)/shard_map/ppermute | solution.py:385
  153.4 1.6 %shard_map.60 = bf16[2048,256]{1,0:T(8,128)(2,1)} custom-call(f32[16,96,128]{2,1,0:T(8,128)S(1)} %get-tuple-element.29.refs_4_.refs_0_, s16[1552,128]{1,0:T(8,128)(2,1)S(1)} %collective-permute-done.7.refs_5_.refs_1_, s16[1552,128]{1,0:T(8,128)(2,1)S(1)} %collective-permute-done.9.refs_6_.refs_2_, ...), custom_call_target="tpu_custom_call", output_to_operand_aliasing={{}: (8, {})} | custom-call | flops 268435456 | bytes 4194304 | tf_op jit(solution)/shard_map/pallas_call | solution.py:313
  (65 shorter events, 26.9 us)
Async XLA Ops:
  2.5 27.3 %collective-permute-start = (bf16[16,96,128]{2,1,0:T(8,128)(2,1)S(1)}, bf16[16,96,128]{2,1,0:T(8,128)(2,1)S(1)}, u32[]{:S(2)}, u32[]{:S(2)}) collective-permute-start(bf16[16,96,128]{2,1,0:T(8,128)(2,1)S(1)} %shard_map.47.refs_0_), channel_id=1, source_target_pairs={{0,4},{4,0},{8,12},{12,8},{16,20},{20,16},{24,28},{28,24},{1,5},{5... | collective-permute-start | bytes 1179656 | tf_op jit(solution)/shard_map/ppermute | solution.py:333
  2.6 27.8 %collective-permute-start.1 = (bf16[16,96,128]{2,1,0:T(8,128)(2,1)S(1)}, bf16[16,96,128]{2,1,0:T(8,128)(2,1)S(1)}, u32[]{:S(2)}, u32[]{:S(2)}) collective-permute-start(bf16[16,96,128]{2,1,0:T(8,128)(2,1)S(1)} %shard_map.47.refs_0_), channel_id=1, source_target_pairs={{0,8},{4,12},{8,0},{12,4},{16,24},{20,28},{24,16},{28,20},{1,9},{5... | collective-permute-start | bytes 1179656 | tf_op jit(solution)/shard_map/ppermute | solution.py:332
  5.6 15.6 %collective-permute-start.23 = (bf16[16,64,128]{2,1,0:T(8,128)(2,1)S(1)}, bf16[16,64,128]{2,1,0:T(8,128)(2,1)S(1)}, u32[]{:S(2)}, u32[]{:S(2)}) collective-permute-start(bf16[16,64,128]{2,1,0:T(8,128)(2,1)S(1)} %shard_map.55.refs_0_), channel_id=1, source_target_pairs={{0,8},{4,12},{8,0},{12,4},{16,24},{20,28},{24,16},{28,20},{1,9},{5... | collective-permute-start | bytes 786440 | tf_op jit(solution)/shard_map/ppermute | solution.py:332
  5.6 17.6 %collective-permute-start.25 = (bf16[16,64,128]{2,1,0:T(8,128)(2,1)S(1)}, bf16[16,64,128]{2,1,0:T(8,128)(2,1)S(1)}, u32[]{:S(2)}, u32[]{:S(2)}) collective-permute-start(bf16[16,64,128]{2,1,0:T(8,128)(2,1)S(1)} %shard_map.55.refs_0_), channel_id=1, source_target_pairs={{0,16},{4,20},{8,24},{12,28},{16,0},{20,4},{24,8},{28,12},{1,17},{... | collective-permute-start | bytes 786440 | tf_op jit(solution)/shard_map/ppermute | solution.py:332
  7.7 20.7 %collective-permute-start.27 = (bf16[16,64,128]{2,1,0:T(8,128)(2,1)S(1)}, bf16[16,64,128]{2,1,0:T(8,128)(2,1)S(1)}, u32[]{:S(2)}, u32[]{:S(2)}) collective-permute-start(bf16[16,64,128]{2,1,0:T(8,128)(2,1)S(1)} %shard_map.55.refs_0_), channel_id=1, source_target_pairs={{0,24},{4,28},{8,16},{12,20},{16,8},{20,12},{24,0},{28,4},{1,25},{... | collective-permute-start | bytes 786440 | tf_op jit(solution)/shard_map/ppermute | solution.py:332
  21.2 24.1 %collective-permute-start.3 = (bf16[16,96,128]{2,1,0:T(8,128)(2,1)S(1)}, bf16[16,96,128]{2,1,0:T(8,128)(2,1)S(1)}, u32[]{:S(2)}, u32[]{:S(2)}) collective-permute-start(bf16[16,96,128]{2,1,0:T(8,128)(2,1)S(1)} %shard_map.47.refs_0_), channel_id=1, source_target_pairs={{0,16},{4,20},{8,24},{12,28},{16,0},{20,4},{24,8},{28,12},{1,17},{... | collective-permute-start | bytes 1179656 | tf_op jit(solution)/shard_map/ppermute | solution.py:332
  23.2 22.0 %collective-permute-start.5 = (bf16[16,96,128]{2,1,0:T(8,128)(2,1)S(1)}, bf16[16,96,128]{2,1,0:T(8,128)(2,1)S(1)}, u32[]{:S(2)}, u32[]{:S(2)}) collective-permute-start(bf16[16,96,128]{2,1,0:T(8,128)(2,1)S(1)} %shard_map.47.refs_0_), channel_id=1, source_target_pairs={{0,24},{4,28},{8,16},{12,20},{16,8},{20,12},{24,0},{28,4},{1,25},{... | collective-permute-start | bytes 1179656 | tf_op jit(solution)/shard_map/ppermute | solution.py:332
  28.4 17.4 %collective-permute-start.12 = (bf16[16,96,128]{2,1,0:T(8,128)(2,1)S(1)}, bf16[16,96,128]{2,1,0:T(8,128)(2,1)S(1)}, u32[]{:S(2)}, u32[]{:S(2)}) collective-permute-start(bf16[16,96,128]{2,1,0:T(8,128)(2,1)S(1)} %shard_map.51.refs_0_), channel_id=1, source_target_pairs={{0,8},{4,12},{8,0},{12,4},{16,24},{20,28},{24,16},{28,20},{1,9},{5... | collective-permute-start | bytes 1179656 | tf_op jit(solution)/shard_map/ppermute | solution.py:332
  29.9 31.2 %collective-permute-start.14 = (bf16[16,96,128]{2,1,0:T(8,128)(2,1)S(1)}, bf16[16,96,128]{2,1,0:T(8,128)(2,1)S(1)}, u32[]{:S(2)}, u32[]{:S(2)}) collective-permute-start(bf16[16,96,128]{2,1,0:T(8,128)(2,1)S(1)} %shard_map.51.refs_0_), channel_id=1, source_target_pairs={{0,16},{4,20},{8,24},{12,28},{16,0},{20,4},{24,8},{28,12},{1,17},{... | collective-permute-start | bytes 1179656 | tf_op jit(solution)/shard_map/ppermute | solution.py:332
  30.4 30.7 %collective-permute-start.16 = (bf16[16,96,128]{2,1,0:T(8,128)(2,1)S(1)}, bf16[16,96,128]{2,1,0:T(8,128)(2,1)S(1)}, u32[]{:S(2)}, u32[]{:S(2)}) collective-permute-start(bf16[16,96,128]{2,1,0:T(8,128)(2,1)S(1)} %shard_map.51.refs_0_), channel_id=1, source_target_pairs={{0,24},{4,28},{8,16},{12,20},{16,8},{20,12},{24,0},{28,4},{1,25},{... | collective-permute-start | bytes 1179656 | tf_op jit(solution)/shard_map/ppermute | solution.py:332
  45.2 17.9 %collective-permute-start.2 = (bf16[16,96,128]{2,1,0:T(8,128)(2,1)S(1)}, bf16[16,96,128]{2,1,0:T(8,128)(2,1)S(1)}, u32[]{:S(2)}, u32[]{:S(2)}) collective-permute-start(bf16[16,96,128]{2,1,0:T(8,128)(2,1)S(1)} %collective-permute-done.1.refs_2_), channel_id=1, source_target_pairs={{0,4},{4,0},{8,12},{12,8},{16,20},{20,16},{24,28},{28,24},{1,5},{5... | collective-permute-start | bytes 1179656 | tf_op jit(solution)/shard_map/ppermute | solution.py:333
  45.2 18.3 %collective-permute-start.4 = (bf16[16,96,128]{2,1,0:T(8,128)(2,1)S(1)}, bf16[16,96,128]{2,1,0:T(8,128)(2,1)S(1)}, u32[]{:S(2)}, u32[]{:S(2)}) collective-permute-start(bf16[16,96,128]{2,1,0:T(8,128)(2,1)S(1)} %collective-permute-done.3.refs_4_), channel_id=1, source_target_pairs={{0,4},{4,0},{8,12},{12,8},{16,20},{20,16},{24,28},{28,24},{1,5},{5... | collective-permute-start | bytes 1179656 | tf_op jit(solution)/shard_map/ppermute | solution.py:333
  45.8 17.9 %collective-permute-start.6 = (bf16[16,96,128]{2,1,0:T(8,128)(2,1)S(1)}, bf16[16,96,128]{2,1,0:T(8,128)(2,1)S(1)}, u32[]{:S(2)}, u32[]{:S(2)}) collective-permute-start(bf16[16,96,128]{2,1,0:T(8,128)(2,1)S(1)} %collective-permute-done.5.refs_6_), channel_id=1, source_target_pairs={{0,4},{4,0},{8,12},{12,8},{16,20},{20,16},{24,28},{28,24},{1,5},{5... | collective-permute-start | bytes 1179656 | tf_op jit(solution)/shard_map/ppermute | solution.py:333
  72.7 21.2 %collective-permute-start.8 = (s16[1552,128]{1,0:T(8,128)(2,1)S(1)}, s16[1552,128]{1,0:T(8,128)(2,1)S(1)}, u32[]{:S(2)}, u32[]{:S(2)}) collective-permute-start(s16[1552,128]{1,0:T(8,128)(2,1)S(1)} %get-tuple-element.30), channel_id=1, source_target_pairs={{0,1},{3,2},{4,5},{7,6},{8,9},{11,10},{12,13},{15,14},{16,17},{19,... | collective-permute-start | bytes 1191944 | tf_op jit(solution)/shard_map/ppermute | solution.py:381
  79.9 22.3 %collective-permute-start.19 = (s16[1552,128]{1,0:T(8,128)(2,1)S(1)}, s16[1552,128]{1,0:T(8,128)(2,1)S(1)}, u32[]{:S(2)}, u32[]{:S(2)}) collective-permute-start(s16[1552,128]{1,0:T(8,128)(2,1)S(1)} %get-tuple-element.35), channel_id=1, source_target_pairs={{0,1},{3,2},{4,5},{7,6},{8,9},{11,10},{12,13},{15,14},{16,17},{19,... | collective-permute-start | bytes 1191944 | tf_op jit(solution)/shard_map/ppermute | solution.py:381
  81.2 33.6 %collective-permute-start.7 = (s16[1552,128]{1,0:T(8,128)(2,1)S(1)}, s16[1552,128]{1,0:T(8,128)(2,1)S(1)}, u32[]{:S(2)}, u32[]{:S(2)}) collective-permute-start(s16[1552,128]{1,0:T(8,128)(2,1)S(1)} %get-tuple-element.30), channel_id=1, source_target_pairs={{1,2},{2,1},{5,6},{6,5},{9,10},{10,9},{13,14},{14,13},{17,18},{18,... | collective-permute-start | bytes 1191944 | tf_op jit(solution)/shard_map/ppermute | solution.py:366
  81.9 18.2 %collective-permute-start.29 = (s16[1040,128]{1,0:T(8,128)(2,1)S(1)}, s16[1040,128]{1,0:T(8,128)(2,1)S(1)}, u32[]{:S(2)}, u32[]{:S(2)}) collective-permute-start(s16[1040,128]{1,0:T(8,128)(2,1)S(1)} %get-tuple-element.40), channel_id=1, source_target_pairs={{1,2},{2,1},{5,6},{6,5},{9,10},{10,9},{13,14},{14,13},{17,18},{18,... | collective-permute-start | bytes 798728 | tf_op jit(solution)/shard_map/ppermute | solution.py:366
  91.1 17.1 %collective-permute-start.32 = (s16[1040,128]{1,0:T(8,128)(2,1)S(1)}, s16[1040,128]{1,0:T(8,128)(2,1)S(1)}, u32[]{:S(2)}, u32[]{:S(2)}) collective-permute-start(s16[1040,128]{1,0:T(8,128)(2,1)S(1)} %get-tuple-element.42), channel_id=1, source_target_pairs={{0,1},{1,0},{2,3},{3,2},{4,5},{5,4},{6,7},{7,6},{8,9},{9,8},{10,11... | collective-permute-start | bytes 798728 | tf_op jit(solution)/shard_map/ppermute | solution.py:369
  93.9 17.2 %collective-permute-start.31 = (s16[1040,128]{1,0:T(8,128)(2,1)S(1)}, s16[1040,128]{1,0:T(8,128)(2,1)S(1)}, u32[]{:S(2)}, u32[]{:S(2)}) collective-permute-start(s16[1040,128]{1,0:T(8,128)(2,1)S(1)} %shard_map.58), channel_id=1, source_target_pairs={{0,2},{1,3},{2,0},{3,1},{4,6},{5,7},{6,4},{7,5},{8,10},{9,11},{10,... | collective-permute-start | bytes 798728 | tf_op jit(solution)/shard_map/ppermute | solution.py:385
  100.1 22.3 %collective-permute-start.10 = (s16[1552,128]{1,0:T(8,128)(2,1)S(1)}, s16[1552,128]{1,0:T(8,128)(2,1)S(1)}, u32[]{:S(2)}, u32[]{:S(2)}) collective-permute-start(s16[1552,128]{1,0:T(8,128)(2,1)S(1)} %get-tuple-element.32), channel_id=1, source_target_pairs={{0,1},{1,0},{2,3},{3,2},{4,5},{5,4},{6,7},{7,6},{8,9},{9,8},{10,11... | collective-permute-start | bytes 1191944 | tf_op jit(solution)/shard_map/ppermute | solution.py:369
  102.2 25.9 %collective-permute-start.9 = (s16[1552,128]{1,0:T(8,128)(2,1)S(1)}, s16[1552,128]{1,0:T(8,128)(2,1)S(1)}, u32[]{:S(2)}, u32[]{:S(2)}) collective-permute-start(s16[1552,128]{1,0:T(8,128)(2,1)S(1)} %shard_map.50), channel_id=1, source_target_pairs={{0,2},{1,3},{2,0},{3,1},{4,6},{5,7},{6,4},{7,5},{8,10},{9,11},{10,... | collective-permute-start | bytes 1191944 | tf_op jit(solution)/shard_map/ppermute | solution.py:385
  108.2 21.5 %collective-permute-start.18 = (s16[1552,128]{1,0:T(8,128)(2,1)S(1)}, s16[1552,128]{1,0:T(8,128)(2,1)S(1)}, u32[]{:S(2)}, u32[]{:S(2)}) collective-permute-start(s16[1552,128]{1,0:T(8,128)(2,1)S(1)} %get-tuple-element.35), channel_id=1, source_target_pairs={{1,2},{2,1},{5,6},{6,5},{9,10},{10,9},{13,14},{14,13},{17,18},{18,... | collective-permute-start | bytes 1191944 | tf_op jit(solution)/shard_map/ppermute | solution.py:366
  111.1 25.6 %collective-permute-start.21 = (s16[1552,128]{1,0:T(8,128)(2,1)S(1)}, s16[1552,128]{1,0:T(8,128)(2,1)S(1)}, u32[]{:S(2)}, u32[]{:S(2)}) collective-permute-start(s16[1552,128]{1,0:T(8,128)(2,1)S(1)} %get-tuple-element.37), channel_id=1, source_target_pairs={{0,1},{1,0},{2,3},{3,2},{4,5},{5,4},{6,7},{7,6},{8,9},{9,8},{10,11... | collective-permute-start | bytes 1191944 | tf_op jit(solution)/shard_map/ppermute | solution.py:369
  114.9 38.6 %collective-permute-start.20 = (s16[1552,128]{1,0:T(8,128)(2,1)S(1)}, s16[1552,128]{1,0:T(8,128)(2,1)S(1)}, u32[]{:S(2)}, u32[]{:S(2)}) collective-permute-start(s16[1552,128]{1,0:T(8,128)(2,1)S(1)} %shard_map.54), channel_id=1, source_target_pairs={{0,2},{1,3},{2,0},{3,1},{4,6},{5,7},{6,4},{7,5},{8,10},{9,11},{10,... | collective-permute-start | bytes 1191944 | tf_op jit(solution)/shard_map/ppermute | solution.py:385
  (13 other events, 222.4 us)

commit v4 on v3

--- a/solution.py
+++ b/solution.py
@@ -11,7 +11,9 @@
 LANES = 128
 UNROLL = 16
 MIB = 1 << 20
-CHUNKS = (4, 6, 6)
+STAGE_MIB = 46
+DIRECT_CHUNKS = 1
+CHUNKS = (3, 5, 8)
 TOP = 32700.0
 STEPS = 8.0
 TINY = 2.0**-110
@@ -64,19 +66,29 @@
 
 
 def stage_kernel(
-    owner_of, mine, pointer_ref, column_ref, values_ref, range_ref, index_ref, row_ref, store_ref
+    owner_of, mine, pointer_ref, column_ref, values_ref, range_ref, index_ref, row_ref, store_ref, sem
 ):
     local_rows = pointer_ref.shape[0] - 1
     slots = column_ref.shape[0]
     row, col = lax.axis_index("row"), lax.axis_index("col")
     group = mine * lax.axis_size("row")
-
-    @pl.loop(0, slots, unroll=4)
-    def _(s):
-        column = column_ref[s] - col * group
-        device = lax.div(column, mine)
-        index_ref[s] = (device ^ row) * mine + column - device * mine
-        row_ref[s] = local_rows
+    total = pointer_ref[local_rows]
+    steps = (total + UNROLL - 1) // UNROLL
+
+    def copy(t):
+        span = pl.ds(t * UNROLL, UNROLL)
+        return pltpu.make_async_copy(values_ref.at[span], store_ref.at[span], sem.at[t])
+
+    @pl.loop(0, steps)
+    def _(t):
+        copy(t).start()
+
+    @pl.loop(0, jnp.minimum(slots // UNROLL, steps + 1))
+    def _(t):
+        for u in range(UNROLL):
+            column = column_ref[t * UNROLL + u] - col * group
+            device = lax.div(column, mine)
+            index_ref[t * UNROLL + u] = (device ^ row) * mine + column - device * mine
 
     @pl.loop(0, local_rows)
     def _(i):
@@ -91,18 +103,17 @@
         range_ref[3 * m] = jnp.where(sent, pointer_ref[first], 0)
         range_ref[3 * m + 1] = jnp.where(sent, pointer_ref[first + owned], 0)
         range_ref[3 * m + 2] = first
-    range_ref[3 * m + 3] = pointer_ref[local_rows]
-
-    @pl.loop(0, (pointer_ref[local_rows] + 3) // 4)
+    range_ref[3 * m + 3] = total
+
+    @pl.loop(0, steps)
     def _(t):
-        for u in range(4):
-            store_ref[4 * t + u] = values_ref[4 * t + u].T
+        copy(t).wait()
 
 
 def stage(pointers, columns, values, owner_of, count, mine):
     smem = pl.BlockSpec(memory_space=pltpu.SMEM)
     whole = pl.BlockSpec(memory_space=pltpu.VMEM)
-    slots = columns.shape[0]
+    slots = values.shape[0]
     return pl.pallas_call(
         functools.partial(stage_kernel, owner_of, mine),
         out_shape=[
@@ -111,10 +122,11 @@
             jax.ShapeDtypeStruct((slots,), jnp.int32),
             jax.ShapeDtypeStruct(values.shape, values.dtype),
         ],
-        in_specs=[smem, smem, whole],
+        in_specs=[smem, smem, pl.BlockSpec(memory_space=pltpu.HBM)],
         out_specs=[smem] * 3 + [whole],
-        compiler_params=params(4),
-        cost_estimate=pl.CostEstimate(flops=1 << 26, bytes_accessed=1 << 12, transcendentals=0),
+        scratch_shapes=[pltpu.SemaphoreType.DMA((-(-slots // UNROLL),))],
+        compiler_params=params(STAGE_MIB),
+        cost_estimate=pl.CostEstimate(flops=1 << 26, bytes_accessed=1 << 22, transcendentals=0),
     )(pointers, columns, values)
 
 
@@ -125,7 +137,12 @@
         for u in range(UNROLL):
             s = low + t * UNROLL + u
             terms.append(
-                jnp.dot(panel[index_ref[s]], store[s], preferred_element_type=jnp.float32)
+                lax.dot_general(
+                    panel[index_ref[s]],
+                    store[s],
+                    (((1,), (1,)), ((), ())),
+                    preferred_element_type=jnp.float32,
+                )
             )
         for u in range(UNROLL):
             s = low + t * UNROLL + u
@@ -359,9 +376,15 @@
     return kinds[-1][0] == "middle" and not {a for a, _ in kinds[0][2]} & {a for a, _ in kinds[-1][2]}
 
 
-def reduce(kinds, messages, width, owned):
+def reduce(kinds, messages, width, owned, chunk):
     got = []
     relayed = {}
+    if chunk < DIRECT_CHUNKS:
+        for n, ((_, d, pairs, _), message) in enumerate(zip(kinds, messages)):
+            if n == 0 and shared(kinds):
+                pairs = pairs + kinds[-1][2]
+            got.append(lax.ppermute(message, "col", pairs))
+        return got
     if shared(kinds):
         got.append(lax.ppermute(messages[0], "col", kinds[-1][2]))
     for (name, d, pairs, _), message in zip(kinds, messages):
@@ -421,7 +444,7 @@
         *others, own = rest(
             ranges, index, rows, store, panel, owned, pointers.shape[0] - 1, count - 1
         )
-        got = reduce(kinds, [lead, *others], own.shape[1], owned)
+        got = reduce(kinds, [lead, *others], own.shape[1], owned, chunk)
         sums.append((own, got))
         while written + LANES <= starts[chunk + 1]:
             taken = [

time: 156 us -> 149 us (0.955)
  waiting for transfers between devices: 95.5 us -> 87.7 us
  starting transfers between devices: 35 us -> 38.9 us
  local copies, waits for them, and re-layouts: 4.02 us -> 1.23 us
    ppermute x9, waiting for transfers between devices: 44.1 us -> 33.3 us  [gather(): lax.ppermute(part, 'row', [(d, d ^ p) for d in range(devices)])]
    ppermute x6 -> x7, waiting for transfers between devices: 43.6 us -> 53.2 us  [reduce(): got.append(lax.ppermute(message, 'col', pairs))]
    ppermute x3 -> x2, waiting for transfers between devices: 6.49 us -> 1.14 us  [reduce(): array = lax.ppermute(message, 'col', hops)]
    ppermute x9, starting transfers between devices: 13.4 us -> 17 us  [gather(): lax.ppermute(part, 'row', [(d, d ^ p) for d in range(devices)])]
    unnamed x8 -> x6, local copies, waits for them, and re-layouts: 4.02 us -> 1.23 us
    ppermute x6 -> x7, starting transfers between devices: 10.9 us -> 12.8 us  [reduce(): got.append(lax.ppermute(message, 'col', pairs))]
    pallas_call x3, Pallas kernels: 6.43 us -> 8.22 us  [rest(): pl.pallas_call(functools.partial(rest_kernel, owned, messages, local_rows...]
    pallas_call x1, Pallas kernels: 4.45 us -> 2.82 us  [stage(): pl.pallas_call(functools.partial(stage_kernel, owner_of, mine), out_shape...]
  transfers between devices with their start and end apart: 33 -> 32, of which waited for: 13 -> 10; matrix products, arithmetic and copies ran while one was open for 0% -> 0% of each run, Pallas kernels for 12% -> 13%
where the time goes in v4:
time: 149 us
  waiting for transfers between devices  87.7 us (59%)
  starting transfers between devices  38.9 us (26%)
  Pallas kernels  20.7 us (14%)
    ppermute x7, waiting for transfers between devices, reduce(): got.append(lax.ppermute(message, 'col', pairs))  53.2 us
    ppermute x9, waiting for transfers between devices, gather(): lax.ppermute(part, 'row', [(d, d ^ p) for d in range(devices)])  33.3 us
    ppermute x9, starting transfers between devices, gather(): lax.ppermute(part, 'row', [(d, d ^ p) for d in range(devices)])  17 us
    ppermute x7, starting transfers between devices, reduce(): got.append(lax.ppermute(message, 'col', pairs))  12.8 us
    pallas_call x3, Pallas kernels, rest(): pl.pallas_call(functools.partial(rest_kernel, owned, messages, local_rows...  8.22 us
    ppermute x2, starting transfers between devices, reduce(): array = lax.ppermute(message, 'col', hops)  5 us
    pallas_call x3, Pallas kernels, head(): pl.pallas_call(functools.partial(head_kernel, owned), out_shape=[jax.Shap...  4.71 us
    pallas_call x2, Pallas kernels, finish(): pl.pallas_call(functools.partial(finish_kernel, owned, sizes), out_shape=...  3.14 us
  transfers between devices with their start and end apart: 32, of which 10 were waited for; matrix products, arithmetic and copies ran while one was open for 0% of the time, Pallas kernels for 13%

profile of v4, /device:TPU:0, one launch (start us, length us, event | category | flops | bytes accessed | tf_op | source)
XLA Modules:
  0.0 148.8 jit_solution(11062552577884549072)
XLA Ops:
  1.5 3.0 %collective-permute-start.12 = (bf16[16,48,128]{2,1,0:T(8,128)(2,1)S(1)}, bf16[16,48,128]{2,1,0:T(8,128)(2,1)S(1)}, u32[]{:S(2)}, u32[]{:S(2)}) collective-permute-start(bf16[16,48,128]{2,1,0:T(8,128)(2,1)S(1)} %shard_map.51.refs_0_), channel_id=1, source_target_pairs={{0,8},{4,12},{8,0},{12,4},{16,24},{20,28},{24,16},{28,20},{1,9},{5... | collective-permute-start | bytes 589832 | tf_op jit(solution)/shard_map/ppermute | solution.py:349
  5.0 2.0 %collective-permute-start.3 = (bf16[16,128,128]{2,1,0:T(8,128)(2,1)S(1)}, bf16[16,128,128]{2,1,0:T(8,128)(2,1)S(1)}, u32[]{:S(2)}, u32[]{:S(2)}) collective-permute-start(bf16[16,128,128]{2,1,0:T(8,128)(2,1)S(1)} %shard_map.47.refs_0_), channel_id=1, source_target_pairs={{0,16},{4,20},{8,24},{12,28},{16,0},{20,4},{24,8},{28,12},{1,17},{... | collective-permute-start | bytes 1572872 | tf_op jit(solution)/shard_map/ppermute | solution.py:349
  10.4 2.0 %collective-permute-start.22 = (bf16[16,80,128]{2,1,0:T(8,128)(2,1)S(1)}, bf16[16,80,128]{2,1,0:T(8,128)(2,1)S(1)}, u32[]{:S(2)}, u32[]{:S(2)}) collective-permute-start(bf16[16,80,128]{2,1,0:T(8,128)(2,1)S(1)} %shard_map.54.refs_0_), channel_id=1, source_target_pairs={{0,8},{4,12},{8,0},{12,4},{16,24},{20,28},{24,16},{28,20},{1,9},{5... | collective-permute-start | bytes 983048 | tf_op jit(solution)/shard_map/ppermute | solution.py:349
  12.3 21.1 %collective-permute-done.14.refs_4_ = bf16[16,48,128]{2,1,0:T(8,128)(2,1)S(1)} collective-permute-done((bf16[16,48,128]{2,1,0:T(8,128)(2,1)S(1)}, bf16[16,48,128]{2,1,0:T(8,128)(2,1)S(1)}, u32[]{:S(2)}, u32[]{:S(2)}) %collective-permute-start.14) | collective-permute-done | bytes 196640 | tf_op jit(solution)/shard_map/ppermute | solution.py:349
  33.5 2.1 %collective-permute-start.24 = (bf16[16,80,128]{2,1,0:T(8,128)(2,1)S(1)}, bf16[16,80,128]{2,1,0:T(8,128)(2,1)S(1)}, u32[]{:S(2)}, u32[]{:S(2)}) collective-permute-start(bf16[16,80,128]{2,1,0:T(8,128)(2,1)S(1)} %shard_map.54.refs_0_), channel_id=1, source_target_pairs={{0,16},{4,20},{8,24},{12,28},{16,0},{20,4},{24,8},{28,12},{1,17},{... | collective-permute-start | bytes 983048 | tf_op jit(solution)/shard_map/ppermute | solution.py:349
  35.6 3.4 %collective-permute-done.22.refs_2_ = bf16[16,80,128]{2,1,0:T(8,128)(2,1)S(1)} collective-permute-done((bf16[16,80,128]{2,1,0:T(8,128)(2,1)S(1)}, bf16[16,80,128]{2,1,0:T(8,128)(2,1)S(1)}, u32[]{:S(2)}, u32[]{:S(2)}) %collective-permute-start.22) | collective-permute-done | bytes 327712 | tf_op jit(solution)/shard_map/ppermute | solution.py:349
  41.5 2.1 %collective-permute-start.26 = (bf16[16,80,128]{2,1,0:T(8,128)(2,1)S(1)}, bf16[16,80,128]{2,1,0:T(8,128)(2,1)S(1)}, u32[]{:S(2)}, u32[]{:S(2)}) collective-permute-start(bf16[16,80,128]{2,1,0:T(8,128)(2,1)S(1)} %shard_map.54.refs_0_), channel_id=1, source_target_pairs={{0,24},{4,28},{8,16},{12,20},{16,8},{20,12},{24,0},{28,4},{1,25},{... | collective-permute-start | bytes 983048 | tf_op jit(solution)/shard_map/ppermute | solution.py:349
  43.6 7.1 %collective-permute-done.26.refs_6_ = bf16[16,80,128]{2,1,0:T(8,128)(2,1)S(1)} collective-permute-done((bf16[16,80,128]{2,1,0:T(8,128)(2,1)S(1)}, bf16[16,80,128]{2,1,0:T(8,128)(2,1)S(1)}, u32[]{:S(2)}, u32[]{:S(2)}) %collective-permute-start.26) | collective-permute-done | bytes 327712 | tf_op jit(solution)/shard_map/ppermute | solution.py:349
  50.7 2.6 %collective-permute-start.16 = (bf16[16,48,128]{2,1,0:T(8,128)(2,1)S(1)}, bf16[16,48,128]{2,1,0:T(8,128)(2,1)S(1)}, u32[]{:S(2)}, u32[]{:S(2)}) collective-permute-start(bf16[16,48,128]{2,1,0:T(8,128)(2,1)S(1)} %shard_map.51.refs_0_), channel_id=1, source_target_pairs={{0,24},{4,28},{8,16},{12,20},{16,8},{20,12},{24,0},{28,4},{1,25},{... | collective-permute-start | bytes 589832 | tf_op jit(solution)/shard_map/ppermute | solution.py:349
  54.1 2.8 %shard_map.46 = (s32[13]{0:T(128)S(1)}, s32[192]{0:T(256)S(1)}, s32[192]{0:T(256)S(1)}, bf16[192,128,128]{2,1,0:T(8,128)(2,1)S(1)}) custom-call(s32[65]{0:T(128)S(1)} %bitcast.4, s32[192]{0:T(256)S(1)} %bitcast.3, bf16[192,128,128]{2,1,0:T(8,128)(2,1)} %bitcast.5), custom_call_target="tpu_custom_call" | custom-call | flops 67108864 | bytes 4194304 | tf_op jit(solution)/shard_map/pallas_call | solution.py:117
  56.9 1.7 %shard_map.48 = (s16[2064,128]{1,0:T(8,128)(2,1)S(1)}, bf16[128,128,128]{2,1,0:T(8,128)(2,1)S(1)}) custom-call(s32[13]{0:T(128)S(1)} %get-tuple-element.24.range_ref, s32[192]{0:T(256)S(1)} %get-tuple-element.25.index_ref, s32[192]{0:T(256)S(1)} %get-tuple-element.26.row_ref, bf16[192,128,128]{2,1,0:T(8,128)(2,1)S(1)} %get-tuple-element.27.store, ...), custom_call_target="tpu_custom_call" | custom-call | flops 402653184 | bytes 4194304 | tf_op jit(solution)/shard_map/pallas_call | solution.py:208
  58.9 3.7 %collective-permute-start.8 = (s16[2064,128]{1,0:T(8,128)(2,1)S(1)}, s16[2064,128]{1,0:T(8,128)(2,1)S(1)}, u32[]{:S(2)}, u32[]{:S(2)}) collective-permute-start(s16[2064,128]{1,0:T(8,128)(2,1)S(1)} %get-tuple-element.30), channel_id=1, source_target_pairs={{0,1},{3,2},{4,5},{7,6},{8,9},{11,10},{12,13},{15,14},{16,17},{19,... | collective-permute-start | bytes 1585160 | tf_op jit(solution)/shard_map/ppermute | solution.py:404
  68.1 2.5 %shard_map.53 = (s16[784,128]{1,0:T(8,128)(2,1)S(1)}, s16[784,128]{1,0:T(8,128)(2,1)S(1)}, f32[16,48,128]{2,1,0:T(8,128)S(1)}) custom-call(s32[13]{0:T(128)S(1)} %get-tuple-element.24.range_ref, s32[192]{0:T(256)S(1)} %get-tuple-element.25.index_ref, s32[192]{0:T(256)S(1)} %get-tuple-element.26.row_ref, bf16[192,128,128]{2,1,0:T(8,128)(2,1)S(1)} %get-tuple-element.27.store, ...), custom_call_target="tpu_custom_call" | custom-call | flops 301989888 | bytes 4194304 | tf_op jit(solution)/shard_map/pallas_call | solution.py:232
  70.6 2.5 %collective-permute-start.18 = (s16[784,128]{1,0:T(8,128)(2,1)S(1)}, s16[784,128]{1,0:T(8,128)(2,1)S(1)}, u32[]{:S(2)}, u32[]{:S(2)}) collective-permute-start(s16[784,128]{1,0:T(8,128)(2,1)S(1)} %get-tuple-element.35), channel_id=1, source_target_pairs={{0,3},{3,0},{1,2},{2,1},{4,7},{7,4},{5,6},{6,5},{8,11},{11,8},{9,1... | collective-permute-start | bytes 602120 | tf_op jit(solution)/shard_map/ppermute | solution.py:386
  75.0 3.6 %collective-permute-start.20 = (s16[784,128]{1,0:T(8,128)(2,1)S(1)}, s16[784,128]{1,0:T(8,128)(2,1)S(1)}, u32[]{:S(2)}, u32[]{:S(2)}) collective-permute-start(s16[784,128]{1,0:T(8,128)(2,1)S(1)} %get-tuple-element.37), channel_id=1, source_target_pairs={{0,1},{1,0},{2,3},{3,2},{4,5},{5,4},{6,7},{7,6},{8,9},{9,8},{10,11... | collective-permute-start | bytes 602120 | tf_op jit(solution)/shard_map/ppermute | solution.py:386
  78.6 3.0 %shard_map.49 = (s16[2064,128]{1,0:T(8,128)(2,1)S(1)}, s16[2064,128]{1,0:T(8,128)(2,1)S(1)}, f32[16,128,128]{2,1,0:T(8,128)S(1)}) custom-call(s32[13]{0:T(128)S(1)} %get-tuple-element.24.range_ref, s32[192]{0:T(256)S(1)} %get-tuple-element.25.index_ref, s32[192]{0:T(256)S(1)} %get-tuple-element.26.row_ref, ...), custom_call_target="tpu_custom_call" | custom-call | flops 805306368 | bytes 4194304 | tf_op jit(solution)/shard_map/pallas_call | solution.py:232
  82.1 7.3 %collective-permute-done.18.refs_1_ = s16[784,128]{1,0:T(8,128)(2,1)S(1)} collective-permute-done((s16[784,128]{1,0:T(8,128)(2,1)S(1)}, s16[784,128]{1,0:T(8,128)(2,1)S(1)}, u32[]{:S(2)}, u32[]{:S(2)}) %collective-permute-start.18) | collective-permute-done | bytes 200736 | tf_op jit(solution)/shard_map/ppermute | solution.py:386
  90.7 3.5 %collective-permute-start.10 = (s16[2064,128]{1,0:T(8,128)(2,1)S(1)}, s16[2064,128]{1,0:T(8,128)(2,1)S(1)}, u32[]{:S(2)}, u32[]{:S(2)}) collective-permute-start(s16[2064,128]{1,0:T(8,128)(2,1)S(1)} %get-tuple-element.32), channel_id=1, source_target_pairs={{0,1},{1,0},{2,3},{3,2},{4,5},{5,4},{6,7},{7,6},{8,9},{9,8},{10,11... | collective-permute-start | bytes 1585160 | tf_op jit(solution)/shard_map/ppermute | solution.py:392
  94.2 2.7 %shard_map.56 = (s16[1296,128]{1,0:T(8,128)(2,1)S(1)}, s16[1296,128]{1,0:T(8,128)(2,1)S(1)}, f32[16,80,128]{2,1,0:T(8,128)S(1)}) custom-call(s32[13]{0:T(128)S(1)} %get-tuple-element.24.range_ref, s32[192]{0:T(256)S(1)} %get-tuple-element.25.index_ref, s32[192]{0:T(256)S(1)} %get-tuple-element.26.row_ref, ...), custom_call_target="tpu_custom_call" | custom-call | flops 503316480 | bytes 4194304 | tf_op jit(solution)/shard_map/pallas_call | solution.py:232
  97.3 2.0 %collective-permute-start.31 = (s16[1296,128]{1,0:T(8,128)(2,1)S(1)}, s16[1296,128]{1,0:T(8,128)(2,1)S(1)}, u32[]{:S(2)}, u32[]{:S(2)}) collective-permute-start(s16[1296,128]{1,0:T(8,128)(2,1)S(1)} %get-tuple-element.42), channel_id=1, source_target_pairs={{0,1},{1,0},{2,3},{3,2},{4,5},{5,4},{6,7},{7,6},{8,9},{9,8},{10,11... | collective-permute-start | bytes 995336 | tf_op jit(solution)/shard_map/ppermute | solution.py:392
  100.4 24.7 %collective-permute-done.31.refs_7_ = s16[1296,128]{1,0:T(8,128)(2,1)S(1)} collective-permute-done((s16[1296,128]{1,0:T(8,128)(2,1)S(1)}, s16[1296,128]{1,0:T(8,128)(2,1)S(1)}, u32[]{:S(2)}, u32[]{:S(2)}) %collective-permute-start.31) | collective-permute-done | bytes 331808 | tf_op jit(solution)/shard_map/ppermute | solution.py:392
  125.1 20.6 %collective-permute-done.30.refs_6_ = s16[1296,128]{1,0:T(8,128)(2,1)S(1)} collective-permute-done((s16[1296,128]{1,0:T(8,128)(2,1)S(1)}, s16[1296,128]{1,0:T(8,128)(2,1)S(1)}, u32[]{:S(2)}, u32[]{:S(2)}) %collective-permute-start.30) | collective-permute-done | bytes 331808 | tf_op jit(solution)/shard_map/ppermute | solution.py:408
  145.7 1.6 %shard_map.58.refs_4_ = bf16[2048,256]{1,0:T(8,128)(2,1)} custom-call(f32[16,48,128]{2,1,0:T(8,128)S(1)} %get-tuple-element.34.refs_0_, s16[784,128]{1,0:T(8,128)(2,1)S(1)} %collective-permute-done.18.refs_1_, s16[784,128]{1,0:T(8,128)(2,1)S(1)} %collective-permute-done.19.refs_2_, s16[784,128]{1,0:T(8,128)(2,1)S(1)} %collective-permute-done.20.refs_3_, ...), custom_call_target="tpu_custom_call" | custom-call | flops 268435456 | bytes 4194304 | tf_op jit(solution)/shard_map/pallas_call | solution.py:330
  147.2 1.6 %shard_map.59 = bf16[2048,256]{1,0:T(8,128)(2,1)} custom-call(f32[16,128,128]{2,1,0:T(8,128)S(1)} %get-tuple-element.29.refs_0_, s16[2064,128]{1,0:T(8,128)(2,1)S(1)} %collective-permute-done.7.refs_1_, s16[2064,128]{1,0:T(8,128)(2,1)S(1)} %collective-permute-done.9.refs_2_, ...), custom_call_target="tpu_custom_call", output_to_operand_aliasing={{}: (4, {})} | custom-call | flops 268435456 | bytes 4194304 | tf_op jit(solution)/shard_map/pallas_call | solution.py:330
  (60 shorter events, 19.2 us)
Async XLA Ops:
  4.9 34.1 %collective-permute-start.1 = (bf16[16,128,128]{2,1,0:T(8,128)(2,1)S(1)}, bf16[16,128,128]{2,1,0:T(8,128)(2,1)S(1)}, u32[]{:S(2)}, u32[]{:S(2)}) collective-permute-start(bf16[16,128,128]{2,1,0:T(8,128)(2,1)S(1)} %shard_map.47.refs_0_), channel_id=1, source_target_pairs={{0,8},{4,12},{8,0},{12,4},{16,24},{20,28},{24,16},{28,20},{1,9},{5... | collective-permute-start | bytes 1572872 | tf_op jit(solution)/shard_map/ppermute | solution.py:349
  5.0 34.5 %collective-permute-start.3 = (bf16[16,128,128]{2,1,0:T(8,128)(2,1)S(1)}, bf16[16,128,128]{2,1,0:T(8,128)(2,1)S(1)}, u32[]{:S(2)}, u32[]{:S(2)}) collective-permute-start(bf16[16,128,128]{2,1,0:T(8,128)(2,1)S(1)} %shard_map.47.refs_0_), channel_id=1, source_target_pairs={{0,16},{4,20},{8,24},{12,28},{16,0},{20,4},{24,8},{28,12},{1,17},{... | collective-permute-start | bytes 1572872 | tf_op jit(solution)/shard_map/ppermute | solution.py:349
  7.1 32.6 %collective-permute-start.5 = (bf16[16,128,128]{2,1,0:T(8,128)(2,1)S(1)}, bf16[16,128,128]{2,1,0:T(8,128)(2,1)S(1)}, u32[]{:S(2)}, u32[]{:S(2)}) collective-permute-start(bf16[16,128,128]{2,1,0:T(8,128)(2,1)S(1)} %shard_map.47.refs_0_), channel_id=1, source_target_pairs={{0,24},{4,28},{8,16},{12,20},{16,8},{20,12},{24,0},{28,4},{1,25},{... | collective-permute-start | bytes 1572872 | tf_op jit(solution)/shard_map/ppermute | solution.py:349
  8.5 25.0 %collective-permute-start.14 = (bf16[16,48,128]{2,1,0:T(8,128)(2,1)S(1)}, bf16[16,48,128]{2,1,0:T(8,128)(2,1)S(1)}, u32[]{:S(2)}, u32[]{:S(2)}) collective-permute-start(bf16[16,48,128]{2,1,0:T(8,128)(2,1)S(1)} %shard_map.51.refs_0_), channel_id=1, source_target_pairs={{0,16},{4,20},{8,24},{12,28},{16,0},{20,4},{24,8},{28,12},{1,17},{... | collective-permute-start | bytes 589832 | tf_op jit(solution)/shard_map/ppermute | solution.py:349
  10.4 28.6 %collective-permute-start.22 = (bf16[16,80,128]{2,1,0:T(8,128)(2,1)S(1)}, bf16[16,80,128]{2,1,0:T(8,128)(2,1)S(1)}, u32[]{:S(2)}, u32[]{:S(2)}) collective-permute-start(bf16[16,80,128]{2,1,0:T(8,128)(2,1)S(1)} %shard_map.54.refs_0_), channel_id=1, source_target_pairs={{0,8},{4,12},{8,0},{12,4},{16,24},{20,28},{24,16},{28,20},{1,9},{5... | collective-permute-start | bytes 983048 | tf_op jit(solution)/shard_map/ppermute | solution.py:349
  39.0 11.7 %collective-permute-start = (bf16[16,128,128]{2,1,0:T(8,128)(2,1)S(1)}, bf16[16,128,128]{2,1,0:T(8,128)(2,1)S(1)}, u32[]{:S(2)}, u32[]{:S(2)}) collective-permute-start(bf16[16,128,128]{2,1,0:T(8,128)(2,1)S(1)} %shard_map.47.refs_0_), channel_id=1, source_target_pairs={{0,4},{4,0},{8,12},{12,8},{16,20},{20,16},{24,28},{28,24},{1,5},{5... | collective-permute-start | bytes 1572872 | tf_op jit(solution)/shard_map/ppermute | solution.py:350
  39.0 14.3 %collective-permute-start.2 = (bf16[16,128,128]{2,1,0:T(8,128)(2,1)S(1)}, bf16[16,128,128]{2,1,0:T(8,128)(2,1)S(1)}, u32[]{:S(2)}, u32[]{:S(2)}) collective-permute-start(bf16[16,128,128]{2,1,0:T(8,128)(2,1)S(1)} %collective-permute-done.1.refs_2_), channel_id=1, source_target_pairs={{0,4},{4,0},{8,12},{12,8},{16,20},{20,16},{24,28},{28,24},{1,5},{5... | collective-permute-start | bytes 1572872 | tf_op jit(solution)/shard_map/ppermute | solution.py:350
  39.5 14.0 %collective-permute-start.4 = (bf16[16,128,128]{2,1,0:T(8,128)(2,1)S(1)}, bf16[16,128,128]{2,1,0:T(8,128)(2,1)S(1)}, u32[]{:S(2)}, u32[]{:S(2)}) collective-permute-start(bf16[16,128,128]{2,1,0:T(8,128)(2,1)S(1)} %collective-permute-done.3.refs_4_), channel_id=1, source_target_pairs={{0,4},{4,0},{8,12},{12,8},{16,20},{20,16},{24,28},{28,24},{1,5},{5... | collective-permute-start | bytes 1572872 | tf_op jit(solution)/shard_map/ppermute | solution.py:350
  39.6 14.3 %collective-permute-start.6 = (bf16[16,128,128]{2,1,0:T(8,128)(2,1)S(1)}, bf16[16,128,128]{2,1,0:T(8,128)(2,1)S(1)}, u32[]{:S(2)}, u32[]{:S(2)}) collective-permute-start(bf16[16,128,128]{2,1,0:T(8,128)(2,1)S(1)} %collective-permute-done.5.refs_6_), channel_id=1, source_target_pairs={{0,4},{4,0},{8,12},{12,8},{16,20},{20,16},{24,28},{28,24},{1,5},{5... | collective-permute-start | bytes 1572872 | tf_op jit(solution)/shard_map/ppermute | solution.py:350
  50.7 11.9 %collective-permute-start.21 = (bf16[16,80,128]{2,1,0:T(8,128)(2,1)S(1)}, bf16[16,80,128]{2,1,0:T(8,128)(2,1)S(1)}, u32[]{:S(2)}, u32[]{:S(2)}) collective-permute-start(bf16[16,80,128]{2,1,0:T(8,128)(2,1)S(1)} %shard_map.54.refs_0_), channel_id=1, source_target_pairs={{0,4},{4,0},{8,12},{12,8},{16,20},{20,16},{24,28},{28,24},{1,5},{5... | collective-permute-start | bytes 983048 | tf_op jit(solution)/shard_map/ppermute | solution.py:350
  53.3 9.4 %collective-permute-start.23 = (bf16[16,80,128]{2,1,0:T(8,128)(2,1)S(1)}, bf16[16,80,128]{2,1,0:T(8,128)(2,1)S(1)}, u32[]{:S(2)}, u32[]{:S(2)}) collective-permute-start(bf16[16,80,128]{2,1,0:T(8,128)(2,1)S(1)} %collective-permute-done.22.refs_2_), channel_id=1, source_target_pairs={{0,4},{4,0},{8,12},{12,8},{16,20},{20,16},{24,28},{28,24},{1,5},{5... | collective-permute-start | bytes 983048 | tf_op jit(solution)/shard_map/ppermute | solution.py:350
  53.6 9.6 %collective-permute-start.25 = (bf16[16,80,128]{2,1,0:T(8,128)(2,1)S(1)}, bf16[16,80,128]{2,1,0:T(8,128)(2,1)S(1)}, u32[]{:S(2)}, u32[]{:S(2)}) collective-permute-start(bf16[16,80,128]{2,1,0:T(8,128)(2,1)S(1)} %collective-permute-done.24.refs_4_), channel_id=1, source_target_pairs={{0,4},{4,0},{8,12},{12,8},{16,20},{20,16},{24,28},{28,24},{1,5},{5... | collective-permute-start | bytes 983048 | tf_op jit(solution)/shard_map/ppermute | solution.py:350
  53.9 9.4 %collective-permute-start.27 = (bf16[16,80,128]{2,1,0:T(8,128)(2,1)S(1)}, bf16[16,80,128]{2,1,0:T(8,128)(2,1)S(1)}, u32[]{:S(2)}, u32[]{:S(2)}) collective-permute-start(bf16[16,80,128]{2,1,0:T(8,128)(2,1)S(1)} %collective-permute-done.26.refs_6_), channel_id=1, source_target_pairs={{0,4},{4,0},{8,12},{12,8},{16,20},{20,16},{24,28},{28,24},{1,5},{5... | collective-permute-start | bytes 983048 | tf_op jit(solution)/shard_map/ppermute | solution.py:350
  58.9 16.1 %collective-permute-start.8 = (s16[2064,128]{1,0:T(8,128)(2,1)S(1)}, s16[2064,128]{1,0:T(8,128)(2,1)S(1)}, u32[]{:S(2)}, u32[]{:S(2)}) collective-permute-start(s16[2064,128]{1,0:T(8,128)(2,1)S(1)} %get-tuple-element.30), channel_id=1, source_target_pairs={{0,1},{3,2},{4,5},{7,6},{8,9},{11,10},{12,13},{15,14},{16,17},{19,... | collective-permute-start | bytes 1585160 | tf_op jit(solution)/shard_map/ppermute | solution.py:404
  65.3 28.9 %collective-permute-start.29 = (s16[1296,128]{1,0:T(8,128)(2,1)S(1)}, s16[1296,128]{1,0:T(8,128)(2,1)S(1)}, u32[]{:S(2)}, u32[]{:S(2)}) collective-permute-start(s16[1296,128]{1,0:T(8,128)(2,1)S(1)} %get-tuple-element.40), channel_id=1, source_target_pairs={{0,1},{3,2},{4,5},{7,6},{8,9},{11,10},{12,13},{15,14},{16,17},{19,... | collective-permute-start | bytes 995336 | tf_op jit(solution)/shard_map/ppermute | solution.py:404
  70.6 18.8 %collective-permute-start.18 = (s16[784,128]{1,0:T(8,128)(2,1)S(1)}, s16[784,128]{1,0:T(8,128)(2,1)S(1)}, u32[]{:S(2)}, u32[]{:S(2)}) collective-permute-start(s16[784,128]{1,0:T(8,128)(2,1)S(1)} %get-tuple-element.35), channel_id=1, source_target_pairs={{0,3},{3,0},{1,2},{2,1},{4,7},{7,4},{5,6},{6,5},{8,11},{11,8},{9,1... | collective-permute-start | bytes 602120 | tf_op jit(solution)/shard_map/ppermute | solution.py:386
  73.1 17.6 %collective-permute-start.19 = (s16[784,128]{1,0:T(8,128)(2,1)S(1)}, s16[784,128]{1,0:T(8,128)(2,1)S(1)}, u32[]{:S(2)}, u32[]{:S(2)}) collective-permute-start(s16[784,128]{1,0:T(8,128)(2,1)S(1)} %get-tuple-element.36), channel_id=1, source_target_pairs={{0,2},{1,3},{2,0},{3,1},{4,6},{5,7},{6,4},{7,5},{8,10},{9,11},{10,... | collective-permute-start | bytes 602120 | tf_op jit(solution)/shard_map/ppermute | solution.py:386
  73.1 26.1 %collective-permute-start.28 = (s16[1296,128]{1,0:T(8,128)(2,1)S(1)}, s16[1296,128]{1,0:T(8,128)(2,1)S(1)}, u32[]{:S(2)}, u32[]{:S(2)}) collective-permute-start(s16[1296,128]{1,0:T(8,128)(2,1)S(1)} %get-tuple-element.40), channel_id=1, source_target_pairs={{1,2},{2,1},{5,6},{6,5},{9,10},{10,9},{13,14},{14,13},{17,18},{18,... | collective-permute-start | bytes 995336 | tf_op jit(solution)/shard_map/ppermute | solution.py:389
  75.0 22.3 %collective-permute-start.20 = (s16[784,128]{1,0:T(8,128)(2,1)S(1)}, s16[784,128]{1,0:T(8,128)(2,1)S(1)}, u32[]{:S(2)}, u32[]{:S(2)}) collective-permute-start(s16[784,128]{1,0:T(8,128)(2,1)S(1)} %get-tuple-element.37), channel_id=1, source_target_pairs={{0,1},{1,0},{2,3},{3,2},{4,5},{5,4},{6,7},{7,6},{8,9},{9,8},{10,11... | collective-permute-start | bytes 602120 | tf_op jit(solution)/shard_map/ppermute | solution.py:386
  89.4 57.8 %collective-permute-start.7 = (s16[2064,128]{1,0:T(8,128)(2,1)S(1)}, s16[2064,128]{1,0:T(8,128)(2,1)S(1)}, u32[]{:S(2)}, u32[]{:S(2)}) collective-permute-start(s16[2064,128]{1,0:T(8,128)(2,1)S(1)} %get-tuple-element.30), channel_id=1, source_target_pairs={{1,2},{2,1},{5,6},{6,5},{9,10},{10,9},{13,14},{14,13},{17,18},{18,... | collective-permute-start | bytes 1585160 | tf_op jit(solution)/shard_map/ppermute | solution.py:389
  90.7 56.5 %collective-permute-start.10 = (s16[2064,128]{1,0:T(8,128)(2,1)S(1)}, s16[2064,128]{1,0:T(8,128)(2,1)S(1)}, u32[]{:S(2)}, u32[]{:S(2)}) collective-permute-start(s16[2064,128]{1,0:T(8,128)(2,1)S(1)} %get-tuple-element.32), channel_id=1, source_target_pairs={{0,1},{1,0},{2,3},{3,2},{4,5},{5,4},{6,7},{7,6},{8,9},{9,8},{10,11... | collective-permute-start | bytes 1585160 | tf_op jit(solution)/shard_map/ppermute | solution.py:392
  94.2 53.0 %collective-permute-start.9 = (s16[2064,128]{1,0:T(8,128)(2,1)S(1)}, s16[2064,128]{1,0:T(8,128)(2,1)S(1)}, u32[]{:S(2)}, u32[]{:S(2)}) collective-permute-start(s16[2064,128]{1,0:T(8,128)(2,1)S(1)} %shard_map.50), channel_id=1, source_target_pairs={{0,2},{1,3},{2,0},{3,1},{4,6},{5,7},{6,4},{7,5},{8,10},{9,11},{10,... | collective-permute-start | bytes 1585160 | tf_op jit(solution)/shard_map/ppermute | solution.py:408
  97.3 27.8 %collective-permute-start.31 = (s16[1296,128]{1,0:T(8,128)(2,1)S(1)}, s16[1296,128]{1,0:T(8,128)(2,1)S(1)}, u32[]{:S(2)}, u32[]{:S(2)}) collective-permute-start(s16[1296,128]{1,0:T(8,128)(2,1)S(1)} %get-tuple-element.42), channel_id=1, source_target_pairs={{0,1},{1,0},{2,3},{3,2},{4,5},{5,4},{6,7},{7,6},{8,9},{9,8},{10,11... | collective-permute-start | bytes 995336 | tf_op jit(solution)/shard_map/ppermute | solution.py:392
  99.3 46.4 %collective-permute-start.30 = (s16[1296,128]{1,0:T(8,128)(2,1)S(1)}, s16[1296,128]{1,0:T(8,128)(2,1)S(1)}, u32[]{:S(2)}, u32[]{:S(2)}) collective-permute-start(s16[1296,128]{1,0:T(8,128)(2,1)S(1)} %shard_map.57), channel_id=1, source_target_pairs={{0,2},{1,3},{2,0},{3,1},{4,6},{5,7},{6,4},{7,5},{8,10},{9,11},{10,... | collective-permute-start | bytes 995336 | tf_op jit(solution)/shard_map/ppermute | solution.py:408
  (11 other events, 154.5 us)

commit v5 on v4

--- a/solution.py
+++ b/solution.py
@@ -13,6 +13,7 @@
 MIB = 1 << 20
 STAGE_MIB = 46
 DIRECT_CHUNKS = 1
+PASSED_FROM = 2
 CHUNKS = (3, 5, 8)
 TOP = 32700.0
 STEPS = 8.0
@@ -167,13 +168,15 @@
 
 def head_kernel(owned, range_ref, index_ref, row_ref, store, *refs):
     *piece_refs, out_ref, panel, acc, codes = refs
-    mine, width = piece_refs[0].shape[:2]
-
-    for p, ref in enumerate(piece_refs):
-
-        @pl.loop(0, mine, unroll=4)
+    width = panel.shape[1]
+    at = 0
+    for ref in piece_refs:
+
+        @pl.loop(0, ref.shape[0], unroll=4)
         def _(j):
-            panel[p * mine + j] = ref[j]
+            panel[at + j] = ref[j]
+
+        at += ref.shape[0]
 
     clear(acc, owned)
     low, high, first = (range_ref[n] for n in range(3))
@@ -200,7 +203,7 @@
 
 def head(ranges, index, rows, store, pieces, owned):
     slots, block = store.shape[:2]
-    mine, width = pieces[0].shape[:2]
+    width = pieces[0].shape[1]
     tail = -(-owned // 16) * 16
     smem = pl.BlockSpec(memory_space=pltpu.SMEM)
     whole = pl.BlockSpec(memory_space=pltpu.VMEM)
@@ -209,7 +212,7 @@
         functools.partial(head_kernel, owned),
         out_shape=[
             jax.ShapeDtypeStruct((owned * width + tail, block), jnp.int16),
-            jax.ShapeDtypeStruct((len(pieces) * mine, width, block), store.dtype),
+            jax.ShapeDtypeStruct((sum(p.shape[0] for p in pieces), width, block), store.dtype),
         ],
         in_specs=[smem] * 3 + [whole] * (1 + len(pieces)),
         out_specs=[whole] * 2,
@@ -343,11 +346,21 @@
     )(*arrays)
 
 
-def gather(part, devices):
+def gather(part, devices, passed):
+    def swap(array, bits):
+        return lax.ppermute(array, "row", [(d, d ^ bits) for d in range(devices)])
+
+    near = {0: [part]}
+    for p in range(2, devices, 2):
+        low = p & -p
+        if passed and p != low and (p ^ low) & ((p ^ low) - 1) == 0:
+            half = part.shape[0] // 2
+            near[p] = [swap(near[p ^ low][0][:half], low), swap(near[low][0][half:], p ^ low)]
+        else:
+            near[p] = [swap(part, p)]
     pieces = []
-    for p in range(0, devices, 2):
-        near = part if p == 0 else lax.ppermute(part, "row", [(d, d ^ p) for d in range(devices)])
-        pieces += [near, lax.ppermute(near, "row", [(d, d ^ 1) for d in range(devices)])]
+    for arrays in near.values():
+        pieces += [*arrays, *(swap(array, 1) for array in arrays)]
     return pieces
 
 
@@ -432,9 +445,9 @@
 
     starts = [total_width * sum(CHUNKS[:n]) // sum(CHUNKS) for n in range(len(CHUNKS) + 1)]
     parts = []
-    for first, last in zip(starts, starts[1:]):
+    for chunk, (first, last) in enumerate(zip(starts, starts[1:])):
         piece = turn(features, block, first, last - first)
-        parts.append(gather(piece, row_count))
+        parts.append(gather(piece, row_count, chunk >= PASSED_FROM))
     ranges, index, rows, store = stage(
         pointers, block_cols[0, 0], values, owner_of, count + 1, mine
     )

time: 149 us -> 143 us (0.960)
  waiting for transfers between devices: 87.7 us -> 82 us
    ppermute x21 -> x23, waiting for transfers between devices: 33.3 us -> 27.6 us  [swap(): return lax.ppermute(array, 'row', [(d, d ^ bits) for d in range(devices)])]
    ppermute x21 -> x23, starting transfers between devices: 19.8 us -> 18.9 us  [swap(): return lax.ppermute(array, 'row', [(d, d ^ bits) for d in range(devices)])]
  transfers between devices with their start and end apart: 32 -> 34, of which waited for: 10 -> 11; matrix products, arithmetic and copies ran while one was open for 0% -> 0% of each run, Pallas kernels for 13% -> 13%
where the time goes in v5:
time: 143 us; the launch traced here: 142 us
  waiting for transfers between devices  82 us (57%)
  starting transfers between devices  37.8 us (26%)
  Pallas kernels  20.7 us (14%)
    ppermute x7, waiting for transfers between devices, reduce(): got.append(lax.ppermute(message, 'col', pairs))  53.2 us
    ppermute x23, waiting for transfers between devices, swap(): return lax.ppermute(array, 'row', [(d, d ^ bits) for d in range(devices)])  27.6 us
    ppermute x23, starting transfers between devices, swap(): return lax.ppermute(array, 'row', [(d, d ^ bits) for d in range(devices)])  18.9 us
    ppermute x7, starting transfers between devices, reduce(): got.append(lax.ppermute(message, 'col', pairs))  12.7 us
    pallas_call x3, Pallas kernels, rest(): pl.pallas_call(functools.partial(rest_kernel, owned, messages, local_rows...  8.21 us
    ppermute x2, starting transfers between devices, reduce(): array = lax.ppermute(message, 'col', hops)  4.81 us
    pallas_call x3, Pallas kernels, head(): pl.pallas_call(functools.partial(head_kernel, owned), out_shape=[jax.Shap...  4.72 us
    pallas_call x2, Pallas kernels, finish(): pl.pallas_call(functools.partial(finish_kernel, owned, sizes), out_shape=...  3.15 us
  transfers between devices with their start and end apart: 34, of which 11 were waited for; matrix products, arithmetic and copies ran while one was open for 0% of the time, Pallas kernels for 13%

profile of v5, /device:TPU:0, one launch (start us, length us, event | category | flops | bytes accessed | tf_op | source)
XLA Modules:
  0.0 142.0 jit_solution(16468452067175365022)
XLA Ops:
  1.6 3.0 %collective-permute-start.1 = (bf16[16,128,128]{2,1,0:T(8,128)(2,1)S(1)}, bf16[16,128,128]{2,1,0:T(8,128)(2,1)S(1)}, u32[]{:S(2)}, u32[]{:S(2)}) collective-permute-start(bf16[16,128,128]{2,1,0:T(8,128)(2,1)S(1)} %shard_map.47.refs_0_), channel_id=1, source_target_pairs={{0,8},{4,12},{8,0},{12,4},{16,24},{20,28},{24,16},{28,20},{1,9},{5... | collective-permute-start | bytes 1572872 | tf_op jit(solution)/shard_map/ppermute | solution.py:351
  7.5 2.0 %collective-permute-start.24 = (bf16[16,80,128]{2,1,0:T(8,128)(2,1)S(1)}, bf16[16,80,128]{2,1,0:T(8,128)(2,1)S(1)}, u32[]{:S(2)}, u32[]{:S(2)}) collective-permute-start(bf16[16,80,128]{2,1,0:T(8,128)(2,1)S(1)} %shard_map.54.refs_0_), channel_id=1, source_target_pairs={{0,8},{4,12},{8,0},{12,4},{16,24},{20,28},{24,16},{28,20},{1,9},{5... | collective-permute-start | bytes 983048 | tf_op jit(solution)/shard_map/ppermute | solution.py:351
  9.5 12.1 %collective-permute-done.14.refs_2_ = bf16[16,48,128]{2,1,0:T(8,128)(2,1)S(1)} collective-permute-done((bf16[16,48,128]{2,1,0:T(8,128)(2,1)S(1)}, bf16[16,48,128]{2,1,0:T(8,128)(2,1)S(1)}, u32[]{:S(2)}, u32[]{:S(2)}) %collective-permute-start.14) | collective-permute-done | bytes 196640 | tf_op jit(solution)/shard_map/ppermute | solution.py:351
  21.6 2.0 %collective-permute-start.26 = (bf16[16,80,128]{2,1,0:T(8,128)(2,1)S(1)}, bf16[16,80,128]{2,1,0:T(8,128)(2,1)S(1)}, u32[]{:S(2)}, u32[]{:S(2)}) collective-permute-start(bf16[16,80,128]{2,1,0:T(8,128)(2,1)S(1)} %shard_map.54.refs_0_), channel_id=1, source_target_pairs={{0,16},{4,20},{8,24},{12,28},{16,0},{20,4},{24,8},{28,12},{1,17},{... | collective-permute-start | bytes 983048 | tf_op jit(solution)/shard_map/ppermute | solution.py:351
  25.7 3.0 %collective-permute-done.24.refs_2_ = bf16[16,80,128]{2,1,0:T(8,128)(2,1)S(1)} collective-permute-done((bf16[16,80,128]{2,1,0:T(8,128)(2,1)S(1)}, bf16[16,80,128]{2,1,0:T(8,128)(2,1)S(1)}, u32[]{:S(2)}, u32[]{:S(2)}) %collective-permute-start.24) | collective-permute-done | bytes 327712 | tf_op jit(solution)/shard_map/ppermute | solution.py:351
  28.6 7.5 %collective-permute-done.26.refs_4_ = bf16[16,80,128]{2,1,0:T(8,128)(2,1)S(1)} collective-permute-done((bf16[16,80,128]{2,1,0:T(8,128)(2,1)S(1)}, bf16[16,80,128]{2,1,0:T(8,128)(2,1)S(1)}, u32[]{:S(2)}, u32[]{:S(2)}) %collective-permute-start.26) | collective-permute-done | bytes 327712 | tf_op jit(solution)/shard_map/ppermute | solution.py:351
  37.6 2.1 %collective-permute-start.6 = (bf16[8,128,128]{2,1,0:T(8,128)(2,1)S(1)}, bf16[8,128,128]{2,1,0:T(8,128)(2,1)S(1)}, u32[]{:S(2)}, u32[]{:S(2)}) collective-permute-start(bf16[8,128,128]{2,1,0:T(8,128)(2,1)S(1)} %slice.9), channel_id=1, source_target_pairs={{0,16},{4,20},{8,24},{12,28},{16,0},{20,4},{24,8},{28,12},{1,17},{... | collective-permute-start | bytes 786440 | tf_op jit(solution)/shard_map/ppermute | solution.py:351
  39.7 2.8 %collective-permute-done.5.refs_6_ = bf16[8,128,128]{2,1,0:T(8,128)(2,1)S(1)} collective-permute-done((bf16[8,128,128]{2,1,0:T(8,128)(2,1)S(1)}, bf16[8,128,128]{2,1,0:T(8,128)(2,1)S(1)}, u32[]{:S(2)}, u32[]{:S(2)}) %collective-permute-start.5) | collective-permute-done | bytes 262176 | tf_op jit(solution)/shard_map/ppermute | solution.py:351
  44.5 2.0 %collective-permute-start.18 = (bf16[16,48,128]{2,1,0:T(8,128)(2,1)S(1)}, bf16[16,48,128]{2,1,0:T(8,128)(2,1)S(1)}, u32[]{:S(2)}, u32[]{:S(2)}) collective-permute-start(bf16[16,48,128]{2,1,0:T(8,128)(2,1)S(1)} %shard_map.51.refs_0_), channel_id=1, source_target_pairs={{0,24},{4,28},{8,16},{12,20},{16,8},{20,12},{24,0},{28,4},{1,25},{... | collective-permute-start | bytes 589832 | tf_op jit(solution)/shard_map/ppermute | solution.py:351
  47.1 2.8 %shard_map.46 = (s32[13]{0:T(128)S(1)}, s32[192]{0:T(256)S(1)}, s32[192]{0:T(256)S(1)}, bf16[192,128,128]{2,1,0:T(8,128)(2,1)S(1)}) custom-call(s32[65]{0:T(128)S(1)} %bitcast.4, s32[192]{0:T(256)S(1)} %bitcast.3, bf16[192,128,128]{2,1,0:T(8,128)(2,1)} %bitcast.5), custom_call_target="tpu_custom_call" | custom-call | flops 67108864 | bytes 4194304 | tf_op jit(solution)/shard_map/pallas_call | solution.py:118
  49.9 1.7 %shard_map.48 = (s16[2064,128]{1,0:T(8,128)(2,1)S(1)}, bf16[128,128,128]{2,1,0:T(8,128)(2,1)S(1)}) custom-call(s32[13]{0:T(128)S(1)} %get-tuple-element.24.range_ref, s32[192]{0:T(256)S(1)} %get-tuple-element.25.index_ref, s32[192]{0:T(256)S(1)} %get-tuple-element.26.row_ref, bf16[192,128,128]{2,1,0:T(8,128)(2,1)S(1)} %get-tuple-element.27.store, ...), custom_call_target="tpu_custom_call" | custom-call | flops 402653184 | bytes 4194304 | tf_op jit(solution)/shard_map/pallas_call | solution.py:211
  52.3 3.5 %collective-permute-start.10 = (s16[2064,128]{1,0:T(8,128)(2,1)S(1)}, s16[2064,128]{1,0:T(8,128)(2,1)S(1)}, u32[]{:S(2)}, u32[]{:S(2)}) collective-permute-start(s16[2064,128]{1,0:T(8,128)(2,1)S(1)} %get-tuple-element.30), channel_id=1, source_target_pairs={{0,1},{3,2},{4,5},{7,6},{8,9},{11,10},{12,13},{15,14},{16,17},{19,... | collective-permute-start | bytes 1585160 | tf_op jit(solution)/shard_map/ppermute | solution.py:417
  61.3 2.5 %shard_map.53 = (s16[784,128]{1,0:T(8,128)(2,1)S(1)}, s16[784,128]{1,0:T(8,128)(2,1)S(1)}, f32[16,48,128]{2,1,0:T(8,128)S(1)}) custom-call(s32[13]{0:T(128)S(1)} %get-tuple-element.24.range_ref, s32[192]{0:T(256)S(1)} %get-tuple-element.25.index_ref, s32[192]{0:T(256)S(1)} %get-tuple-element.26.row_ref, bf16[192,128,128]{2,1,0:T(8,128)(2,1)S(1)} %get-tuple-element.27.store, ...), custom_call_target="tpu_custom_call" | custom-call | flops 301989888 | bytes 4194304 | tf_op jit(solution)/shard_map/pallas_call | solution.py:235
  63.8 2.5 %collective-permute-start.20 = (s16[784,128]{1,0:T(8,128)(2,1)S(1)}, s16[784,128]{1,0:T(8,128)(2,1)S(1)}, u32[]{:S(2)}, u32[]{:S(2)}) collective-permute-start(s16[784,128]{1,0:T(8,128)(2,1)S(1)} %get-tuple-element.35), channel_id=1, source_target_pairs={{0,3},{3,0},{1,2},{2,1},{4,7},{7,4},{5,6},{6,5},{8,11},{11,8},{9,1... | collective-permute-start | bytes 602120 | tf_op jit(solution)/shard_map/ppermute | solution.py:399
  68.2 3.6 %collective-permute-start.22 = (s16[784,128]{1,0:T(8,128)(2,1)S(1)}, s16[784,128]{1,0:T(8,128)(2,1)S(1)}, u32[]{:S(2)}, u32[]{:S(2)}) collective-permute-start(s16[784,128]{1,0:T(8,128)(2,1)S(1)} %get-tuple-element.37), channel_id=1, source_target_pairs={{0,1},{1,0},{2,3},{3,2},{4,5},{5,4},{6,7},{7,6},{8,9},{9,8},{10,11... | collective-permute-start | bytes 602120 | tf_op jit(solution)/shard_map/ppermute | solution.py:399
  71.8 3.0 %shard_map.49 = (s16[2064,128]{1,0:T(8,128)(2,1)S(1)}, s16[2064,128]{1,0:T(8,128)(2,1)S(1)}, f32[16,128,128]{2,1,0:T(8,128)S(1)}) custom-call(s32[13]{0:T(128)S(1)} %get-tuple-element.24.range_ref, s32[192]{0:T(256)S(1)} %get-tuple-element.25.index_ref, s32[192]{0:T(256)S(1)} %get-tuple-element.26.row_ref, ...), custom_call_target="tpu_custom_call" | custom-call | flops 805306368 | bytes 4194304 | tf_op jit(solution)/shard_map/pallas_call | solution.py:235
  75.3 7.3 %collective-permute-done.20.refs_1_ = s16[784,128]{1,0:T(8,128)(2,1)S(1)} collective-permute-done((s16[784,128]{1,0:T(8,128)(2,1)S(1)}, s16[784,128]{1,0:T(8,128)(2,1)S(1)}, u32[]{:S(2)}, u32[]{:S(2)}) %collective-permute-start.20) | collective-permute-done | bytes 200736 | tf_op jit(solution)/shard_map/ppermute | solution.py:399
  83.9 3.5 %collective-permute-start.12 = (s16[2064,128]{1,0:T(8,128)(2,1)S(1)}, s16[2064,128]{1,0:T(8,128)(2,1)S(1)}, u32[]{:S(2)}, u32[]{:S(2)}) collective-permute-start(s16[2064,128]{1,0:T(8,128)(2,1)S(1)} %get-tuple-element.32), channel_id=1, source_target_pairs={{0,1},{1,0},{2,3},{3,2},{4,5},{5,4},{6,7},{7,6},{8,9},{9,8},{10,11... | collective-permute-start | bytes 1585160 | tf_op jit(solution)/shard_map/ppermute | solution.py:405
  87.4 2.7 %shard_map.56 = (s16[1296,128]{1,0:T(8,128)(2,1)S(1)}, s16[1296,128]{1,0:T(8,128)(2,1)S(1)}, f32[16,80,128]{2,1,0:T(8,128)S(1)}) custom-call(s32[13]{0:T(128)S(1)} %get-tuple-element.24.range_ref, s32[192]{0:T(256)S(1)} %get-tuple-element.25.index_ref, s32[192]{0:T(256)S(1)} %get-tuple-element.26.row_ref, ...), custom_call_target="tpu_custom_call" | custom-call | flops 503316480 | bytes 4194304 | tf_op jit(solution)/shard_map/pallas_call | solution.py:235
  90.5 2.0 %collective-permute-start.33 = (s16[1296,128]{1,0:T(8,128)(2,1)S(1)}, s16[1296,128]{1,0:T(8,128)(2,1)S(1)}, u32[]{:S(2)}, u32[]{:S(2)}) collective-permute-start(s16[1296,128]{1,0:T(8,128)(2,1)S(1)} %get-tuple-element.42), channel_id=1, source_target_pairs={{0,1},{1,0},{2,3},{3,2},{4,5},{5,4},{6,7},{7,6},{8,9},{9,8},{10,11... | collective-permute-start | bytes 995336 | tf_op jit(solution)/shard_map/ppermute | solution.py:405
  93.6 24.7 %collective-permute-done.33.refs_7_ = s16[1296,128]{1,0:T(8,128)(2,1)S(1)} collective-permute-done((s16[1296,128]{1,0:T(8,128)(2,1)S(1)}, s16[1296,128]{1,0:T(8,128)(2,1)S(1)}, u32[]{:S(2)}, u32[]{:S(2)}) %collective-permute-start.33) | collective-permute-done | bytes 331808 | tf_op jit(solution)/shard_map/ppermute | solution.py:405
  118.3 20.6 %collective-permute-done.32.refs_6_ = s16[1296,128]{1,0:T(8,128)(2,1)S(1)} collective-permute-done((s16[1296,128]{1,0:T(8,128)(2,1)S(1)}, s16[1296,128]{1,0:T(8,128)(2,1)S(1)}, u32[]{:S(2)}, u32[]{:S(2)}) %collective-permute-start.32) | collective-permute-done | bytes 331808 | tf_op jit(solution)/shard_map/ppermute | solution.py:421
  138.8 1.6 %shard_map.58.refs_4_ = bf16[2048,256]{1,0:T(8,128)(2,1)} custom-call(f32[16,48,128]{2,1,0:T(8,128)S(1)} %get-tuple-element.34.refs_0_, s16[784,128]{1,0:T(8,128)(2,1)S(1)} %collective-permute-done.20.refs_1_, s16[784,128]{1,0:T(8,128)(2,1)S(1)} %collective-permute-done.21.refs_2_, s16[784,128]{1,0:T(8,128)(2,1)S(1)} %collective-permute-done.22.refs_3_, ...), custom_call_target="tpu_custom_call" | custom-call | flops 268435456 | bytes 4194304 | tf_op jit(solution)/shard_map/pallas_call | solution.py:333
  140.4 1.6 %shard_map.59 = bf16[2048,256]{1,0:T(8,128)(2,1)} custom-call(f32[16,128,128]{2,1,0:T(8,128)S(1)} %get-tuple-element.29.refs_0_, s16[2064,128]{1,0:T(8,128)(2,1)S(1)} %collective-permute-done.9.refs_1_, s16[2064,128]{1,0:T(8,128)(2,1)S(1)} %collective-permute-done.11.refs_2_, ...), custom_call_target="tpu_custom_call", output_to_operand_aliasing={{}: (4, {})} | custom-call | flops 268435456 | bytes 4194304 | tf_op jit(solution)/shard_map/pallas_call | solution.py:333
  (66 shorter events, 21.5 us)
Async XLA Ops:
  1.6 23.5 %collective-permute-start.1 = (bf16[16,128,128]{2,1,0:T(8,128)(2,1)S(1)}, bf16[16,128,128]{2,1,0:T(8,128)(2,1)S(1)}, u32[]{:S(2)}, u32[]{:S(2)}) collective-permute-start(bf16[16,128,128]{2,1,0:T(8,128)(2,1)S(1)} %shard_map.47.refs_0_), channel_id=1, source_target_pairs={{0,8},{4,12},{8,0},{12,4},{16,24},{20,28},{24,16},{28,20},{1,9},{5... | collective-permute-start | bytes 1572872 | tf_op jit(solution)/shard_map/ppermute | solution.py:351
  4.6 20.5 %collective-permute-start.3 = (bf16[16,128,128]{2,1,0:T(8,128)(2,1)S(1)}, bf16[16,128,128]{2,1,0:T(8,128)(2,1)S(1)}, u32[]{:S(2)}, u32[]{:S(2)}) collective-permute-start(bf16[16,128,128]{2,1,0:T(8,128)(2,1)S(1)} %shard_map.47.refs_0_), channel_id=1, source_target_pairs={{0,16},{4,20},{8,24},{12,28},{16,0},{20,4},{24,8},{28,12},{1,17},{... | collective-permute-start | bytes 1572872 | tf_op jit(solution)/shard_map/ppermute | solution.py:351
  6.5 15.2 %collective-permute-start.14 = (bf16[16,48,128]{2,1,0:T(8,128)(2,1)S(1)}, bf16[16,48,128]{2,1,0:T(8,128)(2,1)S(1)}, u32[]{:S(2)}, u32[]{:S(2)}) collective-permute-start(bf16[16,48,128]{2,1,0:T(8,128)(2,1)S(1)} %shard_map.51.refs_0_), channel_id=1, source_target_pairs={{0,8},{4,12},{8,0},{12,4},{16,24},{20,28},{24,16},{28,20},{1,9},{5... | collective-permute-start | bytes 589832 | tf_op jit(solution)/shard_map/ppermute | solution.py:351
  7.1 16.6 %collective-permute-start.16 = (bf16[16,48,128]{2,1,0:T(8,128)(2,1)S(1)}, bf16[16,48,128]{2,1,0:T(8,128)(2,1)S(1)}, u32[]{:S(2)}, u32[]{:S(2)}) collective-permute-start(bf16[16,48,128]{2,1,0:T(8,128)(2,1)S(1)} %shard_map.51.refs_0_), channel_id=1, source_target_pairs={{0,16},{4,20},{8,24},{12,28},{16,0},{20,4},{24,8},{28,12},{1,17},{... | collective-permute-start | bytes 589832 | tf_op jit(solution)/shard_map/ppermute | solution.py:351
  7.5 21.2 %collective-permute-start.24 = (bf16[16,80,128]{2,1,0:T(8,128)(2,1)S(1)}, bf16[16,80,128]{2,1,0:T(8,128)(2,1)S(1)}, u32[]{:S(2)}, u32[]{:S(2)}) collective-permute-start(bf16[16,80,128]{2,1,0:T(8,128)(2,1)S(1)} %shard_map.54.refs_0_), channel_id=1, source_target_pairs={{0,8},{4,12},{8,0},{12,4},{16,24},{20,28},{24,16},{28,20},{1,9},{5... | collective-permute-start | bytes 983048 | tf_op jit(solution)/shard_map/ppermute | solution.py:351
  21.6 14.5 %collective-permute-start.26 = (bf16[16,80,128]{2,1,0:T(8,128)(2,1)S(1)}, bf16[16,80,128]{2,1,0:T(8,128)(2,1)S(1)}, u32[]{:S(2)}, u32[]{:S(2)}) collective-permute-start(bf16[16,80,128]{2,1,0:T(8,128)(2,1)S(1)} %shard_map.54.refs_0_), channel_id=1, source_target_pairs={{0,16},{4,20},{8,24},{12,28},{16,0},{20,4},{24,8},{28,12},{1,17},{... | collective-permute-start | bytes 983048 | tf_op jit(solution)/shard_map/ppermute | solution.py:351
  23.7 13.9 %collective-permute-start.28 = (bf16[16,80,128]{2,1,0:T(8,128)(2,1)S(1)}, bf16[16,80,128]{2,1,0:T(8,128)(2,1)S(1)}, u32[]{:S(2)}, u32[]{:S(2)}) collective-permute-start(bf16[16,80,128]{2,1,0:T(8,128)(2,1)S(1)} %shard_map.54.refs_0_), channel_id=1, source_target_pairs={{0,24},{4,28},{8,16},{12,20},{16,8},{20,12},{24,0},{28,4},{1,25},{... | collective-permute-start | bytes 983048 | tf_op jit(solution)/shard_map/ppermute | solution.py:351
  25.1 18.9 %collective-permute-start = (bf16[16,128,128]{2,1,0:T(8,128)(2,1)S(1)}, bf16[16,128,128]{2,1,0:T(8,128)(2,1)S(1)}, u32[]{:S(2)}, u32[]{:S(2)}) collective-permute-start(bf16[16,128,128]{2,1,0:T(8,128)(2,1)S(1)} %shard_map.47.refs_0_), channel_id=1, source_target_pairs={{0,4},{4,0},{8,12},{12,8},{16,20},{20,16},{24,28},{28,24},{1,5},{5... | collective-permute-start | bytes 1572872 | tf_op jit(solution)/shard_map/ppermute | solution.py:351
  25.1 19.4 %collective-permute-start.2 = (bf16[16,128,128]{2,1,0:T(8,128)(2,1)S(1)}, bf16[16,128,128]{2,1,0:T(8,128)(2,1)S(1)}, u32[]{:S(2)}, u32[]{:S(2)}) collective-permute-start(bf16[16,128,128]{2,1,0:T(8,128)(2,1)S(1)} %collective-permute-done.1.refs_2_), channel_id=1, source_target_pairs={{0,4},{4,0},{8,12},{12,8},{16,20},{20,16},{24,28},{28,24},{1,5},{5... | collective-permute-start | bytes 1572872 | tf_op jit(solution)/shard_map/ppermute | solution.py:351
  28.6 17.9 %collective-permute-start.4 = (bf16[16,128,128]{2,1,0:T(8,128)(2,1)S(1)}, bf16[16,128,128]{2,1,0:T(8,128)(2,1)S(1)}, u32[]{:S(2)}, u32[]{:S(2)}) collective-permute-start(bf16[16,128,128]{2,1,0:T(8,128)(2,1)S(1)} %collective-permute-done.3.refs_4_), channel_id=1, source_target_pairs={{0,4},{4,0},{8,12},{12,8},{16,20},{20,16},{24,28},{28,24},{1,5},{5... | collective-permute-start | bytes 1572872 | tf_op jit(solution)/shard_map/ppermute | solution.py:351
  44.0 11.8 %collective-permute-start.23 = (bf16[16,80,128]{2,1,0:T(8,128)(2,1)S(1)}, bf16[16,80,128]{2,1,0:T(8,128)(2,1)S(1)}, u32[]{:S(2)}, u32[]{:S(2)}) collective-permute-start(bf16[16,80,128]{2,1,0:T(8,128)(2,1)S(1)} %shard_map.54.refs_0_), channel_id=1, source_target_pairs={{0,4},{4,0},{8,12},{12,8},{16,20},{20,16},{24,28},{28,24},{1,5},{5... | collective-permute-start | bytes 983048 | tf_op jit(solution)/shard_map/ppermute | solution.py:351
  46.5 9.9 %collective-permute-start.27 = (bf16[16,80,128]{2,1,0:T(8,128)(2,1)S(1)}, bf16[16,80,128]{2,1,0:T(8,128)(2,1)S(1)}, u32[]{:S(2)}, u32[]{:S(2)}) collective-permute-start(bf16[16,80,128]{2,1,0:T(8,128)(2,1)S(1)} %collective-permute-done.26.refs_4_), channel_id=1, source_target_pairs={{0,4},{4,0},{8,12},{12,8},{16,20},{20,16},{24,28},{28,24},{1,5},{5... | collective-permute-start | bytes 983048 | tf_op jit(solution)/shard_map/ppermute | solution.py:351
  47.0 9.5 %collective-permute-start.29 = (bf16[16,80,128]{2,1,0:T(8,128)(2,1)S(1)}, bf16[16,80,128]{2,1,0:T(8,128)(2,1)S(1)}, u32[]{:S(2)}, u32[]{:S(2)}) collective-permute-start(bf16[16,80,128]{2,1,0:T(8,128)(2,1)S(1)} %collective-permute-done.28.refs_6_), channel_id=1, source_target_pairs={{0,4},{4,0},{8,12},{12,8},{16,20},{20,16},{24,28},{28,24},{1,5},{5... | collective-permute-start | bytes 983048 | tf_op jit(solution)/shard_map/ppermute | solution.py:351
  52.3 15.9 %collective-permute-start.10 = (s16[2064,128]{1,0:T(8,128)(2,1)S(1)}, s16[2064,128]{1,0:T(8,128)(2,1)S(1)}, u32[]{:S(2)}, u32[]{:S(2)}) collective-permute-start(s16[2064,128]{1,0:T(8,128)(2,1)S(1)} %get-tuple-element.30), channel_id=1, source_target_pairs={{0,1},{3,2},{4,5},{7,6},{8,9},{11,10},{12,13},{15,14},{16,17},{19,... | collective-permute-start | bytes 1585160 | tf_op jit(solution)/shard_map/ppermute | solution.py:417
  58.5 28.9 %collective-permute-start.31 = (s16[1296,128]{1,0:T(8,128)(2,1)S(1)}, s16[1296,128]{1,0:T(8,128)(2,1)S(1)}, u32[]{:S(2)}, u32[]{:S(2)}) collective-permute-start(s16[1296,128]{1,0:T(8,128)(2,1)S(1)} %get-tuple-element.40), channel_id=1, source_target_pairs={{0,1},{3,2},{4,5},{7,6},{8,9},{11,10},{12,13},{15,14},{16,17},{19,... | collective-permute-start | bytes 995336 | tf_op jit(solution)/shard_map/ppermute | solution.py:417
  63.8 18.8 %collective-permute-start.20 = (s16[784,128]{1,0:T(8,128)(2,1)S(1)}, s16[784,128]{1,0:T(8,128)(2,1)S(1)}, u32[]{:S(2)}, u32[]{:S(2)}) collective-permute-start(s16[784,128]{1,0:T(8,128)(2,1)S(1)} %get-tuple-element.35), channel_id=1, source_target_pairs={{0,3},{3,0},{1,2},{2,1},{4,7},{7,4},{5,6},{6,5},{8,11},{11,8},{9,1... | collective-permute-start | bytes 602120 | tf_op jit(solution)/shard_map/ppermute | solution.py:399
  66.3 17.6 %collective-permute-start.21 = (s16[784,128]{1,0:T(8,128)(2,1)S(1)}, s16[784,128]{1,0:T(8,128)(2,1)S(1)}, u32[]{:S(2)}, u32[]{:S(2)}) collective-permute-start(s16[784,128]{1,0:T(8,128)(2,1)S(1)} %get-tuple-element.36), channel_id=1, source_target_pairs={{0,2},{1,3},{2,0},{3,1},{4,6},{5,7},{6,4},{7,5},{8,10},{9,11},{10,... | collective-permute-start | bytes 602120 | tf_op jit(solution)/shard_map/ppermute | solution.py:399
  66.3 26.1 %collective-permute-start.30 = (s16[1296,128]{1,0:T(8,128)(2,1)S(1)}, s16[1296,128]{1,0:T(8,128)(2,1)S(1)}, u32[]{:S(2)}, u32[]{:S(2)}) collective-permute-start(s16[1296,128]{1,0:T(8,128)(2,1)S(1)} %get-tuple-element.40), channel_id=1, source_target_pairs={{1,2},{2,1},{5,6},{6,5},{9,10},{10,9},{13,14},{14,13},{17,18},{18,... | collective-permute-start | bytes 995336 | tf_op jit(solution)/shard_map/ppermute | solution.py:402
  68.2 22.3 %collective-permute-start.22 = (s16[784,128]{1,0:T(8,128)(2,1)S(1)}, s16[784,128]{1,0:T(8,128)(2,1)S(1)}, u32[]{:S(2)}, u32[]{:S(2)}) collective-permute-start(s16[784,128]{1,0:T(8,128)(2,1)S(1)} %get-tuple-element.37), channel_id=1, source_target_pairs={{0,1},{1,0},{2,3},{3,2},{4,5},{5,4},{6,7},{7,6},{8,9},{9,8},{10,11... | collective-permute-start | bytes 602120 | tf_op jit(solution)/shard_map/ppermute | solution.py:399
  82.6 57.8 %collective-permute-start.9 = (s16[2064,128]{1,0:T(8,128)(2,1)S(1)}, s16[2064,128]{1,0:T(8,128)(2,1)S(1)}, u32[]{:S(2)}, u32[]{:S(2)}) collective-permute-start(s16[2064,128]{1,0:T(8,128)(2,1)S(1)} %get-tuple-element.30), channel_id=1, source_target_pairs={{1,2},{2,1},{5,6},{6,5},{9,10},{10,9},{13,14},{14,13},{17,18},{18,... | collective-permute-start | bytes 1585160 | tf_op jit(solution)/shard_map/ppermute | solution.py:402
  83.9 56.5 %collective-permute-start.12 = (s16[2064,128]{1,0:T(8,128)(2,1)S(1)}, s16[2064,128]{1,0:T(8,128)(2,1)S(1)}, u32[]{:S(2)}, u32[]{:S(2)}) collective-permute-start(s16[2064,128]{1,0:T(8,128)(2,1)S(1)} %get-tuple-element.32), channel_id=1, source_target_pairs={{0,1},{1,0},{2,3},{3,2},{4,5},{5,4},{6,7},{7,6},{8,9},{9,8},{10,11... | collective-permute-start | bytes 1585160 | tf_op jit(solution)/shard_map/ppermute | solution.py:405
  87.4 53.0 %collective-permute-start.11 = (s16[2064,128]{1,0:T(8,128)(2,1)S(1)}, s16[2064,128]{1,0:T(8,128)(2,1)S(1)}, u32[]{:S(2)}, u32[]{:S(2)}) collective-permute-start(s16[2064,128]{1,0:T(8,128)(2,1)S(1)} %shard_map.50), channel_id=1, source_target_pairs={{0,2},{1,3},{2,0},{3,1},{4,6},{5,7},{6,4},{7,5},{8,10},{9,11},{10,... | collective-permute-start | bytes 1585160 | tf_op jit(solution)/shard_map/ppermute | solution.py:421
  90.5 27.8 %collective-permute-start.33 = (s16[1296,128]{1,0:T(8,128)(2,1)S(1)}, s16[1296,128]{1,0:T(8,128)(2,1)S(1)}, u32[]{:S(2)}, u32[]{:S(2)}) collective-permute-start(s16[1296,128]{1,0:T(8,128)(2,1)S(1)} %get-tuple-element.42), channel_id=1, source_target_pairs={{0,1},{1,0},{2,3},{3,2},{4,5},{5,4},{6,7},{7,6},{8,9},{9,8},{10,11... | collective-permute-start | bytes 995336 | tf_op jit(solution)/shard_map/ppermute | solution.py:405
  92.5 46.4 %collective-permute-start.32 = (s16[1296,128]{1,0:T(8,128)(2,1)S(1)}, s16[1296,128]{1,0:T(8,128)(2,1)S(1)}, u32[]{:S(2)}, u32[]{:S(2)}) collective-permute-start(s16[1296,128]{1,0:T(8,128)(2,1)S(1)} %shard_map.57), channel_id=1, source_target_pairs={{0,2},{1,3},{2,0},{3,1},{4,6},{5,7},{6,4},{7,5},{8,10},{9,11},{10,... | collective-permute-start | bytes 995336 | tf_op jit(solution)/shard_map/ppermute | solution.py:421
  (13 other events, 143.3 us)

commit v6 on v5

--- a/solution.py
+++ b/solution.py
@@ -151,7 +151,7 @@
 
 
 def write_message(acc, first, out_ref, codes, owned, width):
-    @pl.loop(0, owned, unroll=4)
+    @pl.loop(0, owned, unroll=min(8, owned))
     def _(i):
         y, code = encode(acc[first + i])
         out_ref[rows_of(i, width), :] = y
@@ -172,7 +172,7 @@
     at = 0
     for ref in piece_refs:
 
-        @pl.loop(0, ref.shape[0], unroll=4)
+        @pl.loop(0, ref.shape[0], unroll=min(8, ref.shape[0]))
         def _(j):
             panel[at + j] = ref[j]
 
@@ -301,7 +301,7 @@
             n += 1
         at += 1 + terms
 
-    @pl.loop(0, owned // 2, unroll=2)
+    @pl.loop(0, owned // 2, unroll=min(4, owned // 2))
     def _(h):
         for k in range(2):
             i = 2 * h + k

time: 143 us -> 142 us (level)
  no operation moved by 1% of the time
where the time goes in v6:
time: 142 us; the launch traced here: 141 us
  waiting for transfers between devices  82.5 us (58%)
  starting transfers between devices  37.5 us (26%)
  Pallas kernels  19.9 us (14%)
    ppermute x7, waiting for transfers between devices, reduce(): got.append(lax.ppermute(message, 'col', pairs))  53.4 us
    ppermute x23, waiting for transfers between devices, swap(): return lax.ppermute(array, 'row', [(d, d ^ bits) for d in range(devices)])  27.7 us
    ppermute x23, starting transfers between devices, swap(): return lax.ppermute(array, 'row', [(d, d ^ bits) for d in range(devices)])  18.9 us
    ppermute x7, starting transfers between devices, reduce(): got.append(lax.ppermute(message, 'col', pairs))  12.5 us
    pallas_call x3, Pallas kernels, rest(): pl.pallas_call(functools.partial(rest_kernel, owned, messages, local_rows...  7.92 us
    ppermute x2, starting transfers between devices, reduce(): array = lax.ppermute(message, 'col', hops)  4.81 us
    pallas_call x3, Pallas kernels, head(): pl.pallas_call(functools.partial(head_kernel, owned), out_shape=[jax.Shap...  4.46 us
  transfers between devices with their start and end apart: 34, of which 11 were waited for; matrix products, arithmetic and copies ran while one was open for 0% of the time, Pallas kernels for 13%

profile of v6, /device:TPU:0, one launch (start us, length us, event | category | flops | bytes accessed | tf_op | source)
XLA Modules:
  0.0 141.4 jit_solution(17904910427684005413)
XLA Ops:
  1.6 3.0 %collective-permute-start.1 = (bf16[16,128,128]{2,1,0:T(8,128)(2,1)S(1)}, bf16[16,128,128]{2,1,0:T(8,128)(2,1)S(1)}, u32[]{:S(2)}, u32[]{:S(2)}) collective-permute-start(bf16[16,128,128]{2,1,0:T(8,128)(2,1)S(1)} %shard_map.47.refs_0_), channel_id=1, source_target_pairs={{0,8},{4,12},{8,0},{12,4},{16,24},{20,28},{24,16},{28,20},{1,9},{5... | collective-permute-start | bytes 1572872 | tf_op jit(solution)/shard_map/ppermute | solution.py:351
  4.6 1.5 %collective-permute-start.3 = (bf16[16,128,128]{2,1,0:T(8,128)(2,1)S(1)}, bf16[16,128,128]{2,1,0:T(8,128)(2,1)S(1)}, u32[]{:S(2)}, u32[]{:S(2)}) collective-permute-start(bf16[16,128,128]{2,1,0:T(8,128)(2,1)S(1)} %shard_map.47.refs_0_), channel_id=1, source_target_pairs={{0,16},{4,20},{8,24},{12,28},{16,0},{20,4},{24,8},{28,12},{1,17},{... | collective-permute-start | bytes 1572872 | tf_op jit(solution)/shard_map/ppermute | solution.py:351
  7.5 2.0 %collective-permute-start.24 = (bf16[16,80,128]{2,1,0:T(8,128)(2,1)S(1)}, bf16[16,80,128]{2,1,0:T(8,128)(2,1)S(1)}, u32[]{:S(2)}, u32[]{:S(2)}) collective-permute-start(bf16[16,80,128]{2,1,0:T(8,128)(2,1)S(1)} %shard_map.54.refs_0_), channel_id=1, source_target_pairs={{0,8},{4,12},{8,0},{12,4},{16,24},{20,28},{24,16},{28,20},{1,9},{5... | collective-permute-start | bytes 983048 | tf_op jit(solution)/shard_map/ppermute | solution.py:351
  9.5 12.1 %collective-permute-done.14.refs_2_ = bf16[16,48,128]{2,1,0:T(8,128)(2,1)S(1)} collective-permute-done((bf16[16,48,128]{2,1,0:T(8,128)(2,1)S(1)}, bf16[16,48,128]{2,1,0:T(8,128)(2,1)S(1)}, u32[]{:S(2)}, u32[]{:S(2)}) %collective-permute-start.14) | collective-permute-done | bytes 196640 | tf_op jit(solution)/shard_map/ppermute | solution.py:351
  21.6 2.0 %collective-permute-start.26 = (bf16[16,80,128]{2,1,0:T(8,128)(2,1)S(1)}, bf16[16,80,128]{2,1,0:T(8,128)(2,1)S(1)}, u32[]{:S(2)}, u32[]{:S(2)}) collective-permute-start(bf16[16,80,128]{2,1,0:T(8,128)(2,1)S(1)} %shard_map.54.refs_0_), channel_id=1, source_target_pairs={{0,16},{4,20},{8,24},{12,28},{16,0},{20,4},{24,8},{28,12},{1,17},{... | collective-permute-start | bytes 983048 | tf_op jit(solution)/shard_map/ppermute | solution.py:351
  25.7 3.0 %collective-permute-done.24.refs_2_ = bf16[16,80,128]{2,1,0:T(8,128)(2,1)S(1)} collective-permute-done((bf16[16,80,128]{2,1,0:T(8,128)(2,1)S(1)}, bf16[16,80,128]{2,1,0:T(8,128)(2,1)S(1)}, u32[]{:S(2)}, u32[]{:S(2)}) %collective-permute-start.24) | collective-permute-done | bytes 327712 | tf_op jit(solution)/shard_map/ppermute | solution.py:351
  28.6 7.5 %collective-permute-done.26.refs_4_ = bf16[16,80,128]{2,1,0:T(8,128)(2,1)S(1)} collective-permute-done((bf16[16,80,128]{2,1,0:T(8,128)(2,1)S(1)}, bf16[16,80,128]{2,1,0:T(8,128)(2,1)S(1)}, u32[]{:S(2)}, u32[]{:S(2)}) %collective-permute-start.26) | collective-permute-done | bytes 327712 | tf_op jit(solution)/shard_map/ppermute | solution.py:351
  37.6 2.1 %collective-permute-start.6 = (bf16[8,128,128]{2,1,0:T(8,128)(2,1)S(1)}, bf16[8,128,128]{2,1,0:T(8,128)(2,1)S(1)}, u32[]{:S(2)}, u32[]{:S(2)}) collective-permute-start(bf16[8,128,128]{2,1,0:T(8,128)(2,1)S(1)} %slice.9), channel_id=1, source_target_pairs={{0,16},{4,20},{8,24},{12,28},{16,0},{20,4},{24,8},{28,12},{1,17},{... | collective-permute-start | bytes 786440 | tf_op jit(solution)/shard_map/ppermute | solution.py:351
  39.7 2.8 %collective-permute-done.5.refs_6_ = bf16[8,128,128]{2,1,0:T(8,128)(2,1)S(1)} collective-permute-done((bf16[8,128,128]{2,1,0:T(8,128)(2,1)S(1)}, bf16[8,128,128]{2,1,0:T(8,128)(2,1)S(1)}, u32[]{:S(2)}, u32[]{:S(2)}) %collective-permute-start.5) | collective-permute-done | bytes 262176 | tf_op jit(solution)/shard_map/ppermute | solution.py:351
  42.5 1.5 %collective-permute-done.6.refs_7_ = bf16[8,128,128]{2,1,0:T(8,128)(2,1)S(1)} collective-permute-done((bf16[8,128,128]{2,1,0:T(8,128)(2,1)S(1)}, bf16[8,128,128]{2,1,0:T(8,128)(2,1)S(1)}, u32[]{:S(2)}, u32[]{:S(2)}) %collective-permute-start.6) | collective-permute-done | bytes 262176 | tf_op jit(solution)/shard_map/ppermute | solution.py:351
  44.5 2.0 %collective-permute-start.18 = (bf16[16,48,128]{2,1,0:T(8,128)(2,1)S(1)}, bf16[16,48,128]{2,1,0:T(8,128)(2,1)S(1)}, u32[]{:S(2)}, u32[]{:S(2)}) collective-permute-start(bf16[16,48,128]{2,1,0:T(8,128)(2,1)S(1)} %shard_map.51.refs_0_), channel_id=1, source_target_pairs={{0,24},{4,28},{8,16},{12,20},{16,8},{20,12},{24,0},{28,4},{1,25},{... | collective-permute-start | bytes 589832 | tf_op jit(solution)/shard_map/ppermute | solution.py:351
  47.1 2.8 %shard_map.46 = (s32[13]{0:T(128)S(1)}, s32[192]{0:T(256)S(1)}, s32[192]{0:T(256)S(1)}, bf16[192,128,128]{2,1,0:T(8,128)(2,1)S(1)}) custom-call(s32[65]{0:T(128)S(1)} %bitcast.4, s32[192]{0:T(256)S(1)} %bitcast.3, bf16[192,128,128]{2,1,0:T(8,128)(2,1)} %bitcast.5), custom_call_target="tpu_custom_call" | custom-call | flops 67108864 | bytes 4194304 | tf_op jit(solution)/shard_map/pallas_call | solution.py:118
  49.9 1.6 %shard_map.48 = (s16[2064,128]{1,0:T(8,128)(2,1)S(1)}, bf16[128,128,128]{2,1,0:T(8,128)(2,1)S(1)}) custom-call(s32[13]{0:T(128)S(1)} %get-tuple-element.24.range_ref, s32[192]{0:T(256)S(1)} %get-tuple-element.25.index_ref, s32[192]{0:T(256)S(1)} %get-tuple-element.26.row_ref, bf16[192,128,128]{2,1,0:T(8,128)(2,1)S(1)} %get-tuple-element.27.store, ...), custom_call_target="tpu_custom_call" | custom-call | flops 402653184 | bytes 4194304 | tf_op jit(solution)/shard_map/pallas_call | solution.py:211
  52.3 3.5 %collective-permute-start.10 = (s16[2064,128]{1,0:T(8,128)(2,1)S(1)}, s16[2064,128]{1,0:T(8,128)(2,1)S(1)}, u32[]{:S(2)}, u32[]{:S(2)}) collective-permute-start(s16[2064,128]{1,0:T(8,128)(2,1)S(1)} %get-tuple-element.30), channel_id=1, source_target_pairs={{0,1},{3,2},{4,5},{7,6},{8,9},{11,10},{12,13},{15,14},{16,17},{19,... | collective-permute-start | bytes 1585160 | tf_op jit(solution)/shard_map/ppermute | solution.py:417
  61.1 2.4 %shard_map.53 = (s16[784,128]{1,0:T(8,128)(2,1)S(1)}, s16[784,128]{1,0:T(8,128)(2,1)S(1)}, f32[16,48,128]{2,1,0:T(8,128)S(1)}) custom-call(s32[13]{0:T(128)S(1)} %get-tuple-element.24.range_ref, s32[192]{0:T(256)S(1)} %get-tuple-element.25.index_ref, s32[192]{0:T(256)S(1)} %get-tuple-element.26.row_ref, bf16[192,128,128]{2,1,0:T(8,128)(2,1)S(1)} %get-tuple-element.27.store, ...), custom_call_target="tpu_custom_call" | custom-call | flops 301989888 | bytes 4194304 | tf_op jit(solution)/shard_map/pallas_call | solution.py:235
  63.6 2.5 %collective-permute-start.20 = (s16[784,128]{1,0:T(8,128)(2,1)S(1)}, s16[784,128]{1,0:T(8,128)(2,1)S(1)}, u32[]{:S(2)}, u32[]{:S(2)}) collective-permute-start(s16[784,128]{1,0:T(8,128)(2,1)S(1)} %get-tuple-element.35), channel_id=1, source_target_pairs={{0,3},{3,0},{1,2},{2,1},{4,7},{7,4},{5,6},{6,5},{8,11},{11,8},{9,1... | collective-permute-start | bytes 602120 | tf_op jit(solution)/shard_map/ppermute | solution.py:399
  68.2 3.4 %collective-permute-start.22 = (s16[784,128]{1,0:T(8,128)(2,1)S(1)}, s16[784,128]{1,0:T(8,128)(2,1)S(1)}, u32[]{:S(2)}, u32[]{:S(2)}) collective-permute-start(s16[784,128]{1,0:T(8,128)(2,1)S(1)} %get-tuple-element.37), channel_id=1, source_target_pairs={{0,1},{1,0},{2,3},{3,2},{4,5},{5,4},{6,7},{7,6},{8,9},{9,8},{10,11... | collective-permute-start | bytes 602120 | tf_op jit(solution)/shard_map/ppermute | solution.py:399
  71.6 2.9 %shard_map.49 = (s16[2064,128]{1,0:T(8,128)(2,1)S(1)}, s16[2064,128]{1,0:T(8,128)(2,1)S(1)}, f32[16,128,128]{2,1,0:T(8,128)S(1)}) custom-call(s32[13]{0:T(128)S(1)} %get-tuple-element.24.range_ref, s32[192]{0:T(256)S(1)} %get-tuple-element.25.index_ref, s32[192]{0:T(256)S(1)} %get-tuple-element.26.row_ref, ...), custom_call_target="tpu_custom_call" | custom-call | flops 805306368 | bytes 4194304 | tf_op jit(solution)/shard_map/pallas_call | solution.py:235
  74.9 7.7 %collective-permute-done.20.refs_1_ = s16[784,128]{1,0:T(8,128)(2,1)S(1)} collective-permute-done((s16[784,128]{1,0:T(8,128)(2,1)S(1)}, s16[784,128]{1,0:T(8,128)(2,1)S(1)}, u32[]{:S(2)}, u32[]{:S(2)}) %collective-permute-start.20) | collective-permute-done | bytes 200736 | tf_op jit(solution)/shard_map/ppermute | solution.py:399
  83.9 3.5 %collective-permute-start.12 = (s16[2064,128]{1,0:T(8,128)(2,1)S(1)}, s16[2064,128]{1,0:T(8,128)(2,1)S(1)}, u32[]{:S(2)}, u32[]{:S(2)}) collective-permute-start(s16[2064,128]{1,0:T(8,128)(2,1)S(1)} %get-tuple-element.32), channel_id=1, source_target_pairs={{0,1},{1,0},{2,3},{3,2},{4,5},{5,4},{6,7},{7,6},{8,9},{9,8},{10,11... | collective-permute-start | bytes 1585160 | tf_op jit(solution)/shard_map/ppermute | solution.py:405
  87.4 2.6 %shard_map.56 = (s16[1296,128]{1,0:T(8,128)(2,1)S(1)}, s16[1296,128]{1,0:T(8,128)(2,1)S(1)}, f32[16,80,128]{2,1,0:T(8,128)S(1)}) custom-call(s32[13]{0:T(128)S(1)} %get-tuple-element.24.range_ref, s32[192]{0:T(256)S(1)} %get-tuple-element.25.index_ref, s32[192]{0:T(256)S(1)} %get-tuple-element.26.row_ref, ...), custom_call_target="tpu_custom_call" | custom-call | flops 503316480 | bytes 4194304 | tf_op jit(solution)/shard_map/pallas_call | solution.py:235
  90.4 2.0 %collective-permute-start.33 = (s16[1296,128]{1,0:T(8,128)(2,1)S(1)}, s16[1296,128]{1,0:T(8,128)(2,1)S(1)}, u32[]{:S(2)}, u32[]{:S(2)}) collective-permute-start(s16[1296,128]{1,0:T(8,128)(2,1)S(1)} %get-tuple-element.42), channel_id=1, source_target_pairs={{0,1},{1,0},{2,3},{3,2},{4,5},{5,4},{6,7},{7,6},{8,9},{9,8},{10,11... | collective-permute-start | bytes 995336 | tf_op jit(solution)/shard_map/ppermute | solution.py:405
  93.5 24.8 %collective-permute-done.33.refs_7_ = s16[1296,128]{1,0:T(8,128)(2,1)S(1)} collective-permute-done((s16[1296,128]{1,0:T(8,128)(2,1)S(1)}, s16[1296,128]{1,0:T(8,128)(2,1)S(1)}, u32[]{:S(2)}, u32[]{:S(2)}) %collective-permute-start.33) | collective-permute-done | bytes 331808 | tf_op jit(solution)/shard_map/ppermute | solution.py:405
  118.3 20.3 %collective-permute-done.32.refs_6_ = s16[1296,128]{1,0:T(8,128)(2,1)S(1)} collective-permute-done((s16[1296,128]{1,0:T(8,128)(2,1)S(1)}, s16[1296,128]{1,0:T(8,128)(2,1)S(1)}, u32[]{:S(2)}, u32[]{:S(2)}) %collective-permute-start.32) | collective-permute-done | bytes 331808 | tf_op jit(solution)/shard_map/ppermute | solution.py:421
  (66 shorter events, 21.5 us)
Async XLA Ops:
  1.6 23.5 %collective-permute-start.1 = (bf16[16,128,128]{2,1,0:T(8,128)(2,1)S(1)}, bf16[16,128,128]{2,1,0:T(8,128)(2,1)S(1)}, u32[]{:S(2)}, u32[]{:S(2)}) collective-permute-start(bf16[16,128,128]{2,1,0:T(8,128)(2,1)S(1)} %shard_map.47.refs_0_), channel_id=1, source_target_pairs={{0,8},{4,12},{8,0},{12,4},{16,24},{20,28},{24,16},{28,20},{1,9},{5... | collective-permute-start | bytes 1572872 | tf_op jit(solution)/shard_map/ppermute | solution.py:351
  4.6 20.5 %collective-permute-start.3 = (bf16[16,128,128]{2,1,0:T(8,128)(2,1)S(1)}, bf16[16,128,128]{2,1,0:T(8,128)(2,1)S(1)}, u32[]{:S(2)}, u32[]{:S(2)}) collective-permute-start(bf16[16,128,128]{2,1,0:T(8,128)(2,1)S(1)} %shard_map.47.refs_0_), channel_id=1, source_target_pairs={{0,16},{4,20},{8,24},{12,28},{16,0},{20,4},{24,8},{28,12},{1,17},{... | collective-permute-start | bytes 1572872 | tf_op jit(solution)/shard_map/ppermute | solution.py:351
  6.5 15.2 %collective-permute-start.14 = (bf16[16,48,128]{2,1,0:T(8,128)(2,1)S(1)}, bf16[16,48,128]{2,1,0:T(8,128)(2,1)S(1)}, u32[]{:S(2)}, u32[]{:S(2)}) collective-permute-start(bf16[16,48,128]{2,1,0:T(8,128)(2,1)S(1)} %shard_map.51.refs_0_), channel_id=1, source_target_pairs={{0,8},{4,12},{8,0},{12,4},{16,24},{20,28},{24,16},{28,20},{1,9},{5... | collective-permute-start | bytes 589832 | tf_op jit(solution)/shard_map/ppermute | solution.py:351
  7.1 16.6 %collective-permute-start.16 = (bf16[16,48,128]{2,1,0:T(8,128)(2,1)S(1)}, bf16[16,48,128]{2,1,0:T(8,128)(2,1)S(1)}, u32[]{:S(2)}, u32[]{:S(2)}) collective-permute-start(bf16[16,48,128]{2,1,0:T(8,128)(2,1)S(1)} %shard_map.51.refs_0_), channel_id=1, source_target_pairs={{0,16},{4,20},{8,24},{12,28},{16,0},{20,4},{24,8},{28,12},{1,17},{... | collective-permute-start | bytes 589832 | tf_op jit(solution)/shard_map/ppermute | solution.py:351
  7.5 21.2 %collective-permute-start.24 = (bf16[16,80,128]{2,1,0:T(8,128)(2,1)S(1)}, bf16[16,80,128]{2,1,0:T(8,128)(2,1)S(1)}, u32[]{:S(2)}, u32[]{:S(2)}) collective-permute-start(bf16[16,80,128]{2,1,0:T(8,128)(2,1)S(1)} %shard_map.54.refs_0_), channel_id=1, source_target_pairs={{0,8},{4,12},{8,0},{12,4},{16,24},{20,28},{24,16},{28,20},{1,9},{5... | collective-permute-start | bytes 983048 | tf_op jit(solution)/shard_map/ppermute | solution.py:351
  21.6 14.5 %collective-permute-start.26 = (bf16[16,80,128]{2,1,0:T(8,128)(2,1)S(1)}, bf16[16,80,128]{2,1,0:T(8,128)(2,1)S(1)}, u32[]{:S(2)}, u32[]{:S(2)}) collective-permute-start(bf16[16,80,128]{2,1,0:T(8,128)(2,1)S(1)} %shard_map.54.refs_0_), channel_id=1, source_target_pairs={{0,16},{4,20},{8,24},{12,28},{16,0},{20,4},{24,8},{28,12},{1,17},{... | collective-permute-start | bytes 983048 | tf_op jit(solution)/shard_map/ppermute | solution.py:351
  23.7 13.9 %collective-permute-start.28 = (bf16[16,80,128]{2,1,0:T(8,128)(2,1)S(1)}, bf16[16,80,128]{2,1,0:T(8,128)(2,1)S(1)}, u32[]{:S(2)}, u32[]{:S(2)}) collective-permute-start(bf16[16,80,128]{2,1,0:T(8,128)(2,1)S(1)} %shard_map.54.refs_0_), channel_id=1, source_target_pairs={{0,24},{4,28},{8,16},{12,20},{16,8},{20,12},{24,0},{28,4},{1,25},{... | collective-permute-start | bytes 983048 | tf_op jit(solution)/shard_map/ppermute | solution.py:351
  25.1 18.9 %collective-permute-start = (bf16[16,128,128]{2,1,0:T(8,128)(2,1)S(1)}, bf16[16,128,128]{2,1,0:T(8,128)(2,1)S(1)}, u32[]{:S(2)}, u32[]{:S(2)}) collective-permute-start(bf16[16,128,128]{2,1,0:T(8,128)(2,1)S(1)} %shard_map.47.refs_0_), channel_id=1, source_target_pairs={{0,4},{4,0},{8,12},{12,8},{16,20},{20,16},{24,28},{28,24},{1,5},{5... | collective-permute-start | bytes 1572872 | tf_op jit(solution)/shard_map/ppermute | solution.py:351
  25.1 19.4 %collective-permute-start.2 = (bf16[16,128,128]{2,1,0:T(8,128)(2,1)S(1)}, bf16[16,128,128]{2,1,0:T(8,128)(2,1)S(1)}, u32[]{:S(2)}, u32[]{:S(2)}) collective-permute-start(bf16[16,128,128]{2,1,0:T(8,128)(2,1)S(1)} %collective-permute-done.1.refs_2_), channel_id=1, source_target_pairs={{0,4},{4,0},{8,12},{12,8},{16,20},{20,16},{24,28},{28,24},{1,5},{5... | collective-permute-start | bytes 1572872 | tf_op jit(solution)/shard_map/ppermute | solution.py:351
  28.6 17.9 %collective-permute-start.4 = (bf16[16,128,128]{2,1,0:T(8,128)(2,1)S(1)}, bf16[16,128,128]{2,1,0:T(8,128)(2,1)S(1)}, u32[]{:S(2)}, u32[]{:S(2)}) collective-permute-start(bf16[16,128,128]{2,1,0:T(8,128)(2,1)S(1)} %collective-permute-done.3.refs_4_), channel_id=1, source_target_pairs={{0,4},{4,0},{8,12},{12,8},{16,20},{20,16},{24,28},{28,24},{1,5},{5... | collective-permute-start | bytes 1572872 | tf_op jit(solution)/shard_map/ppermute | solution.py:351
  44.0 11.8 %collective-permute-start.23 = (bf16[16,80,128]{2,1,0:T(8,128)(2,1)S(1)}, bf16[16,80,128]{2,1,0:T(8,128)(2,1)S(1)}, u32[]{:S(2)}, u32[]{:S(2)}) collective-permute-start(bf16[16,80,128]{2,1,0:T(8,128)(2,1)S(1)} %shard_map.54.refs_0_), channel_id=1, source_target_pairs={{0,4},{4,0},{8,12},{12,8},{16,20},{20,16},{24,28},{28,24},{1,5},{5... | collective-permute-start | bytes 983048 | tf_op jit(solution)/shard_map/ppermute | solution.py:351
  46.5 9.9 %collective-permute-start.27 = (bf16[16,80,128]{2,1,0:T(8,128)(2,1)S(1)}, bf16[16,80,128]{2,1,0:T(8,128)(2,1)S(1)}, u32[]{:S(2)}, u32[]{:S(2)}) collective-permute-start(bf16[16,80,128]{2,1,0:T(8,128)(2,1)S(1)} %collective-permute-done.26.refs_4_), channel_id=1, source_target_pairs={{0,4},{4,0},{8,12},{12,8},{16,20},{20,16},{24,28},{28,24},{1,5},{5... | collective-permute-start | bytes 983048 | tf_op jit(solution)/shard_map/ppermute | solution.py:351
  47.0 9.5 %collective-permute-start.29 = (bf16[16,80,128]{2,1,0:T(8,128)(2,1)S(1)}, bf16[16,80,128]{2,1,0:T(8,128)(2,1)S(1)}, u32[]{:S(2)}, u32[]{:S(2)}) collective-permute-start(bf16[16,80,128]{2,1,0:T(8,128)(2,1)S(1)} %collective-permute-done.28.refs_6_), channel_id=1, source_target_pairs={{0,4},{4,0},{8,12},{12,8},{16,20},{20,16},{24,28},{28,24},{1,5},{5... | collective-permute-start | bytes 983048 | tf_op jit(solution)/shard_map/ppermute | solution.py:351
  52.3 15.9 %collective-permute-start.10 = (s16[2064,128]{1,0:T(8,128)(2,1)S(1)}, s16[2064,128]{1,0:T(8,128)(2,1)S(1)}, u32[]{:S(2)}, u32[]{:S(2)}) collective-permute-start(s16[2064,128]{1,0:T(8,128)(2,1)S(1)} %get-tuple-element.30), channel_id=1, source_target_pairs={{0,1},{3,2},{4,5},{7,6},{8,9},{11,10},{12,13},{15,14},{16,17},{19,... | collective-permute-start | bytes 1585160 | tf_op jit(solution)/shard_map/ppermute | solution.py:417
  58.4 29.0 %collective-permute-start.31 = (s16[1296,128]{1,0:T(8,128)(2,1)S(1)}, s16[1296,128]{1,0:T(8,128)(2,1)S(1)}, u32[]{:S(2)}, u32[]{:S(2)}) collective-permute-start(s16[1296,128]{1,0:T(8,128)(2,1)S(1)} %get-tuple-element.40), channel_id=1, source_target_pairs={{0,1},{3,2},{4,5},{7,6},{8,9},{11,10},{12,13},{15,14},{16,17},{19,... | collective-permute-start | bytes 995336 | tf_op jit(solution)/shard_map/ppermute | solution.py:417
  63.6 19.0 %collective-permute-start.20 = (s16[784,128]{1,0:T(8,128)(2,1)S(1)}, s16[784,128]{1,0:T(8,128)(2,1)S(1)}, u32[]{:S(2)}, u32[]{:S(2)}) collective-permute-start(s16[784,128]{1,0:T(8,128)(2,1)S(1)} %get-tuple-element.35), channel_id=1, source_target_pairs={{0,3},{3,0},{1,2},{2,1},{4,7},{7,4},{5,6},{6,5},{8,11},{11,8},{9,1... | collective-permute-start | bytes 602120 | tf_op jit(solution)/shard_map/ppermute | solution.py:399
  66.1 17.8 %collective-permute-start.21 = (s16[784,128]{1,0:T(8,128)(2,1)S(1)}, s16[784,128]{1,0:T(8,128)(2,1)S(1)}, u32[]{:S(2)}, u32[]{:S(2)}) collective-permute-start(s16[784,128]{1,0:T(8,128)(2,1)S(1)} %get-tuple-element.36), channel_id=1, source_target_pairs={{0,2},{1,3},{2,0},{3,1},{4,6},{5,7},{6,4},{7,5},{8,10},{9,11},{10,... | collective-permute-start | bytes 602120 | tf_op jit(solution)/shard_map/ppermute | solution.py:399
  66.1 26.3 %collective-permute-start.30 = (s16[1296,128]{1,0:T(8,128)(2,1)S(1)}, s16[1296,128]{1,0:T(8,128)(2,1)S(1)}, u32[]{:S(2)}, u32[]{:S(2)}) collective-permute-start(s16[1296,128]{1,0:T(8,128)(2,1)S(1)} %get-tuple-element.40), channel_id=1, source_target_pairs={{1,2},{2,1},{5,6},{6,5},{9,10},{10,9},{13,14},{14,13},{17,18},{18,... | collective-permute-start | bytes 995336 | tf_op jit(solution)/shard_map/ppermute | solution.py:402
  68.2 22.2 %collective-permute-start.22 = (s16[784,128]{1,0:T(8,128)(2,1)S(1)}, s16[784,128]{1,0:T(8,128)(2,1)S(1)}, u32[]{:S(2)}, u32[]{:S(2)}) collective-permute-start(s16[784,128]{1,0:T(8,128)(2,1)S(1)} %get-tuple-element.37), channel_id=1, source_target_pairs={{0,1},{1,0},{2,3},{3,2},{4,5},{5,4},{6,7},{7,6},{8,9},{9,8},{10,11... | collective-permute-start | bytes 602120 | tf_op jit(solution)/shard_map/ppermute | solution.py:399
  82.6 57.4 %collective-permute-start.9 = (s16[2064,128]{1,0:T(8,128)(2,1)S(1)}, s16[2064,128]{1,0:T(8,128)(2,1)S(1)}, u32[]{:S(2)}, u32[]{:S(2)}) collective-permute-start(s16[2064,128]{1,0:T(8,128)(2,1)S(1)} %get-tuple-element.30), channel_id=1, source_target_pairs={{1,2},{2,1},{5,6},{6,5},{9,10},{10,9},{13,14},{14,13},{17,18},{18,... | collective-permute-start | bytes 1585160 | tf_op jit(solution)/shard_map/ppermute | solution.py:402
  83.9 56.1 %collective-permute-start.12 = (s16[2064,128]{1,0:T(8,128)(2,1)S(1)}, s16[2064,128]{1,0:T(8,128)(2,1)S(1)}, u32[]{:S(2)}, u32[]{:S(2)}) collective-permute-start(s16[2064,128]{1,0:T(8,128)(2,1)S(1)} %get-tuple-element.32), channel_id=1, source_target_pairs={{0,1},{1,0},{2,3},{3,2},{4,5},{5,4},{6,7},{7,6},{8,9},{9,8},{10,11... | collective-permute-start | bytes 1585160 | tf_op jit(solution)/shard_map/ppermute | solution.py:405
  87.4 52.6 %collective-permute-start.11 = (s16[2064,128]{1,0:T(8,128)(2,1)S(1)}, s16[2064,128]{1,0:T(8,128)(2,1)S(1)}, u32[]{:S(2)}, u32[]{:S(2)}) collective-permute-start(s16[2064,128]{1,0:T(8,128)(2,1)S(1)} %shard_map.50), channel_id=1, source_target_pairs={{0,2},{1,3},{2,0},{3,1},{4,6},{5,7},{6,4},{7,5},{8,10},{9,11},{10,... | collective-permute-start | bytes 1585160 | tf_op jit(solution)/shard_map/ppermute | solution.py:421
  90.4 27.9 %collective-permute-start.33 = (s16[1296,128]{1,0:T(8,128)(2,1)S(1)}, s16[1296,128]{1,0:T(8,128)(2,1)S(1)}, u32[]{:S(2)}, u32[]{:S(2)}) collective-permute-start(s16[1296,128]{1,0:T(8,128)(2,1)S(1)} %get-tuple-element.42), channel_id=1, source_target_pairs={{0,1},{1,0},{2,3},{3,2},{4,5},{5,4},{6,7},{7,6},{8,9},{9,8},{10,11... | collective-permute-start | bytes 995336 | tf_op jit(solution)/shard_map/ppermute | solution.py:405
  92.4 46.2 %collective-permute-start.32 = (s16[1296,128]{1,0:T(8,128)(2,1)S(1)}, s16[1296,128]{1,0:T(8,128)(2,1)S(1)}, u32[]{:S(2)}, u32[]{:S(2)}) collective-permute-start(s16[1296,128]{1,0:T(8,128)(2,1)S(1)} %shard_map.57), channel_id=1, source_target_pairs={{0,2},{1,3},{2,0},{3,1},{4,6},{5,7},{6,4},{7,5},{8,10},{9,11},{10,... | collective-permute-start | bytes 995336 | tf_op jit(solution)/shard_map/ppermute | solution.py:421
  (13 other events, 143.0 us)
